TPU v7x, 128 devices: a whole 4x4x4 slice. The times are simulated.
128 devices in a mesh: px: 8 (over y_lo, x), py: 16 (over z, y_hi, core).
Axes of the slice: x: 4, y: 4 (y_hi: 2, y_lo: 2; y = y_hi * 2 + y_lo), z: 4, core: 2. Of those that a mesh axis runs over, the one named last changes fastest.
Arguments:
- photons: float32 [4096, 128], P(('px', 'py')), may hold values from 50 to 1000
- halo_cells: int32 [4096, 128], P(('px', 'py')), may hold values from 0 to 442367
- halo_counts: int32 [4096], P(('px', 'py')), may hold values from 1 to 128
- owners: int32 [4096, 1], P(('px', 'py')), may hold values from 0 to 15; in each aligned block of 32 rows (0 to 31, 32 to 63, ...) at most 4 rows name the same one
- density: float32 [384, 384, 384], P('px', 'py'), may hold values from 0.02 to 50
Outputs:
- fraction: float32 [384, 384, 384], P('px', 'py')
Inputs may be any that keep to these rules, and one draw needn't show every extreme that they name: The halos of a block all lie in pencil owners[b] of the block's own slab. Among the 32 blocks of one device no owner appears more than 4 times, a bound that some block reaches. Slots at or past halo_counts[b] are not live and carry arbitrary values. `halo_cells`: A cell index within the owner pencil is (x * 24 + y) * 384 + z with x, y, z local to that pencil.
All inputs are finite; a program needn't handle non-finite values.
Results may differ from a plain program's by a relative error of at most 0.0003.
Values sent between devices are 32-bit elements; how exact they have to be, the bound alone decides.
No kernel may reach another device: no remote copies, remote signals or barrier semaphores. Data moves between devices by JAX's collectives and lax.ppermute only.
A program may use at most 128 MiB of HBM per device.

v0:
```python
import math

import jax
import jax.numpy as jnp
from jax import lax
from jax.sharding import PartitionSpec as P

NG = 384
SLOTS = 128
CAP = 4
RADIUS = 20


def in_one_piece(arrays, axis, split_dim, concat_dim, along):
    widths = [math.prod(a.shape[along:]) for a in arrays]
    both = jnp.concatenate(
        [a.reshape(*a.shape[:along], w) for a, w in zip(arrays, widths)], axis=along
    )
    out = lax.all_to_all(both, axis, split_axis=split_dim, concat_axis=concat_dim, tiled=True)
    tiles = jnp.split(out, [sum(widths[:k]) for k in range(1, len(widths))], axis=along)
    return tuple((b.reshape(*out.shape[:along], *a.shape[along:]) for a, b in zip(arrays, tiles)))


def side_by_side(arrays, axis, split_dim, concat_dim, along):
    ends, at = ([], 0)
    for a in arrays[:-1]:
        at += a.shape[along]
        ends.append(at)
    both = jnp.concatenate(arrays, axis=along)
    return tuple(
        jnp.split(
            lax.all_to_all(both, axis, split_axis=split_dim, concat_axis=concat_dim, tiled=True),
            ends,
            axis=along,
        )
    )


def product(form, left, right):
    return jnp.einsum(form, left, right, precision=lax.Precision.HIGHEST)


def rotate(form, real_part, imag_part, cos_table, sin_table, direction):
    signed_sin = direction * sin_table
    first = product(form, real_part + imag_part, cos_table)
    second = product(form, real_part, signed_sin - cos_table)
    third = product(form, imag_part, cos_table + signed_sin)
    return (first - third, first + second)


def tables(length):
    index_row = jnp.arange(length, dtype=jnp.int32)
    angle = (index_row[:, None] * index_row[None, :] % length).astype(jnp.float32) * (
        2.0 * jnp.pi / length
    )
    return (jnp.cos(angle), jnp.sin(angle))


def signed_frequency(index_values):
    return jnp.where(index_values < NG // 2, index_values, index_values - NG).astype(jnp.float32)


def top_hat(freq_x, freq_y, freq_z):
    radial = jnp.sqrt(freq_x * freq_x + freq_y * freq_y + freq_z * freq_z) * (
        2.0 * jnp.pi * RADIUS / NG
    )
    safe = jnp.where(radial > 0, radial, 1.0)
    value = 3.0 * (jnp.sin(safe) - safe * jnp.cos(safe)) / (safe * safe * safe)
    return jnp.where(radial > 0, value, 1.0)


def paint(photon_rows, cell_rows, live_rows, cell_total):
    weights = jnp.where(live_rows, photon_rows, 0.0)
    empty = jnp.zeros((cell_total,), jnp.float32)
    return empty.at[cell_rows.reshape(-1)].add(weights.reshape(-1))


def on_device(photons, halo_cells, halo_counts, owners, density):
    rows_x, rows_y = (density.shape[0], density.shape[1])
    cell_total = rows_x * rows_y * NG
    count_x = lax.axis_size("px")
    count_y = lax.axis_size("py")
    slot_index = jnp.arange(SLOTS, dtype=jnp.int32)[None, :]
    block_count = photons.shape[0]
    target = owners[:, 0]
    one_hot = (target[:, None] == jnp.arange(count_y, dtype=jnp.int32)[None, :]).astype(jnp.int32)
    slot_rank = jnp.sum(jnp.cumsum(one_hot, axis=0) * one_hot, axis=1) - 1
    position = target * CAP + slot_rank
    placing = position[None, :] == jnp.arange(count_y * CAP, dtype=jnp.int32)[:, None]
    source = jnp.sum(
        jnp.where(placing, jnp.arange(block_count, dtype=jnp.int32)[None, :], 0), axis=1
    )
    filled = jnp.any(placing, axis=1)
    send_photons = photons[source]
    send_cells = halo_cells[source]
    send_counts = jnp.where(filled, halo_counts[source], 0)
    got_photons, got_cells, got_counts = (
        lax.all_to_all(send_photons, "py", split_axis=0, concat_axis=0, tiled=True),
        *in_one_piece((send_cells, send_counts), "py", 0, 0, 1),
    )
    live_rows = slot_index < got_counts[:, None]
    painted = paint(got_photons, got_cells, live_rows, cell_total)
    cos_full, sin_full = tables(NG)
    field_rows = painted.reshape(rows_x * rows_y, NG)
    density_rows = density.reshape(rows_x * rows_y, NG)
    spec_real, spec_imag = rotate("az,zk->ka", field_rows, density_rows, cos_full, sin_full, -1.0)
    cos_y = cos_full.reshape(count_y, rows_y, NG)
    sin_y = sin_full.reshape(count_y, rows_y, NG)
    cos_x = cos_full.reshape(count_x, rows_x, NG)
    sin_x = sin_full.reshape(count_x, rows_x, NG)
    freq_all = signed_frequency(jnp.arange(NG, dtype=jnp.int32))
    devices_all = count_x * count_y
    slab_planes = NG // devices_all
    sent = (
        spec_real.reshape(devices_all, slab_planes, rows_x * rows_y),
        spec_imag.reshape(devices_all, slab_planes, rows_x * rows_y),
    )
    got_real, got_imag = side_by_side((sent[0], sent[1]), ("px", "py"), 0, 2, 1)
    got_real = got_real.reshape(slab_planes, count_x, count_y, rows_x, rows_y)
    got_imag = got_imag.reshape(slab_planes, count_x, count_y, rows_x, rows_y)
    plane_real, plane_imag = rotate("kiqxl,qlm->kixm", got_real, got_imag, cos_y, sin_y, -1.0)
    full_real, full_imag = rotate("kixm,ixn->kmn", plane_real, plane_imag, cos_x, sin_x, -1.0)
    freq_z = signed_frequency(
        lax.axis_index(("px", "py")) * slab_planes + jnp.arange(slab_planes, dtype=jnp.int32)
    )
    window = top_hat(freq_z[:, None, None], freq_all[None, :, None], freq_all[None, None, :])
    full_real = full_real * window
    full_imag = full_imag * window
    plane_real, plane_imag = rotate("kmn,ixn->kmix", full_real, full_imag, cos_x, sin_x, 1.0)
    back_real, back_imag = rotate("kmix,qlm->iqkxl", plane_real, plane_imag, cos_y, sin_y, 1.0)
    sent = (
        back_real.reshape(devices_all, slab_planes, rows_x * rows_y),
        back_imag.reshape(devices_all, slab_planes, rows_x * rows_y),
    )
    got_real, got_imag = side_by_side((sent[0], sent[1]), ("px", "py"), 0, 1, 2)
    got_real = got_real.reshape(NG, rows_x * rows_y)
    got_imag = got_imag.reshape(NG, rows_x * rows_y)
    final_real, final_imag = rotate("ka,kz->az", got_real, got_imag, cos_full, sin_full, 1.0)
    scale = 1.0 / (float(NG) * float(NG) * float(NG))
    photon_smooth = final_real * scale
    density_smooth = final_imag * scale
    fraction = jnp.clip(photon_smooth / jnp.maximum(density_smooth, 0.5), 0.0, 1.0)
    return fraction.reshape(rows_x, rows_y, NG)


def solution(mesh):
    placed = (
        P(("px", "py"), None),
        P(("px", "py"), None),
        P(("px", "py")),
        P(("px", "py"), None),
        P("px", "py", None),
    )
    return jax.shard_map(
        on_device, mesh=mesh, in_specs=placed, out_specs=P("px", "py", None), check_vma=False
    )
```

profile of v0, /device:TPU:7, one launch (start us, length us, event | category | flops | bytes accessed | tf_op | source)
XLA Modules:
  0.0 463.7 jit_solution(1115859090516122004)
XLA Ops:
  5.4 8.6 %all-to-all-start = ((s32[16,4,129]{2,1,0:T(4,128)}), s32[16,4,129]{2,1,0:T(4,128)S(1)}, u32[]{:S(2)}, u32[]{:S(2)}) async-start(s32[16,4,129]{2,1,0:T(4,128)} %pad_add_fusion), calls=%async_computation | async-start | bytes 131072 | tf_op jit(solution)/shard_map/all_to_all | solution.py:19
  15.9 5.4 %all-to-all-done = s32[16,4,129]{2,1,0:T(4,128)S(1)} async-done(((s32[16,4,129]{2,1,0:T(4,128)}), s32[16,4,129]{2,1,0:T(4,128)S(1)}, u32[]{:S(2)}, u32[]{:S(2)}) %all-to-all-start) | async-done | bytes 33056 | tf_op jit(solution)/shard_map/all_to_all | solution.py:19
  25.2 7.2 %all-to-all-done.1 = f32[16,4,128]{2,1,0:T(4,128)S(1)} async-done(((f32[16,4,128]{2,1,0:T(4,128)}), f32[16,4,128]{2,1,0:T(4,128)S(1)}, u32[]{:S(2)}, u32[]{:S(2)}) %all-to-all-start.1) | async-done | bytes 32800 | tf_op jit(solution)/shard_map/all_to_all | solution.py:98
  32.5 43.6 %scatter_custom_fusion = f32[442368]{0:T(1024)S(1)} fusion(s32[8192]{0:T(1024)S(1)} %bitcast.157, f32[8192]{0:T(1024)S(1)} %fusion.190, f32[]{:T(128)} %constant.24.clone.1), kind=kCustom, calls=%fused_computation.55 | custom fusion | flops 8192 | bytes 1769476 | tf_op jit(solution)/shard_map/scatter-add | solution.py:75
  76.5 8.5 %fusion.29 = f32[384,1152]{1,0:T(8,128)S(1)} fusion(f32[1152,384]{1,0:T(8,128)S(1)} %reshape.227, f32[1152,384]{1,0:T(8,128)} %bitcast.152), kind=kOutput, calls=%fused_computation.51 | convolution fusion | flops 2040201216 | bytes 5308416 | tf_op jit(solution)/shard_map/az,zk->ka/dot_general | solution.py:40
  85.1 9.2 %convolution_add_fusion.1 = f32[384,1152]{1,0:T(8,128)} fusion(f32[384,1152]{1,0:T(8,128)S(1)} %fusion.29, f32[1152,384]{1,0:T(8,128)S(1)} %reshape.227), kind=kOutput, calls=%fused_computation.15 | convolution fusion | flops 2040496128 | bytes 5308416 | tf_op jit(solution)/shard_map/az,zk->ka/dot_general | solution.py:40
  94.2 8.9 %convolution_subtract_fusion.1 = f32[384,1152]{1,0:T(8,128)} fusion(f32[384,1152]{1,0:T(8,128)S(1)} %fusion.29, f32[1152,384]{1,0:T(8,128)S(1)} %bitcast.153), kind=kOutput, calls=%fused_computation.16 | convolution fusion | flops 2040496128 | bytes 5308416 | tf_op jit(solution)/shard_map/az,zk->ka/dot_general | solution.py:40
  114.3 5.5 %all-to-all-start.2 = ((f32[128,6,1152]{2,1,0:T(8,128)}), f32[128,6,1152]{2,1,0:T(8,128)}, u32[]{:S(2)}, u32[]{:S(2)}) async-start(f32[128,6,1152]{2,1,0:T(8,128)} %pad_maximum_fusion), calls=%async_computation.2 | async-start | bytes 9437184 | tf_op jit(solution)/shard_map/all_to_all | solution.py:32
  120.0 59.9 %all-to-all-done.2 = f32[128,6,1152]{2,1,0:T(8,128)} async-done(((f32[128,6,1152]{2,1,0:T(8,128)}), f32[128,6,1152]{2,1,0:T(8,128)}, u32[]{:S(2)}, u32[]{:S(2)}) %all-to-all-start.2) | async-done | bytes 3538976 | tf_op jit(solution)/shard_map/all_to_all | solution.py:32
  179.9 6.1 %fusion.258 = (f32[1,3,147456]{2,1,0:T(4,128)S(1)}, f32[1,3,147456]{2,1,0:T(4,128)}) fusion(f32[1,6,147456]{2,1,0:T(8,128)} %bitcast.14), kind=kLoop, calls=%fused_computation.251 | loop fusion | bytes 7077888 | tf_op jit(solution)/shard_map/split | solution.py:31
  186.0 12.4 %reshape.231 = f32[3,8,16,48,24]{4,3,2,1,0:T(8,128)} reshape(f32[1,3,147456]{2,1,0:T(4,128)} %get-tuple-element.6) | data formatting | bytes 3538944 | tf_op jit(solution)/shard_map/reshape | solution.py:119
  198.4 10.9 %reshape.232 = f32[3,8,16,48,24]{4,3,2,1,0:T(8,128)} reshape(f32[1,3,147456]{2,1,0:T(4,128)S(1)} %get-tuple-element.5) | data formatting | bytes 3538944 | tf_op jit(solution)/shard_map/reshape | solution.py:120
  209.3 17.2 %fusion = f32[3,8,48,384,1]{3,2,4,1,0:T(8,128)S(1)} fusion(f32[3,8,16,48,24]{4,3,2,1,0:T(8,128)} %reshape.231, f32[3,8,16,48,24]{4,3,2,1,0:T(8,128)} %reshape.232, s32[16,24]{1,0:T(8,128)S(1)} %multiply_add_fusion), kind=kOutput, calls=%fused_computation.4 | convolution fusion | flops 2040201216 | bytes 5309952 | tf_op jit(solution)/shard_map/kiqxl,qlm->kixm/dot_general | solution.py:40
  226.5 10.6 %bitcast_add_fusion.1 = f32[3,8,48,384]{3,2,1,0:T(8,128)S(1)} fusion(f32[3,8,48,384,1]{3,2,4,1,0:T(8,128)S(1)} %fusion, f32[3,8,16,48,24]{4,3,2,1,0:T(8,128)S(1)} %copy-done.2, s32[16,24]{1,0:T(8,128)S(1)} %multiply_add_fusion), kind=kOutput, calls=%fused_computation.43 | convolution fusion | flops 2040496128 | bytes 5309952 | tf_op jit(solution)/shard_map/kiqxl,qlm->kixm/dot_general | solution.py:40
  237.2 11.0 %bitcast_subtract_fusion.1 = f32[3,8,48,384]{3,2,1,0:T(8,128)S(1)} fusion(f32[3,8,48,384,1]{3,2,4,1,0:T(8,128)S(1)} %fusion, f32[3,8,16,48,24]{4,3,2,1,0:T(8,128)S(1)} %bitcast.151, s32[16,24]{1,0:T(8,128)S(1)} %multiply_add_fusion), kind=kOutput, calls=%fused_computation.44 | convolution fusion | flops 2040496128 | bytes 5309952 | tf_op jit(solution)/shard_map/kiqxl,qlm->kixm/dot_general | solution.py:40
  248.2 6.1 %fusion.27 = f32[3,384,384,1]{2,1,3,0:T(8,128)S(1)} fusion(f32[3,8,48,384]{3,2,1,0:T(8,128)S(1)} %bitcast_subtract_fusion.1, f32[3,8,48,384]{3,2,1,0:T(8,128)S(1)} %bitcast_add_fusion.1, s32[8,48]{1,0:T(8,128)S(1)} %multiply_add_fusion.1), kind=kOutput, calls=%fused_computation.49 | convolution fusion | flops 2040201216 | bytes 5309952 | tf_op jit(solution)/shard_map/kixm,ixn->kmn/dot_general | solution.py:40
  254.3 13.6 %fusion.21 = f32[3,384,384]{2,1,0:T(8,128)S(1)} fusion(f32[3,384,384,1]{2,1,3,0:T(8,128)S(1)} %fusion.27, f32[3,8,48,384]{3,2,1,0:T(8,128)S(1)} %bitcast_subtract_fusion.1, f32[384]{0:T(512)S(1)} %fusion.194, f32[3,384]{1,0:T(4,128)S(1)} %broadcast_add_fusion, s32[8,48]{1,0:T(8,128)S(1)} %multiply_add_fusion.1), kind=kOutput, calls=%fused_computation.40 | convolution fusion | flops 2045804544 | bytes 5316096 | tf_op jit(solution)/shard_map/kixm,ixn->kmn/dot_general | solution.py:40
  267.9 13.7 %fusion.22 = f32[3,384,384]{2,1,0:T(8,128)S(1)} fusion(f32[3,384,384,1]{2,1,3,0:T(8,128)S(1)} %fusion.27, f32[3,8,48,384]{3,2,1,0:T(8,128)S(1)} %bitcast_add_fusion.1, f32[384]{0:T(512)S(1)} %fusion.194, f32[3,384]{1,0:T(4,128)S(1)} %broadcast_add_fusion, s32[8,48]{1,0:T(8,128)S(1)} %multiply_add_fusion.1), kind=kOutput, calls=%fused_computation.42 | convolution fusion | flops 2045804544 | bytes 5316096 | tf_op jit(solution)/shard_map/kixm,ixn->kmn/dot_general | solution.py:40
  281.6 5.8 %fusion.15 = f32[3,384,8,48]{1,3,2,0:T(8,128)S(1)} fusion(f32[3,384,384]{2,1,0:T(8,128)S(1)} %fusion.22, f32[3,384,384]{2,1,0:T(8,128)S(1)} %fusion.21, s32[8,48]{1,0:T(8,128)S(1)} %multiply_add_fusion.1), kind=kOutput, calls=%fused_computation.33 | convolution fusion | flops 2040201216 | bytes 5309952 | tf_op jit(solution)/shard_map/kmn,ixn->kmix/dot_general | solution.py:40
  287.4 5.8 %fusion.34 = f32[3,384,8,48]{1,3,2,0:T(8,128)S(1)} fusion(f32[3,384,8,48]{1,3,2,0:T(8,128)S(1)} %fusion.15, f32[3,384,384]{2,1,0:T(8,128)S(1)} %fusion.22, s32[8,48]{1,0:T(8,128)S(1)} %multiply_add_fusion.1), kind=kOutput, calls=%fused_computation.54 | convolution fusion | flops 2040348672 | bytes 5309952 | tf_op jit(solution)/shard_map/kmn,ixn->kmix/dot_general | solution.py:40
  293.2 5.8 %fusion.31 = f32[3,384,8,48]{1,3,2,0:T(8,128)S(1)} fusion(f32[3,384,8,48]{1,3,2,0:T(8,128)S(1)} %fusion.15, f32[3,384,384]{2,1,0:T(8,128)S(1)} %fusion.21, s32[8,48]{1,0:T(8,128)S(1)} %multiply_add_fusion.1), kind=kOutput, calls=%fused_computation.53 | convolution fusion | flops 2040348672 | bytes 5309952 | tf_op jit(solution)/shard_map/kmn,ixn->kmix/dot_general | solution.py:40
  299.0 10.3 %fusion.19 = f32[16,24,3,8,48]{4,1,3,2,0:T(8,128)S(1)} fusion(f32[3,384,8,48]{1,3,2,0:T(8,128)S(1)} %fusion.31, f32[3,384,8,48]{1,3,2,0:T(8,128)S(1)} %fusion.34, s32[16,24]{1,0:T(8,128)S(1)} %multiply_add_fusion), kind=kOutput, calls=%fused_computation.37 | convolution fusion | flops 2040201216 | bytes 5309952 | tf_op jit(solution)/shard_map/kmix,qlm->iqkxl/dot_general | solution.py:40
  309.3 13.7 %subtract_bitcast_fusion = f32[8,16,3,48,24]{3,4,0,2,1:T(8,128)} fusion(f32[16,24,3,8,48]{4,1,3,2,0:T(8,128)S(1)} %fusion.19, f32[3,384,8,48]{1,3,2,0:T(8,128)S(1)} %fusion.34, s32[16,24]{1,0:T(8,128)S(1)} %multiply_add_fusion), kind=kOutput, calls=%fused_computation.8 | convolution fusion | flops 2040348672 | bytes 5309952 | tf_op jit(solution)/shard_map/kmix,qlm->iqkxl/dot_general | solution.py:40
  323.0 11.8 %add_bitcast_fusion = f32[8,16,3,48,24]{3,4,0,2,1:T(8,128)} fusion(f32[16,24,3,8,48]{4,1,3,2,0:T(8,128)S(1)} %fusion.19, f32[3,384,8,48]{1,3,2,0:T(8,128)S(1)} %fusion.31, s32[16,24]{1,0:T(8,128)S(1)} %multiply_add_fusion), kind=kOutput, calls=%fused_computation.7 | convolution fusion | flops 2040348672 | bytes 5309952 | tf_op jit(solution)/shard_map/kmix,qlm->iqkxl/dot_general | solution.py:40
  334.9 8.2 %copy.33 = f32[8,16,3,48,24]{4,3,1,0,2:T(8,128)} copy(f32[8,16,3,48,24]{3,4,0,2,1:T(8,128)} %subtract_bitcast_fusion) | data formatting | bytes 3538944 | tf_op jit(solution)/shard_map/sub | solution.py:48
  343.0 7.4 %reshape.233 = f32[128,3,1152]{2,0,1:T(8,128)S(1)} reshape(f32[8,16,3,48,24]{4,3,1,0,2:T(8,128)} %copy.33) | data formatting | bytes 3538944 | tf_op jit(solution)/shard_map/reshape | solution.py:132
  350.4 8.2 %copy.34 = f32[8,16,3,48,24]{4,3,1,0,2:T(8,128)} copy(f32[8,16,3,48,24]{3,4,0,2,1:T(8,128)} %add_bitcast_fusion) | data formatting | bytes 3538944 | tf_op jit(solution)/shard_map/add | solution.py:48
  358.5 7.4 %reshape.234 = f32[128,3,1152]{2,0,1:T(8,128)S(1)} reshape(f32[8,16,3,48,24]{4,3,1,0,2:T(8,128)} %copy.34) | data formatting | bytes 3538944 | tf_op jit(solution)/shard_map/reshape | solution.py:133
  368.6 70.1 %all_to_all.51 = f32[128,3,2304]{2,1,0:T(4,128)} all-to-all(f32[128,3,2304]{2,1,0:T(4,128)S(1)} %copy.35), channel_id=1, replica_groups=mesh['px'=8,'py'=16] {'px','py'}, dimensions={0} | all-to-all | bytes 7077888 | tf_op jit(solution)/shard_map/all_to_all | solution.py:32
  443.7 5.8 %fusion.23 = f32[1152,384]{1,0:T(8,128)S(1)} fusion(f32[1,384,2304]{2,1,0:T(8,128)S(1)} %all_to_all.46), kind=kOutput, calls=%fused_computation.45 | convolution fusion | flops 2040201216 | bytes 5308416 | tf_op jit(solution)/shard_map/ka,kz->az/dot_general | solution.py:40
  449.5 6.2 %fusion.3 = f32[1152,384]{1,0:T(8,128)S(1)} fusion(f32[1152,384]{1,0:T(8,128)S(1)} %fusion.23, f32[1,384,2304]{2,1,0:T(8,128)S(1)} %all_to_all.46), kind=kOutput, calls=%fused_computation.12 | convolution fusion | flops 2041233408 | bytes 5308416 | tf_op jit(solution)/shard_map/ka,kz->az/dot_general | solution.py:40
  455.7 7.6 %fusion.6 = f32[1152,384]{1,0:T(8,128)} fusion(f32[1152,384]{1,0:T(8,128)S(1)} %fusion.3, f32[1152,384]{1,0:T(8,128)S(1)} %fusion.23, f32[1,384,2304]{2,1,0:T(8,128)S(1)} %all_to_all.46), kind=kOutput, calls=%fused_computation.18 | convolution fusion | flops 2041675776 | bytes 7077888 | tf_op jit(solution)/shard_map/ka,kz->az/dot_general | solution.py:40
  (47 shorter events, 30.5 us)
Async XLA Ops:
  0.0 4.1 copy-start
  5.4 16.0 %all-to-all-start = ((s32[16,4,129]{2,1,0:T(4,128)}), s32[16,4,129]{2,1,0:T(4,128)S(1)}, u32[]{:S(2)}, u32[]{:S(2)}) async-start(s32[16,4,129]{2,1,0:T(4,128)} %pad_add_fusion), calls=%async_computation | async-start | bytes 131072 | tf_op jit(solution)/shard_map/all_to_all | solution.py:19
  21.3 11.1 %all-to-all-start.1 = ((f32[16,4,128]{2,1,0:T(4,128)}), f32[16,4,128]{2,1,0:T(4,128)S(1)}, u32[]{:S(2)}, u32[]{:S(2)}) async-start(f32[16,4,128]{2,1,0:T(4,128)} %bitcast.9), calls=%async_computation.1 | async-start | bytes 65536 | tf_op jit(solution)/shard_map/all_to_all | solution.py:98
  85.1 9.2 %copy-start.3 = (f32[48,24,384]{2,1,0:T(8,128)S(1)}, f32[48,24,384]{2,1,0:T(8,128)}, u32[]{:S(2)}) copy-start(f32[48,24,384]{2,1,0:T(8,128)} %param.9) | copy-start | bytes 5308420
  114.3 65.6 %all-to-all-start.2 = ((f32[128,6,1152]{2,1,0:T(8,128)}), f32[128,6,1152]{2,1,0:T(8,128)}, u32[]{:S(2)}, u32[]{:S(2)}) async-start(f32[128,6,1152]{2,1,0:T(8,128)} %pad_maximum_fusion), calls=%async_computation.2 | async-start | bytes 9437184 | tf_op jit(solution)/shard_map/all_to_all | solution.py:32
  209.3 17.2 %copy-start.2 = (f32[3,8,16,48,24]{4,3,2,1,0:T(8,128)S(1)}, f32[3,8,16,48,24]{4,3,2,1,0:T(8,128)}, u32[]{:S(2)}) copy-start(f32[3,8,16,48,24]{4,3,2,1,0:T(8,128)} %reshape.231) | copy-start | bytes 5308420
  209.3 27.9 %slice-start = ((s8[9437184]{0:T(1024)(128)(4,1)}), s8[4194304]{0:T(1024)(128)(4,1)S(1)}, s32[]{:S(2)}) async-start(s8[9437184]{0:T(1024)(128)(4,1)} %bitcast.150), calls=%async_computation.4 | async-start | bytes 8388608
  209.3 27.9 %slice-start.1 = ((s8[9437184]{0:T(1024)(128)(4,1)}), s8[4194304]{0:T(1024)(128)(4,1)S(1)}, s32[]{:S(2)}) async-start(s8[9437184]{0:T(1024)(128)(4,1)} %bitcast.150), calls=%async_computation.5 | async-start | bytes 8388608
  226.5 10.7 %slice-start.2 = ((s8[9437184]{0:T(1024)(128)(4,1)}), s8[1048576]{0:T(1024)(128)(4,1)S(1)}, s32[]{:S(2)}) async-start(s8[9437184]{0:T(1024)(128)(4,1)} %bitcast.150), calls=%async_computation.6 | async-start | bytes 2097152
  455.7 7.6 %copy-start.1 = (s32[32,128]{1,0:T(8,128)S(1)}, s32[32,128]{1,0:T(8,128)}, u32[]{:S(2)}) copy-start(s32[32,128]{1,0:T(8,128)} %param.6) | copy-start | bytes 49156
where the time goes:
time: 472 us; the launch traced here: 464 us
  matrix products  172 us (36%)
  local copies, waits for them, and re-layouts  78.9 us (17%)
  waiting for transfers between devices  72.5 us (15%)
  blocking collectives  70.1 us (15%)
  other arithmetic  52 us (11%)
  starting transfers between devices  17.9 us (4%)
    dot_general x18, matrix products, product(): return jnp.einsum(form, left, right, precision=lax.Precision.HIGHEST)  172 us
    all_to_all x1, blocking collectives, side_by_side(): lax.all_to_all(both, axis, split_axis=split_dim, concat_axis=concat_dim,...  70.1 us
    all_to_all x1, waiting for transfers between devices, side_by_side(): lax.all_to_all(both, axis, split_axis=split_dim, concat_axis=concat_dim,...  59.9 us
    scatter-add x1, other arithmetic, paint(): return empty.at[cell_rows.reshape(-1)].add(weights.reshape(-1))  43.6 us
    reshape x1, local copies, waits for them, and re-layouts, on_device(): got_real = got_real.reshape(slab_planes, count_x, count_y, rows_x, rows_y)  12.4 us
    reshape x1, local copies, waits for them, and re-layouts, on_device(): got_imag = got_imag.reshape(slab_planes, count_x, count_y, rows_x, rows_y)  10.9 us
  transfers between devices with their start and end apart: 3, of which 3 were waited for; matrix products, arithmetic and copies ran while one was open for 0% of the time, Pallas kernels for 0%

commit v1 on v0

v1 whole, which is shorter than its diff:
```python
import math

import jax
import jax.numpy as jnp
import ml_dtypes
import numpy as np
from jax import lax
from jax.experimental import pallas as pl
from jax.experimental.pallas import tpu as pltpu
from jax.sharding import PartitionSpec as P

NG = 384
SLOTS = 128
CAP = 4
RADIUS = 20
N_PX = 8
N_PY = 16
N_DEV = 128
CX = 48
CY = 24
ROWS = CX * CY
LB = ROWS // 128
AXES = ("px", "py")
BF = jnp.bfloat16
F32 = jnp.float32


def split_np(table):
    high = table.astype(ml_dtypes.bfloat16)
    low = (table - high.astype(np.float64)).astype(ml_dtypes.bfloat16)
    return high, low


def plane_tables():
    z = np.arange(NG)

    def rows(kz):
        angle = 2.0 * np.pi * ((kz * z) % NG) / NG
        return np.cos(angle), np.sin(angle)

    t_a = np.zeros((2, N_DEV, NG))
    t_bd = np.zeros((2, N_DEV, NG))
    t_bs = np.zeros((2, N_DEV, NG))
    t_c = np.zeros((2, N_DEV, NG))
    for d in range(N_DEV):
        t_a[0, d], t_a[1, d] = rows(d + 1)
        t_c[0, d], t_c[1, d] = rows(64 + d)
        if d < 63:
            t_bd[0, d], t_bd[1, d] = rows(129 + d)
        elif d < 126:
            t_bs[0, d], t_bs[1, d] = rows(d - 62)
        else:
            even = rows(0 if d == 126 else NG // 2)[0]
            t_bs[0, d] = even
            t_bd[1, d] = even
    return tuple(split_np(t.reshape(2 * N_DEV, NG)) for t in (t_a, t_bd, t_bs, t_c))


def real_form(cos_part, sin_part):
    return np.block([[cos_part, sin_part], [-sin_part, cos_part]])


def device_table():
    s = np.arange(N_DEV)
    i, q = s // N_PY, s % N_PY
    frac = np.outer(i, i) / N_PX + np.outer(q, q) / N_PY
    angle = 2.0 * np.pi * (frac % 1.0)
    return split_np(real_form(np.cos(angle), np.sin(angle)))


def lane_table():
    m = np.arange(NG)
    b, y = m // CY, m % CY
    frac = np.outer(b, b) / 16.0 + np.outer(y, y) / CY
    angle = 2.0 * np.pi * (frac % 1.0)
    return split_np(real_form(np.cos(angle), np.sin(angle)).T)


def twiddles():
    k = np.arange(N_DEV)
    kx, ky = k // N_PY, k % N_PY
    r = np.arange(ROWS)
    x, y = r // CY, r % CY
    angle = 2.0 * np.pi * ((np.outer(kx, x) + np.outer(ky, y)) % NG) / NG
    u = np.arange(3)
    b = np.arange(NG) // CY
    angle2 = 2.0 * np.pi * ((np.outer(u, b)) % 48) / 48.0
    tw1 = np.stack([np.cos(angle), np.sin(angle)]).astype(np.float32)
    tw2 = np.concatenate([np.cos(angle2), np.sin(angle2), np.zeros((2, NG))]).astype(np.float32)
    return tw1, tw2


def window(kz):
    row = lax.broadcasted_iota(jnp.int32, (NG, NG), 0)
    lane = lax.broadcasted_iota(jnp.int32, (NG, NG), 1)
    u, k1 = row // N_DEV, row % N_DEV
    kx = k1 // N_PY + N_PX * (u + 3 * (lane // CY))
    ky = k1 % N_PY + N_PY * (lane % CY)
    fx = jnp.where(kx < NG // 2, kx, kx - NG)
    fy = jnp.where(ky < NG // 2, ky, ky - NG)
    square = (fx * fx + fy * fy + kz * kz).astype(F32)
    radial = jnp.sqrt(square) * (2.0 * jnp.pi * RADIUS / NG)
    safe = jnp.where(radial > 0, radial, 1.0)
    value = 3.0 * (jnp.sin(safe) - safe * jnp.cos(safe)) / (safe * safe * safe)
    value = jnp.where(radial > 0, value, 1.0)
    both = (kz > 0) & (kz < NG // 2)
    return value * (jnp.where(both, 2.0, 1.0) / float(NG) ** 3)


def split(value):
    high = value.astype(BF)
    return high, (value - high.astype(F32)).astype(BF)


def dot(left, right, dims=((1,), (0,))):
    return lax.dot_general(left, right, (dims, ((), ())), preferred_element_type=F32)


def dot3(left, right, dims=((1,), (0,))):
    return (
        dot(left[0], right[0], dims) + dot(left[1], right[0], dims) + dot(left[0], right[1], dims)
    )


def sort_kernel(photons, cells, counts, owners, out):
    blocks = photons.shape[0]
    lane = lax.broadcasted_iota(jnp.int32, (blocks, SLOTS), 1)
    live = lane < counts[...]
    weight = jnp.where(live, photons[...], 0.0)
    where = jnp.where(live, cells[...], 0).astype(F32)
    hot = jnp.where(lane == owners[...], 1.0, 0.0)
    tri = jnp.where(
        lax.broadcasted_iota(jnp.int32, (blocks, blocks), 0)
        >= lax.broadcasted_iota(jnp.int32, (blocks, blocks), 1),
        1.0,
        0.0,
    )
    rank = jnp.sum(dot(tri.astype(BF), hot.astype(BF)) * hot, axis=1, keepdims=True) - 1.0
    place = owners[...] * CAP + rank.astype(jnp.int32)
    place_hot = jnp.where(lane == place, 1.0, 0.0).astype(BF)
    slots = N_PY * CAP
    for half, value in enumerate((weight, where)):
        first, rest = value.astype(BF), value
        total = None
        for _ in range(3):
            first = rest.astype(BF)
            rest = rest - first.astype(F32)
            part = dot(place_hot, first, ((0,), (0,)))
            total = part if total is None else total + part
        out[pl.ds(half, slots, stride=2), :] = total[:slots]


def z_first_kernel(density, t_high, t_low, out):
    high, low = split(density[...])
    planes = dot3((t_high[...], t_low[...]), (high, low), ((1,), (1,)))
    store_rows(out, planes, 0, 2 * LB)


def store_rows(out, planes, base, pitch):
    for c in range(2):
        for j in range(LB):
            out[pl.ds(base + c * LB + j, N_DEV, stride=pitch), :] = planes[
                c * N_DEV : (c + 1) * N_DEV, j * 128 : (j + 1) * 128
            ]


def paint_kernel(weights, cells, counts, density, *rest):
    tables, (out, field, high, low) = rest[:6], rest[6:]
    (bd_high, bd_low, bs_high, bs_low, c_high, c_low) = tables
    step = 8
    field[...] = jnp.zeros(field.shape, F32)
    lane = lax.broadcasted_iota(jnp.int32, (1, 128), 1)

    def block(index, carry):
        def some(part, inner):
            for k in range(step):
                cell = cells[index, part * step + k]
                value = weights[index, part * step + k]
                row = lax.shift_right_logical(cell, 7)
                here = lane == (cell & 127)
                field[pl.ds(row, 1), :] += jnp.where(here, value, 0.0)
            return inner

        return lax.fori_loop(0, (counts[index] + step - 1) // step, some, carry)

    lax.fori_loop(0, counts.shape[0], block, 0)
    for k in range(3):
        part_high, part_low = split(field[pl.ds(k, ROWS, stride=3), :])
        high[:, k * 128 : (k + 1) * 128] = part_high
        low[:, k * 128 : (k + 1) * 128] = part_low
    source = (high[...], low[...])
    nt = ((1,), (1,))
    planes = dot3((bs_high[...], bs_low[...]), source, nt)
    planes = planes + dot3((bd_high[...], bd_low[...]), split(density[...]), nt)
    store_rows(out, planes, 0, 4 * LB)
    store_rows(out, dot3((c_high[...], c_low[...]), source, nt), 2 * LB, 4 * LB)


HALF_ROOT3 = math.sqrt(3.0) / 2.0


def middle_kernel(planes, got, dev_high, dev_low, lane_high, lane_low, tw1, tw2, win, out,
                  work, r_high, r_low, l_high, l_low):
    pitch = planes * 2 * LB
    nt = ((1,), (1,))
    for p in range(planes):
        for c in range(2):
            for j in range(LB):
                high, low = split(got[pl.ds((p * 2 + c) * LB + j, N_DEV, stride=pitch), :])
                r_high[c * N_DEV : (c + 1) * N_DEV, j * 128 : (j + 1) * 128] = high
                r_low[c * N_DEV : (c + 1) * N_DEV, j * 128 : (j + 1) * 128] = low
        dev = (dev_high[...], dev_low[...])
        for a in range(3):
            at = slice(a * NG, (a + 1) * NG)
            work[:, at] = dot3(dev, (r_high[:, at], r_low[:, at]))

        def forward(block, carry):
            rows = pl.ds(pl.multiple_of(block * 16, 16), 16)
            rows_im = pl.ds(pl.multiple_of(block * 16 + N_DEV, 16), 16)
            re, im = [], []
            for a in range(3):
                at = slice(a * NG, (a + 1) * NG)
                cos, sin = tw1[0, rows, at], tw1[1, rows, at]
                x, y = work[rows, at], work[rows_im, at]
                re.append(x * cos + y * sin)
                im.append(y * cos - x * sin)
            t_re, t_im = re[1] + re[2], im[1] + im[2]
            d_re, d_im = (re[1] - re[2]) * HALF_ROOT3, (im[1] - im[2]) * HALF_ROOT3
            m_re, m_im = re[0] - 0.5 * t_re, im[0] - 0.5 * t_im
            y_re = (re[0] + t_re, m_re + d_im, m_re - d_im)
            y_im = (im[0] + t_im, m_im - d_re, m_im + d_re)
            for u in range(3):
                cos, sin = tw2[u : u + 1, :], tw2[3 + u : 4 + u, :]
                value_re = y_re[u] * cos + y_im[u] * sin
                value_im = y_im[u] * cos - y_re[u] * sin
                to = pl.ds(pl.multiple_of(block * 16 + u * N_DEV, 16), 16)
                l_high[to, :NG], l_low[to, :NG] = split(value_re)
                l_high[to, NG:], l_low[to, NG:] = split(value_im)
            return carry

        lax.fori_loop(0, N_DEV // 16, forward, 0)
        mat = (lane_high[...], lane_low[...])
        for u in range(3):
            at = slice(u * N_DEV, (u + 1) * N_DEV)
            value = dot3((l_high[at, :], l_low[at, :]), mat)
            w = win[p, at, :]
            l_high[at, :NG], l_low[at, :NG] = split(value[:, :NG] * w)
            l_high[at, NG:], l_low[at, NG:] = split(value[:, NG:] * w)
            value = dot3((l_high[at, :], l_low[at, :]), mat, nt)
            work[0:N_DEV, u * NG : (u + 1) * NG] = value[:, :NG]
            work[N_DEV:, u * NG : (u + 1) * NG] = value[:, NG:]

        def backward(block, carry):
            rows = pl.ds(pl.multiple_of(block * 16, 16), 16)
            rows_im = pl.ds(pl.multiple_of(block * 16 + N_DEV, 16), 16)
            re, im = [], []
            for u in range(3):
                at = slice(u * NG, (u + 1) * NG)
                cos, sin = tw2[u : u + 1, :], tw2[3 + u : 4 + u, :]
                x, y = work[rows, at], work[rows_im, at]
                re.append(x * cos - y * sin)
                im.append(y * cos + x * sin)
            t_re, t_im = re[1] + re[2], im[1] + im[2]
            d_re, d_im = (re[1] - re[2]) * HALF_ROOT3, (im[1] - im[2]) * HALF_ROOT3
            m_re, m_im = re[0] - 0.5 * t_re, im[0] - 0.5 * t_im
            y_re = (re[0] + t_re, m_re - d_im, m_re + d_im)
            y_im = (im[0] + t_im, m_im + d_re, m_im - d_re)
            for a in range(3):
                at = slice(a * NG, (a + 1) * NG)
                cos, sin = tw1[0, rows, at], tw1[1, rows, at]
                r_high[rows, at], r_low[rows, at] = split(y_re[a] * cos - y_im[a] * sin)
                r_high[rows_im, at], r_low[rows_im, at] = split(y_im[a] * cos + y_re[a] * sin)
            return carry

        lax.fori_loop(0, N_DEV // 16, backward, 0)
        tn = ((0,), (0,))
        for a in range(3):
            at = slice(a * NG, (a + 1) * NG)
            value = dot3(dev, (r_high[:, at], r_low[:, at]), tn)
            for c in range(2):
                for j in range(3):
                    out[pl.ds((p * 2 + c) * LB + a * 3 + j, N_DEV, stride=pitch), :] = value[
                        c * N_DEV : (c + 1) * N_DEV, j * 128 : (j + 1) * 128
                    ]


def load_rows(got, base, pitch):
    parts = [
        jnp.concatenate(
            [got[pl.ds(base + c * LB + j, N_DEV, stride=pitch), :] for j in range(LB)], axis=1
        )
        for c in range(2)
    ]
    return split(jnp.concatenate(parts, axis=0))


def z_last_kernel(got_a, got_bc, *rest):
    tables, out = rest[:8], rest[8]
    (a_high, a_low, bd_high, bd_low, bs_high, bs_low, c_high, c_low) = tables
    tn = ((0,), (0,))
    part_a = load_rows(got_a, 0, 2 * LB)
    part_b = load_rows(got_bc, 0, 4 * LB)
    part_c = load_rows(got_bc, 2 * LB, 4 * LB)
    for k in range(LB):
        at = slice(k * 128, (k + 1) * 128)

        def pick(part):
            return part[0][:, at], part[1][:, at]

        dens = dot3(pick(part_a), (a_high[...], a_low[...]), tn)
        dens = dens + dot3(pick(part_b), (bd_high[...], bd_low[...]), tn)
        phot = dot3(pick(part_b), (bs_high[...], bs_low[...]), tn)
        phot = phot + dot3(pick(part_c), (c_high[...], c_low[...]), tn)
        out[at, :] = jnp.clip(phot / jnp.maximum(dens, 0.5), 0.0, 1.0)


def shape(*dims, dtype=F32):
    return jax.ShapeDtypeStruct(dims, dtype)


def exchange(rows, planes):
    width = planes * 2 * ROWS
    send = rows.reshape(N_DEV, 1, width)
    return lax.all_to_all(send, AXES, 0, 0, tiled=True).reshape(N_DEV * width // 128, 128)


def middle(got, planes, dev, lanes, tw, win):
    import functools

    return pl.pallas_call(
        functools.partial(middle_kernel, planes),
        out_shape=shape(N_DEV * planes * 2 * LB, 128),
        scratch_shapes=[
            pltpu.VMEM((2 * N_DEV, ROWS), F32),
            pltpu.VMEM((2 * N_DEV, ROWS), BF),
            pltpu.VMEM((2 * N_DEV, ROWS), BF),
            pltpu.VMEM((NG, 2 * NG), BF),
            pltpu.VMEM((NG, 2 * NG), BF),
        ],
        name=f"middle{planes}",
    )(got, *dev, *lanes, *tw, win)


def on_device(photons, halo_cells, halo_counts, owners, density):
    rows_density = density.reshape(ROWS, NG)
    t_a, t_bd, t_bs, t_c = plane_tables()
    dev, lanes, tw = device_table(), lane_table(), twiddles()

    send = pl.pallas_call(sort_kernel, out_shape=shape(N_PY * CAP * 2, SLOTS), name="sort")(
        photons, halo_cells, halo_counts.reshape(-1, 1), owners
    )
    got = lax.all_to_all(
        send.reshape(N_PY, 2 * CAP, SLOTS), "py", 0, 0, tiled=True
    ).reshape(N_PY * CAP, 2, SLOTS)
    weights, cells = got[:, 0], got[:, 1].astype(jnp.int32)
    slot = jnp.arange(1, SLOTS + 1, dtype=jnp.int32)[None, :]
    counts = jnp.max(jnp.where(weights != 0, slot, 0), axis=1)

    send_a = pl.pallas_call(z_first_kernel, out_shape=shape(N_DEV * 2 * LB, 128), name="zfirst")(
        rows_density, *t_a
    )
    send_a, counts = lax.optimization_barrier((send_a, counts))
    got_a = exchange(send_a, 1)

    smem = pl.BlockSpec(memory_space=pltpu.SMEM)
    vmem = pl.BlockSpec(memory_space=pltpu.VMEM)
    send_bc = pl.pallas_call(
        paint_kernel,
        out_shape=shape(N_DEV * 4 * LB, 128),
        in_specs=[smem, smem, smem] + [vmem] * 7,
        scratch_shapes=[
            pltpu.VMEM((ROWS * 3, 128), F32),
            pltpu.VMEM((ROWS, NG), BF),
            pltpu.VMEM((ROWS, NG), BF),
        ],
        name="paint",
    )(weights, cells, counts, rows_density, *t_bd, *t_bs, *t_c)
    got_a, send_bc = lax.optimization_barrier((got_a, send_bc))
    got_bc = exchange(send_bc, 2)

    me = lax.axis_index(AXES)
    kz_b = jnp.where(me < 63, 129 + me, jnp.where(me < 126, me - 62, (me - 126) * (NG // 2)))
    win_a = window(me + 1)[None]
    win_bc = jnp.stack([window(kz_b), window(me + 64)])
    back_a = middle(got_a, 1, dev, lanes, tw, win_a)
    got_bc, back_a = lax.optimization_barrier((got_bc, back_a))
    home_a = exchange(back_a, 1)
    back_bc = middle(got_bc, 2, dev, lanes, tw, win_bc)
    home_a, back_bc = lax.optimization_barrier((home_a, back_bc))
    home_bc = exchange(back_bc, 2)
    fraction = pl.pallas_call(z_last_kernel, out_shape=shape(ROWS, NG), name="zlast")(
        home_a, home_bc, *t_a, *t_bd, *t_bs, *t_c
    )
    return fraction.reshape(CX, CY, NG)


def solution(mesh):
    placed = (
        P(("px", "py"), None),
        P(("px", "py"), None),
        P(("px", "py")),
        P(("px", "py"), None),
        P("px", "py", None),
    )
    return jax.shard_map(
        on_device, mesh=mesh, in_specs=placed, out_specs=P("px", "py", None), check_vma=False
    )
```

time: 472 us -> 178 us (0.38); the launches traced: 464 us -> 175 us
  matrix products: 172 us -> 0 us
  local copies, waits for them, and re-layouts: 78.9 us -> 5.16 us
  Pallas kernels: 0 us -> 61.9 us
  waiting for transfers between devices: 72.5 us -> 15.2 us
  other arithmetic: 52 us -> 12.9 us
  blocking collectives: 70.1 us -> 41.7 us
  starting transfers between devices: 17.9 us -> 37.6 us
    dot_general x18 -> x0, matrix products: 172 us -> none  [product(): return jnp.einsum(form, left, right, precision=lax.Precision.HIGHEST)]
    pallas_call x0 -> x6, Pallas kernels: none -> 61.9 us  [the longest x2 31.5 us: middle(): pl.pallas_call(functools.partial(middle_kernel, planes), out_shape=shape(...]
    all_to_all x3 -> x4, waiting for transfers between devices: 72.5 us -> 15.2 us  [the longest x3 11.7 us: exchange(): lax.all_to_all(send, AXES, 0, 0, tiled=True)]
    scatter-add x1 -> x0, other arithmetic: 43.6 us -> none  [paint(): return empty.at[cell_rows.reshape(-1)].add(weights.reshape(-1))]
    reshape x7 -> x1, local copies, waits for them, and re-layouts: 44.8 us -> 1.34 us  [on_device(): halo_counts.reshape(-1, 1)]
    all_to_all x1, blocking collectives: 70.1 us -> 41.7 us  [exchange(): lax.all_to_all(send, AXES, 0, 0, tiled=True)]
    all_to_all x3 -> x4, starting transfers between devices: 17.9 us -> 37.6 us  [the longest x3 29 us: exchange(): lax.all_to_all(send, AXES, 0, 0, tiled=True)]
    mul x4 -> x1, other arithmetic: 0.03 us -> 9.22 us  [window(): return value * (jnp.where(both, 2.0, 1.0) / float(NG) ** 3)]
  transfers between devices with their start and end apart: 3 -> 4, of which waited for: 3 -> 3; matrix products, arithmetic and copies ran while one was open for 0% -> 7% of each run, Pallas kernels for 0% -> 30%
where the time goes in v1:
time: 178 us; the launch traced here: 175 us
  Pallas kernels  61.9 us (35%)
  blocking collectives  41.7 us (23%)
  starting transfers between devices  37.6 us (21%)
  waiting for transfers between devices  15.2 us (9%)
  other arithmetic  12.9 us (7%)
  local copies, waits for them, and re-layouts  5.16 us (3%)
    all_to_all x1, blocking collectives, exchange(): lax.all_to_all(send, AXES, 0, 0, tiled=True)  41.7 us
    pallas_call x2, Pallas kernels, middle(): pl.pallas_call(functools.partial(middle_kernel, planes), out_shape=shape(...  31.5 us
    all_to_all x3, starting transfers between devices, exchange(): lax.all_to_all(send, AXES, 0, 0, tiled=True)  29 us
    pallas_call x1, Pallas kernels, on_device(): pl.pallas_call(paint_kernel, out_shape=shape(N_DEV * 4 * LB, 128), in_spe...  17.2 us
    all_to_all x3, waiting for transfers between devices, exchange(): lax.all_to_all(send, AXES, 0, 0, tiled=True)  11.7 us
    mul x1, other arithmetic, window(): return value * (jnp.where(both, 2.0, 1.0) / float(NG) ** 3)  9.22 us
    all_to_all x1, starting transfers between devices, on_device(): lax.all_to_all(send.reshape(N_PY, 2 * CAP, SLOTS), 'py', 0, 0, tiled=True)  8.63 us
    pallas_call x1, Pallas kernels, on_device(): pl.pallas_call(z_last_kernel, out_shape=shape(ROWS, NG), name='zlast')  7.52 us
  transfers between devices with their start and end apart: 4, of which 3 were waited for; matrix products, arithmetic and copies ran while one was open for 7% of the time, Pallas kernels for 30%

profile of v1, /device:TPU:7, one launch (start us, length us, event | category | flops | bytes accessed | tf_op | source)
XLA Modules:
  0.0 174.5 jit_solution(8332006694906720679)
XLA Ops:
  0.0 1.3 copy.26.counts
  1.3 1.3 copy.27.owners
  2.7 2.0 %sort.1 = f32[128,128]{1,0:T(8,128)} custom-call(f32[32,128]{1,0:T(8,128)} %photons.1, s32[32,128]{1,0:T(8,128)} %cells.1, s32[32,1]{1,0:T(8,128)} %copy.26.counts, s32[32,1]{1,0:T(8,128)} %copy.27.owners), custom_call_target="tpu_custom_call" | custom-call | tf_op jit(solution)/shard_map/sort/pallas_call | solution.py:349
  4.6 8.6 %all-to-all-start = ((f32[16,8,128]{2,1,0:T(8,128)}), f32[16,8,128]{2,1,0:T(8,128)S(1)}, u32[]{:S(2)}, u32[]{:S(2)}) async-start(f32[16,8,128]{2,1,0:T(8,128)} %bitcast.32), calls=%async_computation | async-start | bytes 131072 | tf_op jit(solution)/shard_map/all_to_all | solution.py:352
  13.3 3.8 %zfirst.1 = f32[2304,128]{1,0:T(8,128)} custom-call(f32[1152,384]{1,0:T(8,128)} %bitcast.23, bf16[256,384]{1,0:T(8,128)(2,1)} %constant.176.clone.t_high.rest_0_, bf16[256,384]{1,0:T(8,128)(2,1)} %constant.177.clone.t_low.rest_1_), custom_call_target="tpu_custom_call" | custom-call | tf_op jit(solution)/shard_map/zfirst/pallas_call | solution.py:359
  17.1 3.5 %all-to-all-done = f32[16,8,128]{2,1,0:T(8,128)S(1)} async-done(((f32[16,8,128]{2,1,0:T(8,128)}), f32[16,8,128]{2,1,0:T(8,128)S(1)}, u32[]{:S(2)}, u32[]{:S(2)}) %all-to-all-start) | async-done | bytes 65568 | tf_op jit(solution)/shard_map/all_to_all | solution.py:352
  20.6 0.1 fusion.35
  20.7 0.0 copy-start.3
  20.7 0.7 select_reduce_fusion.counts
  21.4 0.0 copy-done.3
  21.4 5.9 %all-to-all-start.1 = ((f32[128,1,2304]{2,1,0:T(1,128)}), f32[128,1,2304]{2,1,0:T(1,128)S(1)}, u32[]{:S(2)}, u32[]{:S(2)}) async-start(f32[128,1,2304]{2,1,0:T(1,128)} %bitcast.25), calls=%async_computation.1 | async-start | bytes 2359296 | tf_op jit(solution)/shard_map/all_to_all | solution.py:324
  27.2 0.6 convert_bitcast_fusion.cells
  27.8 17.2 %paint.1 = f32[4608,128]{1,0:T(8,128)} custom-call(f32[64,128]{1,0:T(8,128)} %bitcast.30, s32[64,128]{1,0:T(8,128)} %convert_bitcast_fusion.cells, s32[64]{0:T(128)} %select_reduce_fusion.counts, f32[1152,384]{1,0:T(8,128)} %bitcast.24, bf16[256,384]{1,0:T(8,128)(2,1)} %constant.178.clone.rest_0_.rest_2_, bf16[256,384]{1,0:T(8,128)(2,1)} %constant.179.clone.rest_1_.rest_3_, ...), custom_call_target="tpu_custom_call" | custom-call | tf_op jit(solution)/shard_map/paint/pallas_call | solution.py:367
  45.0 0.7 all-to-all-done.1
  45.7 0.0 copy-start.1
  45.7 1.0 copy-done.1
  46.7 16.1 %all-to-all-start.2 = ((f32[128,1,4608]{2,1,0:T(1,128)}), f32[128,1,4608]{2,1,0:T(1,128)S(1)}, u32[]{:S(2)}, u32[]{:S(2)}) async-start(f32[128,1,4608]{2,1,0:T(1,128)} %bitcast.22), calls=%async_computation.2 | async-start | bytes 4718592 | tf_op jit(solution)/shard_map/all_to_all | solution.py:324
  62.9 9.2 %fusion.1 = (f32[1,384,384]{2,1,0:T(8,128)}, f32[1,384,384]{2,1,0:T(8,128)}, f32[1,384,384]{2,1,0:T(8,128)}) fusion(f32[]{:T(128)S(6)} %div.105, s32[]{:T(128)S(6)} %mul.339, s32[384]{0:T(512)S(1)} %get-tuple-element.29, s32[384]{0:T(512)S(1)} %get-tuple-element.30, pred[384]{0:T(512)(128)(4,1)S(1)} %get-tuple-element.33, s32[384]{0:T(512)S(1)} %get-tuple-element.28, ...), kind=kLoop, calls=%fused_computation.24 | loop fusion | flops 11354112 | bytes 1783320 | tf_op jit(solution)/shard_map/mul | solution.py:107
  72.1 11.4 %middle1.1 = f32[2304,128]{1,0:T(8,128)} custom-call(f32[2304,128]{1,0:T(8,128)} %bitcast.26, bf16[256,256]{1,0:T(8,128)(2,1)} %constant.184.clone.dev_high, bf16[256,256]{1,0:T(8,128)(2,1)} %constant.185.clone.dev_low, bf16[768,768]{1,0:T(8,128)(2,1)} %constant.186.clone.lane_high, bf16[768,768]{1,0:T(8,128)(2,1)} %constant.187.clone.lane_low, ...), custom_call_target="tpu_custom_call" | custom-call | tf_op jit(solution)/shard_map/middle1/pallas_call | solution.py:330
  83.6 11.0 %all-to-all-done.2 = f32[128,1,4608]{2,1,0:T(1,128)S(1)} async-done(((f32[128,1,4608]{2,1,0:T(1,128)}), f32[128,1,4608]{2,1,0:T(1,128)S(1)}, u32[]{:S(2)}, u32[]{:S(2)}) %all-to-all-start.2) | async-done | bytes 2359328 | tf_op jit(solution)/shard_map/all_to_all | solution.py:324
  94.6 0.0 copy-start
  94.6 1.4 copy-done
  96.0 7.0 %all-to-all-start.3 = ((f32[128,1,2304]{2,1,0:T(1,128)}), f32[128,1,2304]{2,1,0:T(1,128)S(1)}, u32[]{:S(2)}, u32[]{:S(2)}) async-start(f32[128,1,2304]{2,1,0:T(1,128)} %bitcast.28), calls=%async_computation.3 | async-start | bytes 2359296 | tf_op jit(solution)/shard_map/all_to_all | solution.py:324
  103.0 2.3 %pad_maximum_fusion.win = f32[2,384,384]{2,1,0:T(8,128)} fusion(f32[1,384,384]{2,1,0:T(8,128)} %get-tuple-element.24, f32[1,384,384]{2,1,0:T(8,128)} %get-tuple-element.23), kind=kLoop, calls=%fused_computation.6 | loop fusion | flops 294912 | bytes 2359296 | tf_op jit(solution)/shard_map/stack | solution.py:384
  105.3 20.0 %middle2.1 = f32[4608,128]{1,0:T(8,128)} custom-call(f32[4608,128]{1,0:T(8,128)} %bitcast.19, bf16[256,256]{1,0:T(8,128)(2,1)} %constant.184.clone.dev_high, bf16[256,256]{1,0:T(8,128)(2,1)} %constant.185.clone.dev_low, bf16[768,768]{1,0:T(8,128)(2,1)} %constant.186.clone.lane_high, bf16[768,768]{1,0:T(8,128)(2,1)} %constant.187.clone.lane_low, ...), custom_call_target="tpu_custom_call" | custom-call | tf_op jit(solution)/shard_map/middle2/pallas_call | solution.py:330
  125.3 0.0 all-to-all-done.3
  125.3 0.0 copy-start.2
  125.3 41.7 %all_to_all.25 = f32[128,1,4608]{2,1,0:T(1,128)} all-to-all(f32[128,1,4608]{2,1,0:T(1,128)} %bitcast.20), channel_id=1, replica_groups=mesh['px'=8,'py'=16] {'px','py'}, dimensions={0} | all-to-all | bytes 4718592 | tf_op jit(solution)/shard_map/all_to_all | solution.py:324
  167.0 0.0 copy-done.2
  167.0 7.5 %zlast.1 = f32[1152,384]{1,0:T(8,128)} custom-call(f32[2304,128]{1,0:T(8,128)} %bitcast.27, f32[4608,128]{1,0:T(8,128)} %bitcast.21, bf16[256,384]{1,0:T(8,128)(2,1)} %constant.176.clone.t_high.rest_0_, bf16[256,384]{1,0:T(8,128)(2,1)} %constant.177.clone.t_low.rest_1_, bf16[256,384]{1,0:T(8,128)(2,1)} %constant.178.clone.rest_0_.rest_2_, ...), custom_call_target="tpu_custom_call" | custom-call | tf_op jit(solution)/shard_map/zlast/pallas_call | solution.py:391
  (7 shorter events, 0.0 us)
Async XLA Ops:
  4.6 16.0 %all-to-all-start = ((f32[16,8,128]{2,1,0:T(8,128)}), f32[16,8,128]{2,1,0:T(8,128)S(1)}, u32[]{:S(2)}, u32[]{:S(2)}) async-start(f32[16,8,128]{2,1,0:T(8,128)} %bitcast.32), calls=%async_computation | async-start | bytes 131072 | tf_op jit(solution)/shard_map/all_to_all | solution.py:352
  20.7 0.7 copy-start.3
  21.4 24.3 %all-to-all-start.1 = ((f32[128,1,2304]{2,1,0:T(1,128)}), f32[128,1,2304]{2,1,0:T(1,128)S(1)}, u32[]{:S(2)}, u32[]{:S(2)}) async-start(f32[128,1,2304]{2,1,0:T(1,128)} %bitcast.25), calls=%async_computation.1 | async-start | bytes 2359296 | tf_op jit(solution)/shard_map/all_to_all | solution.py:324
  45.7 1.0 copy-start.1
  46.7 47.9 %all-to-all-start.2 = ((f32[128,1,4608]{2,1,0:T(1,128)}), f32[128,1,4608]{2,1,0:T(1,128)S(1)}, u32[]{:S(2)}, u32[]{:S(2)}) async-start(f32[128,1,4608]{2,1,0:T(1,128)} %bitcast.22), calls=%async_computation.2 | async-start | bytes 4718592 | tf_op jit(solution)/shard_map/all_to_all | solution.py:324
  94.6 1.4 copy-start
  96.0 29.3 %all-to-all-start.3 = ((f32[128,1,2304]{2,1,0:T(1,128)}), f32[128,1,2304]{2,1,0:T(1,128)S(1)}, u32[]{:S(2)}, u32[]{:S(2)}) async-start(f32[128,1,2304]{2,1,0:T(1,128)} %bitcast.28), calls=%async_computation.3 | async-start | bytes 2359296 | tf_op jit(solution)/shard_map/all_to_all | solution.py:324
  125.3 41.7 %copy-start.2 = (f32[128,1,2304]{2,1,0:T(1,128)}, f32[128,1,2304]{2,1,0:T(1,128)S(1)}, u32[]{:S(2)}) copy-start(f32[128,1,2304]{2,1,0:T(1,128)S(1)} %all-to-all-done.3) | copy-start | bytes 3538948

commit v2 on v0

v2 whole, which is shorter than its diff:
```python
import functools
import math

import jax
import jax.numpy as jnp
import ml_dtypes
import numpy as np
from jax import lax
from jax.experimental import pallas as pl
from jax.experimental.pallas import tpu as pltpu
from jax.sharding import PartitionSpec as P

NG = 384
SLOTS = 128
CAP = 4
RADIUS = 20
N_PX = 8
N_PY = 16
N_DEV = 128
CX = 48
CY = 24
ROWS = CX * CY
LB = ROWS // 128
PLANES = 3
WIDTH = 2 * LB
PITCH = PLANES * WIDTH
FIELDS = 4
AXES = ("px", "py")
BF = jnp.bfloat16
F32 = jnp.float32
NT = ((1,), (1,))
NN = ((1,), (0,))
TN = ((0,), (0,))
HALF_ROOT3 = math.sqrt(3.0) / 2.0

LANE_A, LANE_A2, LANE_B, LANE_Y = (
    g.reshape(-1) for g in np.meshgrid(range(3), range(3), range(16), range(8), indexing="ij")
)
LANE_CX = 16 * LANE_A + LANE_B
LANE_CY = 8 * LANE_A2 + LANE_Y


def split_np(table):
    high = table.astype(ml_dtypes.bfloat16)
    low = (table - high.astype(np.float64)).astype(ml_dtypes.bfloat16)
    return high, low


def z_table():
    z = np.arange(NG)
    table = np.zeros((3 * N_DEV, NG))
    for d in range(N_DEV):
        angle = 2.0 * np.pi * (((64 + d) * z) % NG) / NG
        table[d], table[N_DEV + d] = np.cos(angle), np.sin(angle)
    for d in range(N_DEV // 2):
        angle = 2.0 * np.pi * ((d * z) % NG) / NG
        table[2 * N_DEV + d], table[2 * N_DEV + 64 + d] = np.cos(angle), np.sin(angle)
    table[2 * N_DEV + 64] = 1.0 - 2.0 * (z % 2)
    return split_np(table)


def real_form(frac):
    angle = 2.0 * np.pi * (frac % 1.0)
    cos, sin = np.cos(angle), np.sin(angle)
    return np.block([[cos, sin], [-sin, cos]])


def device_table():
    s = np.arange(N_DEV)
    i, q = s // N_PY, s % N_PY
    return split_np(real_form(np.outer(i, i) / N_PX + np.outer(q, q) / N_PY))


def lane_table():
    m = np.arange(128)
    b, y = m // 8, m % 8
    return split_np(real_form(np.outer(b, b) / 16.0 + np.outer(y, y) / 8.0).T)


def twiddles():
    angle_x = 2.0 * np.pi * np.outer(np.arange(N_PX), LANE_CX) / NG
    angle_y = 2.0 * np.pi * np.outer(np.arange(N_PY), LANE_CY) / NG
    tw_x = np.stack([np.cos(angle_x), np.sin(angle_x)]).astype(np.float32)
    tw_y = np.stack([np.cos(angle_y), np.sin(angle_y)]).astype(np.float32)
    angle2 = 2.0 * np.pi * (LANE_B * LANE_A / 48.0 + LANE_Y * LANE_A2 / 24.0)
    tw2 = np.zeros((8, ROWS), np.float32)
    tw2[0], tw2[1] = np.cos(angle2), np.sin(angle2)
    return tw_x, tw_y, tw2


def window(kz):
    row = lax.broadcasted_iota(jnp.int32, (ROWS, 128), 0)
    lane = lax.broadcasted_iota(jnp.int32, (ROWS, 128), 1)
    u, k1 = row // N_DEV, row % N_DEV
    kx = k1 // N_PY + N_PX * (u // 3 + 3 * (lane // 8))
    ky = k1 % N_PY + N_PY * (u % 3 + 3 * (lane % 8))
    fx = jnp.where(kx < NG // 2, kx, kx - NG)
    fy = jnp.where(ky < NG // 2, ky, ky - NG)
    square = (fx * fx + fy * fy + kz * kz).astype(F32)
    radial = jnp.sqrt(square) * (2.0 * jnp.pi * RADIUS / NG)
    safe = jnp.where(radial > 0, radial, 1.0)
    value = 3.0 * (jnp.sin(safe) - safe * jnp.cos(safe)) / (safe * safe * safe)
    value = jnp.where(radial > 0, value, 1.0)
    both = (kz > 0) & (kz < NG // 2)
    return value * (jnp.where(both, 2.0, 1.0) / float(NG) ** 3)


def split(value):
    high = value.astype(BF)
    return high, (value - high.astype(F32)).astype(BF)


def dot(left, right, dims=NN):
    return lax.dot_general(left, right, (dims, ((), ())), preferred_element_type=F32)


def dot3(left, right, dims=NN):
    return (
        dot(left[0], right[0], dims) + dot(left[1], right[0], dims) + dot(left[0], right[1], dims)
    )


def sort_kernel(photons, cells, counts, owners, out):
    blocks = photons.shape[0]
    slots = N_PY * CAP
    target = owners[...]
    hot = jnp.where(
        lax.broadcasted_iota(jnp.int32, (N_PY, blocks), 0) == target, 1.0, 0.0
    )
    before = jnp.where(
        lax.broadcasted_iota(jnp.int32, (blocks, blocks), 0)
        < lax.broadcasted_iota(jnp.int32, (blocks, blocks), 1),
        1.0,
        0.0,
    )
    rank = jnp.sum(dot(hot.astype(BF), before.astype(BF)) * hot, axis=0, keepdims=True)
    place = target * CAP + rank.astype(jnp.int32)
    place_hot = jnp.where(
        lax.broadcasted_iota(jnp.int32, (slots, blocks), 0) == place, 1.0, 0.0
    )
    count = jnp.sum(place_hot * counts[...].astype(F32), axis=1, keepdims=True)
    live = lax.broadcasted_iota(jnp.int32, (slots, SLOTS), 1) < count.astype(jnp.int32)
    place_hot = place_hot.astype(BF)
    for half, value in enumerate((photons[...], cells[...].astype(F32))):
        rest, total = value, None
        for _ in range(3):
            first = rest.astype(BF)
            rest = rest - first.astype(F32)
            part = dot(place_hot, first)
            total = part if total is None else total + part
        out[pl.ds(half, slots, stride=2), :] = jnp.where(live, total, 0.0)


def z_density_kernel(density, t_high, t_low, out, few, high, low):
    for a in range(3):
        for a2 in range(3):
            block = density[a * 16 : (a + 1) * 16, a2 * 8 : (a2 + 1) * 8, :].reshape(128, NG)
            at = slice((a * 3 + a2) * 128, (a * 3 + a2 + 1) * 128)
            high[at, :], low[at, :] = split(block)
    for part in range(3):
        at = slice(part * N_DEV, (part + 1) * N_DEV)
        value = dot3((t_high[at, :], t_low[at, :]), (high[...], low[...]), NT)
        if part < 2:
            store_plane(out, part * LB, WIDTH, value)
        else:
            few[...] = value


def store_plane(out, start, pitch, value):
    for j in range(LB):
        rows = pl.ds(start + j, value.shape[0], stride=pitch)
        out[rows, :] = value[:, j * 128 : (j + 1) * 128]


def paint_kernel(weights, cells, counts, z_density, t_high, t_low, out, *scratch):
    fields, high, low = scratch[:FIELDS], scratch[FIELDS], scratch[FIELDS + 1]
    step = 8
    for field in fields:
        field[...] = jnp.zeros(field.shape, F32)
    lane = lax.broadcasted_iota(jnp.int32, (1, 128), 1)

    def block(index, carry):
        count = counts[index]
        for begin in range(0, SLOTS, step):

            @pl.when(count > begin)
            def _():
                for k in range(step):
                    cell = cells[index, begin + k]
                    value = weights[index, begin + k]
                    row = lax.shift_right_logical(cell, 7)
                    here = lane == (jnp.full((1, 128), cell, jnp.int32) & 127)
                    fields[k % FIELDS][pl.ds(row, 1), :] += jnp.where(here, value, 0.0)

        return carry

    lax.fori_loop(0, counts.shape[0], block, 0)
    for part in range(3):
        for a in range(3):
            for a2 in range(3):
                tiles = []
                for b in range(16):
                    row = (16 * a + b) * CY + 8 * a2
                    tile = fields[0][pl.ds(row * 3 + part, 8, stride=3), :]
                    for field in fields[1:]:
                        tile = tile + field[pl.ds(row * 3 + part, 8, stride=3), :]
                    tiles.append(tile)
                at = slice((a * 3 + a2) * 128, (a * 3 + a2 + 1) * 128)
                to = slice(part * 128, (part + 1) * 128)
                high[at, to], low[at, to] = split(jnp.concatenate(tiles, axis=0))
    source = (high[...], low[...])
    pitch = 2 * WIDTH
    for c in range(2):
        at = slice(c * N_DEV, (c + 1) * N_DEV)
        value = dot3((t_high[at, :], t_low[at, :]), source, NT)
        store_plane(out, WIDTH + c * LB, pitch, value)
    at = slice(2 * N_DEV, 3 * N_DEV)
    few = dot3((t_high[at, :], t_low[at, :]), source, NT)
    half = N_DEV // 2
    first = lax.broadcasted_iota(jnp.int32, (half, ROWS), 0) == 0
    dens_cos, dens_sin = z_density[:half, :], z_density[half:, :]
    phot_cos, phot_sin = few[:half], few[half:]
    store_plane(out, 0, pitch, jnp.where(first, phot_cos, dens_cos))
    store_plane(out, LB, pitch, jnp.where(first, dens_cos, dens_sin))
    store_plane(out, half * pitch, pitch, jnp.where(first, phot_sin, phot_cos))
    store_plane(out, half * pitch + LB, pitch, jnp.where(first, dens_sin, phot_sin))


def three(re, im, sign):
    t_re, t_im = re[1] + re[2], im[1] + im[2]
    d_re = (re[1] - re[2]) * (sign * HALF_ROOT3)
    d_im = (im[1] - im[2]) * (sign * HALF_ROOT3)
    m_re, m_im = re[0] - 0.5 * t_re, im[0] - 0.5 * t_im
    return (re[0] + t_re, m_re - d_im, m_re + d_im), (im[0] + t_im, m_im + d_re, m_im - d_re)


def nine(re, im, sign):
    for group in [(0, 1, 2), (3, 4, 5), (6, 7, 8), (0, 3, 6), (1, 4, 7), (2, 5, 8)]:
        new_re, new_im = three([re[g] for g in group], [im[g] for g in group], sign)
        for k, g in enumerate(group):
            re[g], im[g] = new_re[k], new_im[k]


def middle_kernel(planes, first_plane, got, *rest):
    if first_plane:
        rest = rest[1:]
    count = len(TABLE_SHAPES) + 1
    sources, out, rest = rest[:count], rest[count], rest[count + 1 :]
    tables, (tw1, work, r_high, r_low, l_high, l_low, back, sems) = rest[:count], rest[count:]
    dev_high, dev_low, lane_high, lane_low, tw_x, tw_y, tw2, win = tables
    copies = [
        pltpu.make_async_copy(source, table, sems.at[k])
        for k, (source, table) in enumerate(zip(sources, tables))
    ]
    for copy in copies:
        copy.start()
    pitch = planes * WIDTH
    for p in range(planes):
        for c in range(2):
            for j in range(LB):
                high, low = split(got[pl.ds((p * 2 + c) * LB + j, N_DEV, stride=pitch), :])
                at, to = slice(c * N_DEV, (c + 1) * N_DEV), slice(j * 128, (j + 1) * 128)
                r_high[p, at, to] = high
                r_low[p, at, to] = low
    for copy in copies:
        copy.wait()
    for k in range(N_PX):
        cos_x, sin_x = tw_x[0, k : k + 1, :], tw_x[1, k : k + 1, :]
        cos_y, sin_y = tw_y[0], tw_y[1]
        at = slice(k * N_PY, (k + 1) * N_PY)
        tw1[0, at, :] = cos_x * cos_y - sin_x * sin_y
        tw1[1, at, :] = sin_x * cos_y + cos_x * sin_y

    def plane(p, carry):
        dev = (dev_high[...], dev_low[...])
        for a in range(3):
            at = slice(a * NG, (a + 1) * NG)
            work[:, at] = dot3(dev, (r_high[p, :, at], r_low[p, :, at]))

        def forward(block, inner):
            rows = pl.ds(pl.multiple_of(block * 16, 16), 16)
            rows_im = pl.ds(pl.multiple_of(block * 16 + N_DEV, 16), 16)
            re, im = [], []
            for j in range(LB):
                at = slice(j * 128, (j + 1) * 128)
                cos, sin = tw1[0, rows, at], tw1[1, rows, at]
                x, y = work[rows, at], work[rows_im, at]
                re.append(x * cos + y * sin)
                im.append(y * cos - x * sin)
            nine(re, im, -1.0)
            for j in range(LB):
                at = slice(j * 128, (j + 1) * 128)
                cos, sin = tw2[0:1, at], tw2[1:2, at]
                to = pl.ds(pl.multiple_of(block * 16 + j * N_DEV, 16), 16)
                l_high[to, :128], l_low[to, :128] = split(re[j] * cos + im[j] * sin)
                l_high[to, 128:], l_low[to, 128:] = split(im[j] * cos - re[j] * sin)
            return inner

        lax.fori_loop(0, N_DEV // 16, forward, 0)
        mat = (lane_high[...], lane_low[...])
        for k in range(3):
            at = slice(k * NG, (k + 1) * NG)
            value = dot3((l_high[at, :], l_low[at, :]), mat)
            w = win[p, at, :]
            l_high[at, :128], l_low[at, :128] = split(value[:, :128] * w)
            l_high[at, 128:], l_low[at, 128:] = split(value[:, 128:] * w)
            back[at, :] = dot3((l_high[at, :], l_low[at, :]), mat, NT)

        def backward(block, inner):
            rows = pl.ds(pl.multiple_of(block * 16, 16), 16)
            rows_im = pl.ds(pl.multiple_of(block * 16 + N_DEV, 16), 16)
            re, im = [], []
            for j in range(LB):
                at = slice(j * 128, (j + 1) * 128)
                cos, sin = tw2[0:1, at], tw2[1:2, at]
                of = pl.ds(pl.multiple_of(block * 16 + j * N_DEV, 16), 16)
                x, y = back[of, :128], back[of, 128:]
                re.append(x * cos - y * sin)
                im.append(y * cos + x * sin)
            nine(re, im, 1.0)
            for j in range(LB):
                at = slice(j * 128, (j + 1) * 128)
                cos, sin = tw1[0, rows, at], tw1[1, rows, at]
                r_high[p, rows, at], r_low[p, rows, at] = split(re[j] * cos - im[j] * sin)
                r_high[p, rows_im, at], r_low[p, rows_im, at] = split(im[j] * cos + re[j] * sin)
            return inner

        lax.fori_loop(0, N_DEV // 16, backward, 0)
        for a in range(3):
            at = slice(a * NG, (a + 1) * NG)
            value = dot3(dev, (r_high[p, :, at], r_low[p, :, at]), TN)
            for c in range(2):
                for j in range(3):
                    start = (first_plane + p) * WIDTH + c * LB + a * 3 + j
                    out[pl.ds(start, N_DEV, stride=PITCH), :] = value[
                        c * N_DEV : (c + 1) * N_DEV, j * 128 : (j + 1) * 128
                    ]
        return carry

    lax.fori_loop(0, planes, plane, 0)


def z_last_kernel(got, t_high, t_low, out):
    a = pl.program_id(0)
    half = N_DEV // 2
    first = lax.broadcasted_iota(jnp.int32, (half, 128), 0) == 0
    dens, phot = [], []
    for a2 in range(3):

        def load(plane, c, begin=0, count=N_DEV):
            start = begin * PITCH + (plane * 2 + c) * LB + a * 3 + a2
            return got[pl.ds(start, count, stride=PITCH), :]

        re_low, im_low = load(1, 0, 0, half), load(1, 1, 0, half)
        re_top, im_top = load(1, 0, half, half), load(1, 1, half, half)
        dens.append(
            jnp.concatenate(
                [
                    load(0, 0),
                    load(0, 1),
                    jnp.where(first, im_low, re_low),
                    jnp.where(first, im_top, im_low),
                ],
                axis=0,
            )
        )
        phot.append(
            jnp.concatenate(
                [
                    load(2, 0),
                    load(2, 1),
                    jnp.where(first, re_low, re_top),
                    jnp.where(first, re_top, im_top),
                ],
                axis=0,
            )
        )
    table = (t_high[...], t_low[...])
    smooth_d = dot3(split(jnp.concatenate(dens, axis=1)), table, TN)
    smooth_p = dot3(split(jnp.concatenate(phot, axis=1)), table, TN)
    value = jnp.clip(smooth_p / jnp.maximum(smooth_d, 0.5), 0.0, 1.0)
    for a2 in range(3):
        out[:, a2 * 8 : (a2 + 1) * 8, :] = value[a2 * 128 : (a2 + 1) * 128].reshape(16, 8, NG)


TABLE_SHAPES = [((256, 256), BF)] * 4 + [
    ((2, N_PX, ROWS), F32),
    ((2, N_PY, ROWS), F32),
    ((8, ROWS), F32),
]


def placed_in(space, *arrays):
    return [pltpu.with_memory_space_constraint(jnp.asarray(a), space) for a in arrays]


def limit(mib):
    return pltpu.CompilerParams(vmem_limit_bytes=mib * 2**20)


def exchange(rows):
    send = rows.reshape(N_DEV, 1, rows.size // N_DEV)
    return lax.all_to_all(send, AXES, 0, 0, tiled=True).reshape(rows.shape)


def middle(got, planes, first_plane, tables, win, begun=None):
    anywhere = pl.BlockSpec(memory_space=pl.ANY)
    vmem = pl.BlockSpec(memory_space=pltpu.VMEM)
    begun = [] if begun is None else [begun]
    shapes = TABLE_SHAPES + [(win.shape, F32)]
    return pl.pallas_call(
        functools.partial(middle_kernel, planes, first_plane),
        out_shape=pltpu.VMEM((N_DEV * PITCH, 128), F32),
        in_specs=[vmem] * (1 + len(begun)) + [anywhere] * len(shapes),
        input_output_aliases={1: 0} if begun else {},
        scratch_shapes=[pltpu.VMEM(*shape) for shape in shapes]
        + [
            pltpu.VMEM((2, N_DEV, ROWS), F32),
            pltpu.VMEM((2 * N_DEV, ROWS), F32),
            pltpu.VMEM((planes, 2 * N_DEV, ROWS), BF),
            pltpu.VMEM((planes, 2 * N_DEV, ROWS), BF),
            pltpu.VMEM((ROWS, 256), BF),
            pltpu.VMEM((ROWS, 256), BF),
            pltpu.VMEM((ROWS, 256), F32),
            pltpu.SemaphoreType.DMA((len(shapes),)),
        ],
        compiler_params=limit(20),
        name=f"middle{planes}",
    )(*placed_in(pltpu.VMEM, got, *begun), *placed_in(pltpu.HBM, *tables, win))


def on_device(photons, halo_cells, halo_counts, owners, density):
    table = z_table()
    tables = (*device_table(), *lane_table(), *twiddles())

    send = pl.pallas_call(
        sort_kernel,
        out_shape=jax.ShapeDtypeStruct((N_PY * CAP * 2, SLOTS), F32),
        name="sort",
    )(photons, halo_cells, halo_counts.reshape(1, -1), owners.reshape(1, -1))
    halos = lax.all_to_all(send.reshape(N_PY, 2 * CAP, SLOTS), "py", 0, 0, tiled=True)

    send_a, few = pl.pallas_call(
        z_density_kernel,
        out_shape=(
            jax.ShapeDtypeStruct((N_DEV * WIDTH, 128), F32),
            jax.ShapeDtypeStruct((N_DEV, ROWS), F32),
        ),
        scratch_shapes=[pltpu.VMEM((ROWS, NG), BF), pltpu.VMEM((ROWS, NG), BF)],
        name="zdensity",
    )(density, *table)
    send_a, halos = lax.optimization_barrier((send_a, halos))
    got_a = exchange(send_a)

    halos = halos.reshape(N_PY * CAP, 2, SLOTS)
    weights, cells = halos[:, 0], halos[:, 1].astype(jnp.int32)
    slot = jnp.arange(1, SLOTS + 1, dtype=jnp.int32)[None, :]
    counts = jnp.max(jnp.where(weights != 0, slot, 0), axis=1)
    smem = pl.BlockSpec(memory_space=pltpu.SMEM)
    vmem = pl.BlockSpec(memory_space=pltpu.VMEM)
    send_bc = pl.pallas_call(
        paint_kernel,
        out_shape=jax.ShapeDtypeStruct((N_DEV * 2 * WIDTH, 128), F32),
        in_specs=[smem, smem, smem, vmem, vmem, vmem],
        scratch_shapes=[pltpu.VMEM((ROWS * 3, 128), F32)] * FIELDS
        + [pltpu.VMEM((ROWS, NG), BF), pltpu.VMEM((ROWS, NG), BF)],
        name="paint",
    )(weights, cells, counts, few, *table)
    got_a, send_bc = lax.optimization_barrier((got_a, send_bc))
    got_bc = exchange(send_bc)

    me = lax.axis_index(AXES)
    half = N_DEV // 2
    low = jnp.where(me % half == 0, (me // half) * (NG // 2), me % half)
    win_a = window(me + 64)
    win_bc = jnp.stack([window(low), win_a])
    back = middle(got_a, 1, 0, tables, win_a[None])
    back = middle(got_bc, 2, 1, tables, win_bc, back)
    got = exchange(back)
    whole = pl.BlockSpec((N_DEV * PITCH, 128), lambda i: (0, 0))
    whole_t = pl.BlockSpec((3 * N_DEV, NG), lambda i: (0, 0))
    return pl.pallas_call(
        z_last_kernel,
        grid=(3,),
        in_specs=[whole, whole_t, whole_t],
        out_specs=pl.BlockSpec((16, CY, NG), lambda i: (i, 0, 0)),
        out_shape=jax.ShapeDtypeStruct((CX, CY, NG), F32),
        compiler_params=limit(16),
        name="zlast",
    )(*placed_in(pltpu.VMEM, got, *table))


def solution(mesh):
    placed = (
        P(("px", "py"), None),
        P(("px", "py"), None),
        P(("px", "py")),
        P(("px", "py"), None),
        P("px", "py", None),
    )
    return jax.shard_map(
        on_device, mesh=mesh, in_specs=placed, out_specs=P("px", "py", None), check_vma=False
    )
```

time: 472 us -> 158 us (0.33); the launches traced: 464 us -> 157 us
  matrix products: 172 us -> 0 us
  local copies, waits for them, and re-layouts: 78.9 us -> 1.13 us
  waiting for transfers between devices: 72.5 us -> 21.1 us
  Pallas kernels: 0 us -> 46 us
  other arithmetic: 52 us -> 9.07 us
  blocking collectives: 70.1 us -> 52.7 us
  starting transfers between devices: 17.9 us -> 26.5 us
    dot_general x18 -> x0, matrix products: 172 us -> none  [product(): return jnp.einsum(form, left, right, precision=lax.Precision.HIGHEST)]
    all_to_all x3, waiting for transfers between devices: 72.5 us -> 21.1 us  [the longest x2 18.8 us: exchange(): return lax.all_to_all(send, AXES, 0, 0, tiled=True).reshape(rows.shape)]
    pallas_call x0 -> x6, Pallas kernels: none -> 46 us  [the longest x2 18.8 us: middle(): pl.pallas_call(functools.partial(middle_kernel, planes, first_plane), out...]
    reshape x7 -> x0, local copies, waits for them, and re-layouts: 44.8 us -> none  [the longest x1 12.4 us: on_device(): got_real = got_real.reshape(slab_planes, count_x, count_y, rows_x, rows_y)]
    scatter-add x1 -> x0, other arithmetic: 43.6 us -> none  [paint(): return empty.at[cell_rows.reshape(-1)].add(weights.reshape(-1))]
    all_to_all x1, blocking collectives: 70.1 us -> 52.7 us  [exchange(): return lax.all_to_all(send, AXES, 0, 0, tiled=True).reshape(rows.shape)]
    all_to_all x3, starting transfers between devices: 17.9 us -> 26.5 us  [the longest x2 17.9 us: exchange(): return lax.all_to_all(send, AXES, 0, 0, tiled=True).reshape(rows.shape)]
    add x1 -> x0, local copies, waits for them, and re-layouts: 8.17 us -> none  [rotate(): return (first - third, first + second)]
  transfers between devices with their start and end apart: 3 -> 3, of which waited for: 3 -> 3; matrix products, arithmetic and copies ran while one was open for 0% -> 6% of each run, Pallas kernels for 0% -> 17%
where the time goes in v2:
time: 158 us; the launch traced here: 157 us
  blocking collectives  52.7 us (33%)
  Pallas kernels  46 us (29%)
  starting transfers between devices  26.5 us (17%)
  waiting for transfers between devices  21.1 us (13%)
  other arithmetic  9.07 us (6%)
    all_to_all x1, blocking collectives, exchange(): return lax.all_to_all(send, AXES, 0, 0, tiled=True).reshape(rows.shape)  52.7 us
    all_to_all x2, waiting for transfers between devices, exchange(): return lax.all_to_all(send, AXES, 0, 0, tiled=True).reshape(rows.shape)  18.8 us
    pallas_call x2, Pallas kernels, middle(): pl.pallas_call(functools.partial(middle_kernel, planes, first_plane), out...  18.8 us
    all_to_all x2, starting transfers between devices, exchange(): return lax.all_to_all(send, AXES, 0, 0, tiled=True).reshape(rows.shape)  17.9 us
    pallas_call x1, Pallas kernels, on_device(): pl.pallas_call(paint_kernel, out_shape=jax.ShapeDtypeStruct((N_DEV * 2 *...  15.7 us
    all_to_all x1, starting transfers between devices, on_device(): lax.all_to_all(send.reshape(N_PY, 2 * CAP, SLOTS), 'py', 0, 0, tiled=True)  8.63 us
    mul x1, other arithmetic, window(): return value * (jnp.where(both, 2.0, 1.0) / float(NG) ** 3)  6.58 us
    pallas_call x1, Pallas kernels, on_device(): pl.pallas_call(z_density_kernel, out_shape=(jax.ShapeDtypeStruct((N_DEV *...  5.07 us
  transfers between devices with their start and end apart: 3, of which 3 were waited for; matrix products, arithmetic and copies ran while one was open for 6% of the time, Pallas kernels for 17%

profile of v2, /device:TPU:7, one launch (start us, length us, event | category | flops | bytes accessed | tf_op | source)
XLA Modules:
  0.0 156.8 jit_solution(6704733494762817832)
XLA Ops:
  0.0 1.7 %sort.1 = f32[128,128]{1,0:T(8,128)} custom-call(f32[32,128]{1,0:T(8,128)} %photons.1, s32[32,128]{1,0:T(8,128)} %cells.1, s32[1,32]{1,0:T(1,128)} %bitcast.26, s32[1,32]{1,0:T(1,128)} %bitcast.27), custom_call_target="tpu_custom_call" | custom-call | tf_op jit(solution)/shard_map/sort/pallas_call | solution.py:436
  1.7 8.6 %all-to-all-start = ((f32[16,8,128]{2,1,0:T(8,128)}), f32[16,8,128]{2,1,0:T(8,128)S(1)}, u32[]{:S(2)}, u32[]{:S(2)}) async-start(f32[16,8,128]{2,1,0:T(8,128)} %bitcast.24), calls=%async_computation | async-start | bytes 131072 | tf_op jit(solution)/shard_map/all_to_all | solution.py:441
  10.3 5.1 %zdensity.1 = (f32[2304,128]{1,0:T(8,128)}, f32[128,1152]{1,0:T(8,128)}) custom-call(f32[48,24,384]{2,1,0:T(8,128)} %density.1, bf16[384,384]{1,0:T(8,128)(2,1)} %constant.187.clone.t_high, bf16[384,384]{1,0:T(8,128)(2,1)} %constant.188.clone.t_low), custom_call_target="tpu_custom_call" | custom-call | tf_op jit(solution)/shard_map/zdensity/pallas_call | solution.py:443
  15.4 2.3 %all-to-all-done = f32[16,8,128]{2,1,0:T(8,128)S(1)} async-done(((f32[16,8,128]{2,1,0:T(8,128)}), f32[16,8,128]{2,1,0:T(8,128)S(1)}, u32[]{:S(2)}, u32[]{:S(2)}) %all-to-all-start) | async-done | bytes 65568 | tf_op jit(solution)/shard_map/all_to_all | solution.py:441
  17.6 7.1 %all-to-all-start.1 = ((f32[128,1,2304]{2,1,0:T(1,128)}), f32[128,1,2304]{2,1,0:T(1,128)S(1)}, u32[]{:S(2)}, u32[]{:S(2)}) async-start(f32[128,1,2304]{2,1,0:T(1,128)} %bitcast.20), calls=%async_computation.1 | async-start | bytes 2359296 | tf_op jit(solution)/shard_map/all_to_all | solution.py:403
  24.7 0.1 fusion.36
  24.8 0.0 copy-start.5
  24.8 0.6 select_reduce_fusion.counts
  25.4 0.6 convert_bitcast_fusion.cells
  26.0 0.0 copy-done.5
  26.0 15.7 %paint.1 = f32[4608,128]{1,0:T(8,128)} custom-call(f32[64,128]{1,0:T(8,128)} %bitcast.22, s32[64,128]{1,0:T(8,128)} %convert_bitcast_fusion.cells, s32[64]{0:T(128)} %select_reduce_fusion.counts, f32[128,1152]{1,0:T(8,128)} %get-tuple-element.14.z_density, bf16[384,384]{1,0:T(8,128)(2,1)} %constant.187.clone.t_high, bf16[384,384]{1,0:T(8,128)(2,1)} %constant.188.clone.t_low), custom_call_target="tpu_custom_call" | custom-call | tf_op jit(solution)/shard_map/paint/pallas_call | solution.py:461
  41.7 1.4 all-to-all-done.1
  43.2 0.0 copy-start
  43.2 1.0 copy-done
  44.2 10.8 %all-to-all-start.2 = ((f32[128,1,4608]{2,1,0:T(1,128)}), f32[128,1,4608]{2,1,0:T(1,128)}, u32[]{:S(2)}, u32[]{:S(2)}) async-start(f32[128,1,4608]{2,1,0:T(1,128)} %bitcast.19), calls=%async_computation.2 | async-start | bytes 4718592 | tf_op jit(solution)/shard_map/all_to_all | solution.py:403
  55.1 0.0 copy-start.1
  55.1 6.6 %fusion.8 = (f32[1,1152,128]{2,1,0:T(8,128)S(1)}, f32[1,1152,128]{2,1,0:T(8,128)S(1)}) fusion(f32[]{:T(128)S(6)} %div.110, s32[]{:T(128)S(6)} %mul.256, s32[128]{0:T(128)S(1)} %get-tuple-element.30, s32[128]{0:T(128)S(1)} %get-tuple-element.31, pred[128]{0:T(512)(128)(4,1)S(1)} %get-tuple-element.27, s32[128]{0:T(128)S(1)} %get-tuple-element.29, ...), kind=kLoop, calls=%fused_computation.31 | loop fusion | flops 11501568 | bytes 1202704 | tf_op jit(solution)/shard_map/mul | solution.py:105
  61.7 0.0 copy-start.4
  61.7 1.2 pad_maximum_fusion.rest_8_
  62.9 0.0 copy-done.4
  63.0 0.0 copy-done.1
  63.0 6.1 %middle1.1.rest_0_ = f32[6912,128]{1,0:T(8,128)S(1)} custom-call(f32[2304,128]{1,0:T(8,128)S(1)} %bitcast.18, bf16[256,256]{1,0:T(8,128)(2,1)} %constant.189.clone.rest_0_.rest_1_, bf16[256,256]{1,0:T(8,128)(2,1)} %constant.190.clone.rest_1_.rest_2_, bf16[256,256]{1,0:T(8,128)(2,1)} %constant.191.clone.rest_2_.rest_3_, ...), custom_call_target="tpu_custom_call" | custom-call | tf_op jit(solution)/shard_map/middle1/pallas_call | solution.py:411
  69.0 17.4 %all-to-all-done.2 = f32[128,1,4608]{2,1,0:T(1,128)} async-done(((f32[128,1,4608]{2,1,0:T(1,128)}), f32[128,1,4608]{2,1,0:T(1,128)}, u32[]{:S(2)}, u32[]{:S(2)}) %all-to-all-start.2) | async-done | bytes 2359328 | tf_op jit(solution)/shard_map/all_to_all | solution.py:403
  86.5 12.8 %middle2.1 = f32[6912,128]{1,0:T(8,128)S(1)} custom-call(f32[4608,128]{1,0:T(8,128)} %bitcast.9.got, f32[6912,128]{1,0:T(8,128)S(1)} %middle1.1.rest_0_, bf16[256,256]{1,0:T(8,128)(2,1)} %constant.189.clone.rest_0_.rest_1_, bf16[256,256]{1,0:T(8,128)(2,1)} %constant.190.clone.rest_1_.rest_2_, ...), custom_call_target="tpu_custom_call", output_to_operand_aliasing={{}: (1, {})} | custom-call | tf_op jit(solution)/shard_map/middle2/pallas_call | solution.py:411
  99.2 0.0 copy-start.2
  99.3 0.0 copy-start.3
  99.3 52.7 %all_to_all.20 = f32[128,1,6912]{2,1,0:T(1,128)S(1)} all-to-all(f32[128,1,6912]{2,1,0:T(1,128)S(1)} %bitcast.16), channel_id=1, replica_groups=mesh['px'=8,'py'=16] {'px','py'}, dimensions={0} | all-to-all | bytes 7077888 | tf_op jit(solution)/shard_map/all_to_all | solution.py:403
  152.0 0.0 copy-done.2
  152.0 0.0 copy-done.3
  152.0 4.8 %zlast.1 = f32[48,24,384]{2,1,0:T(8,128)} custom-call(f32[6912,128]{1,0:T(8,128)S(1)} %bitcast.17, bf16[384,384]{1,0:T(8,128)(2,1)S(1)} %copy-done.3, bf16[384,384]{1,0:T(8,128)(2,1)S(1)} %copy-done.2), custom_call_target="tpu_custom_call" | custom-call | tf_op jit(solution)/shard_map/zlast/pallas_call | solution.py:482
  (7 shorter events, 0.0 us)
Async XLA Ops:
  1.7 16.0 %all-to-all-start = ((f32[16,8,128]{2,1,0:T(8,128)}), f32[16,8,128]{2,1,0:T(8,128)S(1)}, u32[]{:S(2)}, u32[]{:S(2)}) async-start(f32[16,8,128]{2,1,0:T(8,128)} %bitcast.24), calls=%async_computation | async-start | bytes 131072 | tf_op jit(solution)/shard_map/all_to_all | solution.py:441
  17.6 25.5 %all-to-all-start.1 = ((f32[128,1,2304]{2,1,0:T(1,128)}), f32[128,1,2304]{2,1,0:T(1,128)S(1)}, u32[]{:S(2)}, u32[]{:S(2)}) async-start(f32[128,1,2304]{2,1,0:T(1,128)} %bitcast.20), calls=%async_computation.1 | async-start | bytes 2359296 | tf_op jit(solution)/shard_map/all_to_all | solution.py:403
  24.8 1.3 copy-start.5
  43.2 1.0 copy-start
  44.2 42.3 %all-to-all-start.2 = ((f32[128,1,4608]{2,1,0:T(1,128)}), f32[128,1,4608]{2,1,0:T(1,128)}, u32[]{:S(2)}, u32[]{:S(2)}) async-start(f32[128,1,4608]{2,1,0:T(1,128)} %bitcast.19), calls=%async_computation.2 | async-start | bytes 4718592 | tf_op jit(solution)/shard_map/all_to_all | solution.py:403
  55.1 7.9 %copy-start.1 = (f32[128,1,2304]{2,1,0:T(1,128)S(1)}, f32[128,1,2304]{2,1,0:T(1,128)}, u32[]{:S(2)}) copy-start(f32[128,1,2304]{2,1,0:T(1,128)} %copy-done) | copy-start | bytes 3538948
  61.7 1.3 copy-start.4
  99.2 52.7 %copy-start.2 = (bf16[384,384]{1,0:T(8,128)(2,1)S(1)}, bf16[384,384]{1,0:T(8,128)(2,1)}, u32[]{:S(2)}) copy-start(bf16[384,384]{1,0:T(8,128)(2,1)} %constant.188.clone.t_low) | copy-start | bytes 884740
  99.3 52.7 %copy-start.3 = (bf16[384,384]{1,0:T(8,128)(2,1)S(1)}, bf16[384,384]{1,0:T(8,128)(2,1)}, u32[]{:S(2)}) copy-start(bf16[384,384]{1,0:T(8,128)(2,1)} %constant.187.clone.t_high) | copy-start | bytes 884740

commit v3 on v2

--- a/solution.py
+++ b/solution.py
@@ -115,8 +115,11 @@
 
 
 def dot3(left, right, dims=NN):
-    return (
-        dot(left[0], right[0], dims) + dot(left[1], right[0], dims) + dot(left[0], right[1], dims)
+    (left_dim,), (right_dim,) = dims
+    return dot(
+        jnp.concatenate([left[0], left[1], left[0]], axis=left_dim),
+        jnp.concatenate([right[0], right[0], right[1]], axis=right_dim),
+        dims,
     )
 
 
@@ -157,41 +160,47 @@
             block = density[a * 16 : (a + 1) * 16, a2 * 8 : (a2 + 1) * 8, :].reshape(128, NG)
             at = slice((a * 3 + a2) * 128, (a * 3 + a2 + 1) * 128)
             high[at, :], low[at, :] = split(block)
-    for part in range(3):
-        at = slice(part * N_DEV, (part + 1) * N_DEV)
-        value = dot3((t_high[at, :], t_low[at, :]), (high[...], low[...]), NT)
-        if part < 2:
-            store_plane(out, part * LB, WIDTH, value)
-        else:
-            few[...] = value
+    for a in range(3):
+        at = slice(a * NG, (a + 1) * NG)
+        value = dot3((t_high[...], t_low[...]), (high[at, :], low[at, :]), NT)
+        for c in range(2):
+            store_plane(out, c * LB + 3 * a, WIDTH, value[c * N_DEV : (c + 1) * N_DEV])
+        few[:, at] = value[2 * N_DEV :]
 
 
 def store_plane(out, start, pitch, value):
-    for j in range(LB):
+    for j in range(value.shape[1] // 128):
         rows = pl.ds(start + j, value.shape[0], stride=pitch)
         out[rows, :] = value[:, j * 128 : (j + 1) * 128]
 
 
 def paint_kernel(weights, cells, counts, z_density, t_high, t_low, out, *scratch):
     fields, high, low = scratch[:FIELDS], scratch[FIELDS], scratch[FIELDS + 1]
-    step = 8
     for field in fields:
         field[...] = jnp.zeros(field.shape, F32)
     lane = lax.broadcasted_iota(jnp.int32, (1, 128), 1)
 
     def block(index, carry):
         count = counts[index]
-        for begin in range(0, SLOTS, step):
-
+
+        def some(begin, step):
+            for k in range(begin, begin + step):
+                cell = cells[index, k]
+                value = weights[index, k]
+                row = lax.shift_right_logical(cell, 7)
+                here = lane == (jnp.full((1, 128), cell, jnp.int32) & 127)
+                fields[k % FIELDS][pl.ds(row, 1), :] += jnp.where(here, value, 0.0)
+
+        def halves(begin, size):
             @pl.when(count > begin)
             def _():
-                for k in range(step):
-                    cell = cells[index, begin + k]
-                    value = weights[index, begin + k]
-                    row = lax.shift_right_logical(cell, 7)
-                    here = lane == (jnp.full((1, 128), cell, jnp.int32) & 127)
-                    fields[k % FIELDS][pl.ds(row, 1), :] += jnp.where(here, value, 0.0)
-
+                if size == 16:
+                    some(begin, size)
+                else:
+                    halves(begin, size // 2)
+                    halves(begin + size // 2, size // 2)
+
+        halves(0, SLOTS)
         return carry
 
     lax.fori_loop(0, counts.shape[0], block, 0)
@@ -208,22 +217,22 @@
                 at = slice((a * 3 + a2) * 128, (a * 3 + a2 + 1) * 128)
                 to = slice(part * 128, (part + 1) * 128)
                 high[at, to], low[at, to] = split(jnp.concatenate(tiles, axis=0))
-    source = (high[...], low[...])
     pitch = 2 * WIDTH
-    for c in range(2):
-        at = slice(c * N_DEV, (c + 1) * N_DEV)
-        value = dot3((t_high[at, :], t_low[at, :]), source, NT)
-        store_plane(out, WIDTH + c * LB, pitch, value)
-    at = slice(2 * N_DEV, 3 * N_DEV)
-    few = dot3((t_high[at, :], t_low[at, :]), source, NT)
     half = N_DEV // 2
-    first = lax.broadcasted_iota(jnp.int32, (half, ROWS), 0) == 0
-    dens_cos, dens_sin = z_density[:half, :], z_density[half:, :]
-    phot_cos, phot_sin = few[:half], few[half:]
-    store_plane(out, 0, pitch, jnp.where(first, phot_cos, dens_cos))
-    store_plane(out, LB, pitch, jnp.where(first, dens_cos, dens_sin))
-    store_plane(out, half * pitch, pitch, jnp.where(first, phot_sin, phot_cos))
-    store_plane(out, half * pitch + LB, pitch, jnp.where(first, dens_sin, phot_sin))
+    first = lax.broadcasted_iota(jnp.int32, (half, NG), 0) == 0
+    for a in range(3):
+        at = slice(a * NG, (a + 1) * NG)
+        value = dot3((t_high[...], t_low[...]), (high[at, :], low[at, :]), NT)
+        for c in range(2):
+            plane = value[c * N_DEV : (c + 1) * N_DEV]
+            store_plane(out, WIDTH + c * LB + 3 * a, pitch, plane)
+        dens_cos, dens_sin = z_density[:half, at], z_density[half:, at]
+        phot_cos, phot_sin = value[2 * N_DEV : 2 * N_DEV + half], value[2 * N_DEV + half :]
+        low_rows, top_rows = 3 * a, half * pitch + 3 * a
+        store_plane(out, low_rows, pitch, jnp.where(first, phot_cos, dens_cos))
+        store_plane(out, low_rows + LB, pitch, jnp.where(first, dens_cos, dens_sin))
+        store_plane(out, top_rows, pitch, jnp.where(first, phot_sin, phot_cos))
+        store_plane(out, top_rows + LB, pitch, jnp.where(first, dens_sin, phot_sin))
 
 
 def three(re, im, sign):
@@ -241,19 +250,18 @@
             re[g], im[g] = new_re[k], new_im[k]
 
 
-def middle_kernel(planes, first_plane, got, *rest):
-    if first_plane:
-        rest = rest[1:]
-    count = len(TABLE_SHAPES) + 1
+def middle_kernel(planes, got, *rest):
+    count = len(TABLE_SHAPES) + (2 if planes == 2 else 1)
     sources, out, rest = rest[:count], rest[count], rest[count + 1 :]
     tables, (tw1, work, r_high, r_low, l_high, l_low, back, sems) = rest[:count], rest[count:]
-    dev_high, dev_low, lane_high, lane_low, tw_x, tw_y, tw2, win = tables
+    dev_high, dev_low, lane_high, lane_low, tw_x, tw_y, tw2, win = tables[:8]
     copies = [
         pltpu.make_async_copy(source, table, sems.at[k])
         for k, (source, table) in enumerate(zip(sources, tables))
     ]
     for copy in copies:
         copy.start()
+    first_plane, out_pitch = (1, PITCH) if planes == 2 else (0, WIDTH)
     pitch = planes * WIDTH
     for p in range(planes):
         for c in range(2):
@@ -262,7 +270,7 @@
                 at, to = slice(c * N_DEV, (c + 1) * N_DEV), slice(j * 128, (j + 1) * 128)
                 r_high[p, at, to] = high
                 r_low[p, at, to] = low
-    for copy in copies:
+    for copy in copies[:7]:
         copy.wait()
     for k in range(N_PX):
         cos_x, sin_x = tw_x[0, k : k + 1, :], tw_x[1, k : k + 1, :]
@@ -297,6 +305,12 @@
             return inner
 
         lax.fori_loop(0, N_DEV // 16, forward, 0)
+
+        @pl.when(p == 0)
+        def _():
+            for copy in copies[7:]:
+                copy.wait()
+
         mat = (lane_high[...], lane_low[...])
         for k in range(3):
             at = slice(k * NG, (k + 1) * NG)
@@ -332,12 +346,15 @@
             for c in range(2):
                 for j in range(3):
                     start = (first_plane + p) * WIDTH + c * LB + a * 3 + j
-                    out[pl.ds(start, N_DEV, stride=PITCH), :] = value[
+                    out[pl.ds(start, N_DEV, stride=out_pitch), :] = value[
                         c * N_DEV : (c + 1) * N_DEV, j * 128 : (j + 1) * 128
                     ]
         return carry
 
     lax.fori_loop(0, planes, plane, 0)
+    if planes == 2:
+        for j in range(WIDTH):
+            out[pl.ds(j, N_DEV, stride=PITCH), :] = tables[8][pl.ds(j, N_DEV, stride=WIDTH), :]
 
 
 def z_last_kernel(got, t_high, t_low, out):
@@ -403,16 +420,17 @@
     return lax.all_to_all(send, AXES, 0, 0, tiled=True).reshape(rows.shape)
 
 
-def middle(got, planes, first_plane, tables, win, begun=None):
-    anywhere = pl.BlockSpec(memory_space=pl.ANY)
-    vmem = pl.BlockSpec(memory_space=pltpu.VMEM)
-    begun = [] if begun is None else [begun]
-    shapes = TABLE_SHAPES + [(win.shape, F32)]
+def middle(got, planes, sources):
+    shapes = TABLE_SHAPES + [(source.shape, F32) for source in sources[len(TABLE_SHAPES) :]]
+    if planes == 2:
+        out_shape = pltpu.VMEM((N_DEV * PITCH, 128), F32)
+    else:
+        out_shape = jax.ShapeDtypeStruct((N_DEV * WIDTH, 128), F32)
     return pl.pallas_call(
-        functools.partial(middle_kernel, planes, first_plane),
-        out_shape=pltpu.VMEM((N_DEV * PITCH, 128), F32),
-        in_specs=[vmem] * (1 + len(begun)) + [anywhere] * len(shapes),
-        input_output_aliases={1: 0} if begun else {},
+        functools.partial(middle_kernel, planes),
+        out_shape=out_shape,
+        in_specs=[pl.BlockSpec(memory_space=pltpu.VMEM)]
+        + [pl.BlockSpec(memory_space=pl.ANY)] * len(shapes),
         scratch_shapes=[pltpu.VMEM(*shape) for shape in shapes]
         + [
             pltpu.VMEM((2, N_DEV, ROWS), F32),
@@ -426,7 +444,7 @@
         ],
         compiler_params=limit(20),
         name=f"middle{planes}",
-    )(*placed_in(pltpu.VMEM, got, *begun), *placed_in(pltpu.HBM, *tables, win))
+    )(*placed_in(pltpu.VMEM, got), *placed_in(pltpu.HBM, *sources))
 
 
 def on_device(photons, halo_cells, halo_counts, owners, density):
@@ -466,7 +484,6 @@
         + [pltpu.VMEM((ROWS, NG), BF), pltpu.VMEM((ROWS, NG), BF)],
         name="paint",
     )(weights, cells, counts, few, *table)
-    got_a, send_bc = lax.optimization_barrier((got_a, send_bc))
     got_bc = exchange(send_bc)
 
     me = lax.axis_index(AXES)
@@ -474,8 +491,8 @@
     low = jnp.where(me % half == 0, (me // half) * (NG // 2), me % half)
     win_a = window(me + 64)
     win_bc = jnp.stack([window(low), win_a])
-    back = middle(got_a, 1, 0, tables, win_a[None])
-    back = middle(got_bc, 2, 1, tables, win_bc, back)
+    back_a = middle(got_a, 1, (*tables, win_a[None]))
+    back = middle(got_bc, 2, (*tables, win_bc, back_a))
     got = exchange(back)
     whole = pl.BlockSpec((N_DEV * PITCH, 128), lambda i: (0, 0))
     whole_t = pl.BlockSpec((3 * N_DEV, NG), lambda i: (0, 0))

time: 158 us -> 151 us (0.956)
  Pallas kernels: 46 us -> 37.3 us
  waiting for transfers between devices: 21.1 us -> 26.7 us
  starting transfers between devices: 26.5 us -> 21.8 us
    pallas_call x1, Pallas kernels: 15.7 us -> 10.2 us  [on_device(): pl.pallas_call(paint_kernel, out_shape=jax.ShapeDtypeStruct((N_DEV * 2 *...]
    all_to_all x2, waiting for transfers between devices: 18.8 us -> 23.8 us  [exchange(): return lax.all_to_all(send, AXES, 0, 0, tiled=True).reshape(rows.shape)]
    all_to_all x2, starting transfers between devices: 17.9 us -> 13.2 us  [exchange(): return lax.all_to_all(send, AXES, 0, 0, tiled=True).reshape(rows.shape)]
    pallas_call x2, Pallas kernels: 18.8 us -> 16.6 us  [middle(): pl.pallas_call(functools.partial(middle_kernel, planes), out_shape=out_sh...]
  transfers between devices with their start and end apart: 3 -> 3, of which waited for: 3 -> 3; matrix products, arithmetic and copies ran while one was open for 6% -> 6% of each run, Pallas kernels for 17% -> 14%
where the time goes in v3:
time: 151 us; the launch traced here: 149 us
  blocking collectives  52.7 us (35%)
  Pallas kernels  37.3 us (25%)
  waiting for transfers between devices  26.7 us (18%)
  starting transfers between devices  21.8 us (14%)
  other arithmetic  9.07 us (6%)
    all_to_all x1, blocking collectives, exchange(): return lax.all_to_all(send, AXES, 0, 0, tiled=True).reshape(rows.shape)  52.7 us
    all_to_all x2, waiting for transfers between devices, exchange(): return lax.all_to_all(send, AXES, 0, 0, tiled=True).reshape(rows.shape)  23.8 us
    pallas_call x2, Pallas kernels, middle(): pl.pallas_call(functools.partial(middle_kernel, planes), out_shape=out_sh...  16.6 us
    all_to_all x2, starting transfers between devices, exchange(): return lax.all_to_all(send, AXES, 0, 0, tiled=True).reshape(rows.shape)  13.2 us
    pallas_call x1, Pallas kernels, on_device(): pl.pallas_call(paint_kernel, out_shape=jax.ShapeDtypeStruct((N_DEV * 2 *...  10.2 us
    all_to_all x1, starting transfers between devices, on_device(): lax.all_to_all(send.reshape(N_PY, 2 * CAP, SLOTS), 'py', 0, 0, tiled=True)  8.63 us
    mul x1, other arithmetic, window(): return value * (jnp.where(both, 2.0, 1.0) / float(NG) ** 3)  6.58 us
    pallas_call x1, Pallas kernels, on_device(): pl.pallas_call(z_density_kernel, out_shape=(jax.ShapeDtypeStruct((N_DEV *...  4.47 us
  transfers between devices with their start and end apart: 3, of which 3 were waited for; matrix products, arithmetic and copies ran while one was open for 6% of the time, Pallas kernels for 14%

profile of v3, /device:TPU:7, one launch (start us, length us, event | category | flops | bytes accessed | tf_op | source)
XLA Modules:
  0.0 148.9 jit_solution(12337018880746526309)
XLA Ops:
  0.0 1.7 %sort.1 = f32[128,128]{1,0:T(8,128)} custom-call(f32[32,128]{1,0:T(8,128)} %photons.1, s32[32,128]{1,0:T(8,128)} %cells.1, s32[1,32]{1,0:T(1,128)} %bitcast.27, s32[1,32]{1,0:T(1,128)} %bitcast.28), custom_call_target="tpu_custom_call" | custom-call | tf_op jit(solution)/shard_map/sort/pallas_call | solution.py:454
  1.7 8.6 %all-to-all-start = ((f32[16,8,128]{2,1,0:T(8,128)}), f32[16,8,128]{2,1,0:T(8,128)S(1)}, u32[]{:S(2)}, u32[]{:S(2)}) async-start(f32[16,8,128]{2,1,0:T(8,128)} %bitcast.25), calls=%async_computation | async-start | bytes 131072 | tf_op jit(solution)/shard_map/all_to_all | solution.py:459
  10.3 4.5 %zdensity.1 = (f32[2304,128]{1,0:T(8,128)}, f32[128,1152]{1,0:T(8,128)}) custom-call(f32[48,24,384]{2,1,0:T(8,128)} %density.1, bf16[384,384]{1,0:T(8,128)(2,1)} %constant.187.clone.t_high, bf16[384,384]{1,0:T(8,128)(2,1)} %constant.188.clone.t_low), custom_call_target="tpu_custom_call" | custom-call | tf_op jit(solution)/shard_map/zdensity/pallas_call | solution.py:461
  14.8 2.9 %all-to-all-done = f32[16,8,128]{2,1,0:T(8,128)S(1)} async-done(((f32[16,8,128]{2,1,0:T(8,128)}), f32[16,8,128]{2,1,0:T(8,128)S(1)}, u32[]{:S(2)}, u32[]{:S(2)}) %all-to-all-start) | async-done | bytes 65568 | tf_op jit(solution)/shard_map/all_to_all | solution.py:459
  17.6 6.5 %all-to-all-start.2 = ((f32[128,1,2304]{2,1,0:T(1,128)}), f32[128,1,2304]{2,1,0:T(1,128)S(1)}, u32[]{:S(2)}, u32[]{:S(2)}) async-start(f32[128,1,2304]{2,1,0:T(1,128)} %bitcast.21), calls=%async_computation.2 | async-start | bytes 2359296 | tf_op jit(solution)/shard_map/all_to_all | solution.py:420
  24.1 0.1 fusion.36
  24.2 0.0 copy-start.4
  24.2 0.7 select_reduce_fusion.counts
  24.9 0.6 convert_bitcast_fusion.cells
  25.5 0.0 copy-done.4
  25.5 10.2 %paint.1 = f32[4608,128]{1,0:T(8,128)} custom-call(f32[64,128]{1,0:T(8,128)} %bitcast.23, s32[64,128]{1,0:T(8,128)} %convert_bitcast_fusion.cells, s32[64]{0:T(128)} %select_reduce_fusion.counts, f32[128,1152]{1,0:T(8,128)} %get-tuple-element.11.z_density, bf16[384,384]{1,0:T(8,128)(2,1)} %constant.187.clone.t_high, bf16[384,384]{1,0:T(8,128)(2,1)} %constant.188.clone.t_low), custom_call_target="tpu_custom_call" | custom-call | tf_op jit(solution)/shard_map/paint/pallas_call | solution.py:479
  35.7 6.9 %all-to-all-done.2 = f32[128,1,2304]{2,1,0:T(1,128)S(1)} async-done(((f32[128,1,2304]{2,1,0:T(1,128)}), f32[128,1,2304]{2,1,0:T(1,128)S(1)}, u32[]{:S(2)}, u32[]{:S(2)}) %all-to-all-start.2) | async-done | bytes 1179680 | tf_op jit(solution)/shard_map/all_to_all | solution.py:420
  42.6 6.7 %all-to-all-start.1 = ((f32[128,1,4608]{2,1,0:T(1,128)}), f32[128,1,4608]{2,1,0:T(1,128)S(1)}, u32[]{:S(2)}, u32[]{:S(2)}) async-start(f32[128,1,4608]{2,1,0:T(1,128)} %bitcast.20), calls=%async_computation.1 | async-start | bytes 4718592 | tf_op jit(solution)/shard_map/all_to_all | solution.py:420
  49.4 6.6 %fusion.7 = (f32[1,1152,128]{2,1,0:T(8,128)S(1)}, f32[1,1152,128]{2,1,0:T(8,128)S(1)}) fusion(f32[]{:T(128)S(6)} %div.108, s32[]{:T(128)S(6)} %mul.248, s32[128]{0:T(128)S(1)} %get-tuple-element.26, s32[128]{0:T(128)S(1)} %get-tuple-element.27, pred[128]{0:T(512)(128)(4,1)S(1)} %get-tuple-element.23, s32[128]{0:T(128)S(1)} %get-tuple-element.25, ...), kind=kLoop, calls=%fused_computation.30 | loop fusion | flops 11501568 | bytes 1202704 | tf_op jit(solution)/shard_map/mul | solution.py:105
  55.9 0.0 copy-start.3
  55.9 1.2 pad_maximum_fusion.rest_7_
  57.1 0.0 copy-done.3
  57.2 5.8 %middle1.1.rest_8_ = f32[2304,128]{1,0:T(8,128)S(1)} custom-call(f32[2304,128]{1,0:T(8,128)S(1)} %bitcast.19, bf16[256,256]{1,0:T(8,128)(2,1)} %constant.189.clone.rest_0_, bf16[256,256]{1,0:T(8,128)(2,1)} %constant.190.clone.rest_1_, bf16[256,256]{1,0:T(8,128)(2,1)} %constant.191.clone.rest_2_, bf16[256,256]{1,0:T(8,128)(2,1)} %constant.192.clone.rest_3_, ...), custom_call_target="tpu_custom_call" | custom-call | tf_op jit(solution)/shard_map/middle1/pallas_call | solution.py:429
  63.0 0.0 copy-start
  63.0 1.0 copy-done
  64.1 16.9 %all-to-all-done.1 = f32[128,1,4608]{2,1,0:T(1,128)S(1)} async-done(((f32[128,1,4608]{2,1,0:T(1,128)}), f32[128,1,4608]{2,1,0:T(1,128)S(1)}, u32[]{:S(2)}, u32[]{:S(2)}) %all-to-all-start.1) | async-done | bytes 2359328 | tf_op jit(solution)/shard_map/all_to_all | solution.py:420
  81.0 10.8 %middle2.1 = f32[6912,128]{1,0:T(8,128)S(1)} custom-call(f32[4608,128]{1,0:T(8,128)S(1)} %bitcast.18, bf16[256,256]{1,0:T(8,128)(2,1)} %constant.189.clone.rest_0_, bf16[256,256]{1,0:T(8,128)(2,1)} %constant.190.clone.rest_1_, bf16[256,256]{1,0:T(8,128)(2,1)} %constant.191.clone.rest_2_, bf16[256,256]{1,0:T(8,128)(2,1)} %constant.192.clone.rest_3_, ...), custom_call_target="tpu_custom_call" | custom-call | tf_op jit(solution)/shard_map/middle2/pallas_call | solution.py:429
  91.8 0.0 copy-start.1
  91.8 0.0 copy-start.2
  91.8 52.7 %all_to_all.20 = f32[128,1,6912]{2,1,0:T(1,128)S(1)} all-to-all(f32[128,1,6912]{2,1,0:T(1,128)S(1)} %bitcast.16), channel_id=1, replica_groups=mesh['px'=8,'py'=16] {'px','py'}, dimensions={0} | all-to-all | bytes 7077888 | tf_op jit(solution)/shard_map/all_to_all | solution.py:420
  144.5 0.0 copy-done.1
  144.5 0.0 copy-done.2
  144.5 4.4 %zlast.1 = f32[48,24,384]{2,1,0:T(8,128)} custom-call(f32[6912,128]{1,0:T(8,128)S(1)} %bitcast.17, bf16[384,384]{1,0:T(8,128)(2,1)S(1)} %copy-done.2, bf16[384,384]{1,0:T(8,128)(2,1)S(1)} %copy-done.1), custom_call_target="tpu_custom_call" | custom-call | tf_op jit(solution)/shard_map/zlast/pallas_call | solution.py:499
  (7 shorter events, 0.0 us)
Async XLA Ops:
  1.7 16.0 %all-to-all-start = ((f32[16,8,128]{2,1,0:T(8,128)}), f32[16,8,128]{2,1,0:T(8,128)S(1)}, u32[]{:S(2)}, u32[]{:S(2)}) async-start(f32[16,8,128]{2,1,0:T(8,128)} %bitcast.25), calls=%async_computation | async-start | bytes 131072 | tf_op jit(solution)/shard_map/all_to_all | solution.py:459
  17.6 25.0 %all-to-all-start.2 = ((f32[128,1,2304]{2,1,0:T(1,128)}), f32[128,1,2304]{2,1,0:T(1,128)S(1)}, u32[]{:S(2)}, u32[]{:S(2)}) async-start(f32[128,1,2304]{2,1,0:T(1,128)} %bitcast.21), calls=%async_computation.2 | async-start | bytes 2359296 | tf_op jit(solution)/shard_map/all_to_all | solution.py:420
  24.2 1.3 copy-start.4
  42.6 38.4 %all-to-all-start.1 = ((f32[128,1,4608]{2,1,0:T(1,128)}), f32[128,1,4608]{2,1,0:T(1,128)S(1)}, u32[]{:S(2)}, u32[]{:S(2)}) async-start(f32[128,1,4608]{2,1,0:T(1,128)} %bitcast.20), calls=%async_computation.1 | async-start | bytes 4718592 | tf_op jit(solution)/shard_map/all_to_all | solution.py:420
  55.9 1.2 copy-start.3
  63.0 1.0 copy-start
  91.8 52.7 %copy-start.1 = (bf16[384,384]{1,0:T(8,128)(2,1)S(1)}, bf16[384,384]{1,0:T(8,128)(2,1)}, u32[]{:S(2)}) copy-start(bf16[384,384]{1,0:T(8,128)(2,1)} %constant.188.clone.t_low) | copy-start | bytes 884740
  91.8 52.7 %copy-start.2 = (bf16[384,384]{1,0:T(8,128)(2,1)S(1)}, bf16[384,384]{1,0:T(8,128)(2,1)}, u32[]{:S(2)}) copy-start(bf16[384,384]{1,0:T(8,128)(2,1)} %constant.187.clone.t_high) | copy-start | bytes 884740

commit v4 on v3

--- a/solution.py
+++ b/solution.py
@@ -88,23 +88,6 @@
     return tw_x, tw_y, tw2
 
 
-def window(kz):
-    row = lax.broadcasted_iota(jnp.int32, (ROWS, 128), 0)
-    lane = lax.broadcasted_iota(jnp.int32, (ROWS, 128), 1)
-    u, k1 = row // N_DEV, row % N_DEV
-    kx = k1 // N_PY + N_PX * (u // 3 + 3 * (lane // 8))
-    ky = k1 % N_PY + N_PY * (u % 3 + 3 * (lane % 8))
-    fx = jnp.where(kx < NG // 2, kx, kx - NG)
-    fy = jnp.where(ky < NG // 2, ky, ky - NG)
-    square = (fx * fx + fy * fy + kz * kz).astype(F32)
-    radial = jnp.sqrt(square) * (2.0 * jnp.pi * RADIUS / NG)
-    safe = jnp.where(radial > 0, radial, 1.0)
-    value = 3.0 * (jnp.sin(safe) - safe * jnp.cos(safe)) / (safe * safe * safe)
-    value = jnp.where(radial > 0, value, 1.0)
-    both = (kz > 0) & (kz < NG // 2)
-    return value * (jnp.where(both, 2.0, 1.0) / float(NG) ** 3)
-
-
 def split(value):
     high = value.astype(BF)
     return high, (value - high.astype(F32)).astype(BF)
@@ -121,6 +104,32 @@
         jnp.concatenate([right[0], right[0], right[1]], axis=right_dim),
         dims,
     )
+
+
+def window_kernel(kz_ref, out):
+    step = 64
+
+    def block(index, carry):
+        kz = kz_ref[index // (ROWS // step)]
+        begin = pl.multiple_of((index % (ROWS // step)) * step, step)
+        row = lax.broadcasted_iota(jnp.int32, (step, 128), 0) + begin
+        lane = lax.broadcasted_iota(jnp.int32, (step, 128), 1)
+        u, k1 = begin // N_DEV, row & (N_DEV - 1)
+        kx = (k1 >> 4) + N_PX * (u // 3 + 3 * (lane >> 3))
+        ky = (k1 & 15) + N_PY * (u % 3 + 3 * (lane & 7))
+        fx = jnp.where(kx < NG // 2, kx, kx - NG)
+        fy = jnp.where(ky < NG // 2, ky, ky - NG)
+        square = (fx * fx + fy * fy + kz * kz).astype(F32)
+        radial = jnp.sqrt(square) * (2.0 * math.pi * RADIUS / NG)
+        safe = jnp.where(radial > 0, radial, 1.0)
+        value = 3.0 * (jnp.sin(safe) - safe * jnp.cos(safe)) / (safe * safe * safe)
+        value = jnp.where(radial > 0, value, 1.0)
+        both = (kz > 0) & (kz < NG // 2)
+        scale = jnp.where(both, 2.0 / float(NG) ** 3, 1.0 / float(NG) ** 3)
+        out[index // (ROWS // step), pl.ds(begin, step), :] = value * scale
+        return carry
+
+    lax.fori_loop(0, 2 * ROWS // step, block, 0)
 
 
 def sort_kernel(photons, cells, counts, owners, out):
@@ -278,83 +287,99 @@
         at = slice(k * N_PY, (k + 1) * N_PY)
         tw1[0, at, :] = cos_x * cos_y - sin_x * sin_y
         tw1[1, at, :] = sin_x * cos_y + cos_x * sin_y
-
-    def plane(p, carry):
-        dev = (dev_high[...], dev_low[...])
-        for a in range(3):
-            at = slice(a * NG, (a + 1) * NG)
-            work[:, at] = dot3(dev, (r_high[p, :, at], r_low[p, :, at]))
-
-        def forward(block, inner):
-            rows = pl.ds(pl.multiple_of(block * 16, 16), 16)
-            rows_im = pl.ds(pl.multiple_of(block * 16 + N_DEV, 16), 16)
-            re, im = [], []
-            for j in range(LB):
-                at = slice(j * 128, (j + 1) * 128)
-                cos, sin = tw1[0, rows, at], tw1[1, rows, at]
-                x, y = work[rows, at], work[rows_im, at]
-                re.append(x * cos + y * sin)
-                im.append(y * cos - x * sin)
-            nine(re, im, -1.0)
-            for j in range(LB):
-                at = slice(j * 128, (j + 1) * 128)
-                cos, sin = tw2[0:1, at], tw2[1:2, at]
-                to = pl.ds(pl.multiple_of(block * 16 + j * N_DEV, 16), 16)
-                l_high[to, :128], l_low[to, :128] = split(re[j] * cos + im[j] * sin)
-                l_high[to, 128:], l_low[to, 128:] = split(im[j] * cos - re[j] * sin)
-            return inner
-
-        lax.fori_loop(0, N_DEV // 16, forward, 0)
-
-        @pl.when(p == 0)
-        def _():
-            for copy in copies[7:]:
-                copy.wait()
-
-        mat = (lane_high[...], lane_low[...])
-        for k in range(3):
-            at = slice(k * NG, (k + 1) * NG)
-            value = dot3((l_high[at, :], l_low[at, :]), mat)
-            w = win[p, at, :]
-            l_high[at, :128], l_low[at, :128] = split(value[:, :128] * w)
-            l_high[at, 128:], l_low[at, 128:] = split(value[:, 128:] * w)
-            back[at, :] = dot3((l_high[at, :], l_low[at, :]), mat, NT)
-
-        def backward(block, inner):
-            rows = pl.ds(pl.multiple_of(block * 16, 16), 16)
-            rows_im = pl.ds(pl.multiple_of(block * 16 + N_DEV, 16), 16)
-            re, im = [], []
-            for j in range(LB):
-                at = slice(j * 128, (j + 1) * 128)
-                cos, sin = tw2[0:1, at], tw2[1:2, at]
-                of = pl.ds(pl.multiple_of(block * 16 + j * N_DEV, 16), 16)
-                x, y = back[of, :128], back[of, 128:]
-                re.append(x * cos - y * sin)
-                im.append(y * cos + x * sin)
-            nine(re, im, 1.0)
-            for j in range(LB):
-                at = slice(j * 128, (j + 1) * 128)
-                cos, sin = tw1[0, rows, at], tw1[1, rows, at]
-                r_high[p, rows, at], r_low[p, rows, at] = split(re[j] * cos - im[j] * sin)
-                r_high[p, rows_im, at], r_low[p, rows_im, at] = split(im[j] * cos + re[j] * sin)
-            return inner
-
-        lax.fori_loop(0, N_DEV // 16, backward, 0)
-        for a in range(3):
-            at = slice(a * NG, (a + 1) * NG)
-            value = dot3(dev, (r_high[p, :, at], r_low[p, :, at]), TN)
-            for c in range(2):
-                for j in range(3):
-                    start = (first_plane + p) * WIDTH + c * LB + a * 3 + j
-                    out[pl.ds(start, N_DEV, stride=out_pitch), :] = value[
-                        c * N_DEV : (c + 1) * N_DEV, j * 128 : (j + 1) * 128
-                    ]
-        return carry
-
-    lax.fori_loop(0, planes, plane, 0)
-    if planes == 2:
-        for j in range(WIDTH):
-            out[pl.ds(j, N_DEV, stride=PITCH), :] = tables[8][pl.ds(j, N_DEV, stride=WIDTH), :]
+    dev = (dev_high[...], dev_low[...])
+    mat = (lane_high[...], lane_low[...])
+
+    def across(p, a):
+        at = slice(a * NG, (a + 1) * NG)
+        work[p, :, at] = dot3(dev, (r_high[p, :, at], r_low[p, :, at]))
+
+    def row_block(block, offset=0):
+        if isinstance(block, int):
+            return slice(block * 16 + offset, block * 16 + offset + 16)
+        return pl.ds(pl.multiple_of(block * 16 + offset, 16), 16)
+
+    def forward(p, block):
+        rows, rows_im = row_block(block), row_block(block, N_DEV)
+        re, im = [], []
+        for j in range(LB):
+            at = slice(j * 128, (j + 1) * 128)
+            cos, sin = tw1[0, rows, at], tw1[1, rows, at]
+            x, y = work[p, rows, at], work[p, rows_im, at]
+            re.append(x * cos + y * sin)
+            im.append(y * cos - x * sin)
+        nine(re, im, -1.0)
+        for j in range(LB):
+            at = slice(j * 128, (j + 1) * 128)
+            cos, sin = tw2[0:1, at], tw2[1:2, at]
+            to = row_block(block, j * N_DEV)
+            l_high[p, to, :128], l_low[p, to, :128] = split(re[j] * cos + im[j] * sin)
+            l_high[p, to, 128:], l_low[p, to, 128:] = split(im[j] * cos - re[j] * sin)
+
+    def along(p, k):
+        at = slice(k * NG, (k + 1) * NG)
+        value = dot3((l_high[p, at, :], l_low[p, at, :]), mat)
+        w = win[planes - 1 - p, at, :]
+        l_high[p, at, :128], l_low[p, at, :128] = split(value[:, :128] * w)
+        l_high[p, at, 128:], l_low[p, at, 128:] = split(value[:, 128:] * w)
+        back[p, at, :] = dot3((l_high[p, at, :], l_low[p, at, :]), mat, NT)
+
+    def backward(p, block):
+        rows, rows_im = row_block(block), row_block(block, N_DEV)
+        re, im = [], []
+        for j in range(LB):
+            at = slice(j * 128, (j + 1) * 128)
+            cos, sin = tw2[0:1, at], tw2[1:2, at]
+            of = row_block(block, j * N_DEV)
+            x, y = back[p, of, :128], back[p, of, 128:]
+            re.append(x * cos - y * sin)
+            im.append(y * cos + x * sin)
+        nine(re, im, 1.0)
+        for j in range(LB):
+            at = slice(j * 128, (j + 1) * 128)
+            cos, sin = tw1[0, rows, at], tw1[1, rows, at]
+            r_high[p, rows, at], r_low[p, rows, at] = split(re[j] * cos - im[j] * sin)
+            r_high[p, rows_im, at], r_low[p, rows_im, at] = split(im[j] * cos + re[j] * sin)
+
+    def home(p, a):
+        at = slice(a * NG, (a + 1) * NG)
+        value = dot3(dev, (r_high[p, :, at], r_low[p, :, at]), TN)
+        for c in range(2):
+            start = (first_plane + p) * WIDTH + c * LB + a * 3
+            store_plane(out, start, out_pitch, value[c * N_DEV : (c + 1) * N_DEV])
+
+    def wait_rest():
+        for copy in copies[7:]:
+            copy.wait()
+
+    stages = [(across, 3), (forward, N_PX), (along, 3), (backward, N_PX), (home, 3)]
+    if planes == 1:
+        for stage, (work_of, parts) in enumerate(stages):
+            if stage == 2:
+                wait_rest()
+            if parts == N_PX:
+
+                def step(block, carry, work_of=work_of):
+                    work_of(0, block)
+                    return carry
+
+                lax.fori_loop(0, parts, step, 0)
+            else:
+                for part in range(parts):
+                    work_of(0, part)
+        return
+    for stage in range(len(stages) + 1):
+        if stage == 2:
+            wait_rest()
+        both = []
+        for p in range(2):
+            if 0 <= stage - p < len(stages):
+                work_of, parts = stages[stage - p]
+                both += [((k + 0.5) / parts, p, work_of, k) for k in range(parts)]
+        for _, p, work_of, part in sorted(both, key=lambda item: item[:2]):
+            work_of(p, part)
+    for j in range(WIDTH):
+        out[pl.ds(j, N_DEV, stride=PITCH), :] = tables[8][pl.ds(j, N_DEV, stride=WIDTH), :]
 
 
 def z_last_kernel(got, t_high, t_low, out):
@@ -434,15 +459,15 @@
         scratch_shapes=[pltpu.VMEM(*shape) for shape in shapes]
         + [
             pltpu.VMEM((2, N_DEV, ROWS), F32),
-            pltpu.VMEM((2 * N_DEV, ROWS), F32),
+            pltpu.VMEM((planes, 2 * N_DEV, ROWS), F32),
             pltpu.VMEM((planes, 2 * N_DEV, ROWS), BF),
             pltpu.VMEM((planes, 2 * N_DEV, ROWS), BF),
-            pltpu.VMEM((ROWS, 256), BF),
-            pltpu.VMEM((ROWS, 256), BF),
-            pltpu.VMEM((ROWS, 256), F32),
+            pltpu.VMEM((planes, ROWS, 256), BF),
+            pltpu.VMEM((planes, ROWS, 256), BF),
+            pltpu.VMEM((planes, ROWS, 256), F32),
             pltpu.SemaphoreType.DMA((len(shapes),)),
         ],
-        compiler_params=limit(20),
+        compiler_params=limit(24),
         name=f"middle{planes}",
     )(*placed_in(pltpu.VMEM, got), *placed_in(pltpu.HBM, *sources))
 
@@ -489,10 +514,14 @@
     me = lax.axis_index(AXES)
     half = N_DEV // 2
     low = jnp.where(me % half == 0, (me // half) * (NG // 2), me % half)
-    win_a = window(me + 64)
-    win_bc = jnp.stack([window(low), win_a])
-    back_a = middle(got_a, 1, (*tables, win_a[None]))
-    back = middle(got_bc, 2, (*tables, win_bc, back_a))
+    win = pl.pallas_call(
+        window_kernel,
+        out_shape=jax.ShapeDtypeStruct((2, ROWS, 128), F32),
+        in_specs=[smem],
+        name="window",
+    )(jnp.stack([me + 64, low]).astype(jnp.int32))
+    back_a = middle(got_a, 1, (*tables, win))
+    back = middle(got_bc, 2, (*tables, win, back_a))
     got = exchange(back)
     whole = pl.BlockSpec((N_DEV * PITCH, 128), lambda i: (0, 0))
     whole_t = pl.BlockSpec((3 * N_DEV, NG), lambda i: (0, 0))

time: 151 us -> 149 us (0.987)
  other arithmetic: 9.07 us -> 1.93 us
  Pallas kernels: 37.3 us -> 41.4 us
    pallas_call x0 -> x1, Pallas kernels: none -> 8.75 us  [on_device(): pl.pallas_call(window_kernel, out_shape=jax.ShapeDtypeStruct((2, ROWS, 12...]
    mul x1 -> x0, other arithmetic: 6.58 us -> none  [window(): return value * (jnp.where(both, 2.0, 1.0) / float(NG) ** 3)]
    pallas_call x2, Pallas kernels: 16.6 us -> 14.2 us  [middle(): pl.pallas_call(functools.partial(middle_kernel, planes), out_shape=out_sh...]
    pallas_call x1, Pallas kernels: 10.2 us -> 7.94 us  [on_device(): pl.pallas_call(paint_kernel, out_shape=jax.ShapeDtypeStruct((N_DEV * 2 *...]
  transfers between devices with their start and end apart: 3 -> 3, of which waited for: 3 -> 3; matrix products, arithmetic and copies ran while one was open for 6% -> 1% of each run, Pallas kernels for 14% -> 18%
where the time goes in v4:
time: 149 us; the launch traced here: 146 us
  blocking collectives  52.7 us (35%)
  Pallas kernels  41.4 us (28%)
  waiting for transfers between devices  27.4 us (18%)
  starting transfers between devices  21.8 us (15%)
  other arithmetic  1.93 us (1%)
    all_to_all x1, blocking collectives, exchange(): return lax.all_to_all(send, AXES, 0, 0, tiled=True).reshape(rows.shape)  52.7 us
    all_to_all x2, waiting for transfers between devices, exchange(): return lax.all_to_all(send, AXES, 0, 0, tiled=True).reshape(rows.shape)  24.6 us
    pallas_call x2, Pallas kernels, middle(): pl.pallas_call(functools.partial(middle_kernel, planes), out_shape=out_sh...  14.2 us
    all_to_all x2, starting transfers between devices, exchange(): return lax.all_to_all(send, AXES, 0, 0, tiled=True).reshape(rows.shape)  13.2 us
    pallas_call x1, Pallas kernels, on_device(): pl.pallas_call(window_kernel, out_shape=jax.ShapeDtypeStruct((2, ROWS, 12...  8.75 us
    all_to_all x1, starting transfers between devices, on_device(): lax.all_to_all(send.reshape(N_PY, 2 * CAP, SLOTS), 'py', 0, 0, tiled=True)  8.63 us
    pallas_call x1, Pallas kernels, on_device(): pl.pallas_call(paint_kernel, out_shape=jax.ShapeDtypeStruct((N_DEV * 2 *...  7.94 us
    pallas_call x1, Pallas kernels, on_device(): pl.pallas_call(z_density_kernel, out_shape=(jax.ShapeDtypeStruct((N_DEV *...  4.48 us
  transfers between devices with their start and end apart: 3, of which 3 were waited for; matrix products, arithmetic and copies ran while one was open for 1% of the time, Pallas kernels for 18%

profile of v4, /device:TPU:7, one launch (start us, length us, event | category | flops | bytes accessed | tf_op | source)
XLA Modules:
  0.0 146.4 jit_solution(384610759742595309)
XLA Ops:
  0.0 1.6 %sort.1 = f32[128,128]{1,0:T(8,128)} custom-call(f32[32,128]{1,0:T(8,128)} %photons.1, s32[32,128]{1,0:T(8,128)} %cells.1, s32[1,32]{1,0:T(1,128)} %bitcast.29, s32[1,32]{1,0:T(1,128)} %bitcast.30), custom_call_target="tpu_custom_call" | custom-call | tf_op jit(solution)/shard_map/sort/pallas_call | solution.py:479
  1.6 8.6 %all-to-all-start = ((f32[16,8,128]{2,1,0:T(8,128)}), f32[16,8,128]{2,1,0:T(8,128)S(1)}, u32[]{:S(2)}, u32[]{:S(2)}) async-start(f32[16,8,128]{2,1,0:T(8,128)} %bitcast.27), calls=%async_computation | async-start | bytes 131072 | tf_op jit(solution)/shard_map/all_to_all | solution.py:484
  10.3 4.5 %zdensity.1 = (f32[2304,128]{1,0:T(8,128)}, f32[128,1152]{1,0:T(8,128)}) custom-call(f32[48,24,384]{2,1,0:T(8,128)} %density.1, bf16[384,384]{1,0:T(8,128)(2,1)} %constant.65.clone.t_high, bf16[384,384]{1,0:T(8,128)(2,1)} %constant.66.clone.t_low), custom_call_target="tpu_custom_call" | custom-call | tf_op jit(solution)/shard_map/zdensity/pallas_call | solution.py:486
  14.8 2.8 %all-to-all-done = f32[16,8,128]{2,1,0:T(8,128)S(1)} async-done(((f32[16,8,128]{2,1,0:T(8,128)}), f32[16,8,128]{2,1,0:T(8,128)S(1)}, u32[]{:S(2)}, u32[]{:S(2)}) %all-to-all-start) | async-done | bytes 65568 | tf_op jit(solution)/shard_map/all_to_all | solution.py:484
  17.6 6.5 %all-to-all-start.2 = ((f32[128,1,2304]{2,1,0:T(1,128)}), f32[128,1,2304]{2,1,0:T(1,128)S(1)}, u32[]{:S(2)}, u32[]{:S(2)}) async-start(f32[128,1,2304]{2,1,0:T(1,128)} %bitcast.23), calls=%async_computation.2 | async-start | bytes 2359296 | tf_op jit(solution)/shard_map/all_to_all | solution.py:445
  24.1 0.1 fusion
  24.2 0.0 copy-start.3
  24.2 0.7 select_reduce_fusion.counts
  24.9 0.6 convert_bitcast_fusion.cells
  25.5 0.0 copy-done.3
  25.5 7.9 %paint.1 = f32[4608,128]{1,0:T(8,128)} custom-call(f32[64,128]{1,0:T(8,128)} %bitcast.25, s32[64,128]{1,0:T(8,128)} %convert_bitcast_fusion.cells, s32[64]{0:T(128)} %select_reduce_fusion.counts, f32[128,1152]{1,0:T(8,128)} %get-tuple-element.11.z_density, bf16[384,384]{1,0:T(8,128)(2,1)} %constant.65.clone.t_high, bf16[384,384]{1,0:T(8,128)(2,1)} %constant.66.clone.t_low), custom_call_target="tpu_custom_call" | custom-call | tf_op jit(solution)/shard_map/paint/pallas_call | solution.py:504
  33.5 9.1 %all-to-all-done.2 = f32[128,1,2304]{2,1,0:T(1,128)S(1)} async-done(((f32[128,1,2304]{2,1,0:T(1,128)}), f32[128,1,2304]{2,1,0:T(1,128)S(1)}, u32[]{:S(2)}, u32[]{:S(2)}) %all-to-all-start.2) | async-done | bytes 1179680 | tf_op jit(solution)/shard_map/all_to_all | solution.py:445
  42.6 6.7 %all-to-all-start.1 = ((f32[128,1,4608]{2,1,0:T(1,128)}), f32[128,1,4608]{2,1,0:T(1,128)S(1)}, u32[]{:S(2)}, u32[]{:S(2)}) async-start(f32[128,1,4608]{2,1,0:T(1,128)} %bitcast.22), calls=%async_computation.1 | async-start | bytes 4718592 | tf_op jit(solution)/shard_map/all_to_all | solution.py:445
  49.3 0.6 pad_add_fusion.kz_ref
  49.9 8.8 %window.1.rest_7_ = f32[2,1152,128]{2,1,0:T(8,128)} custom-call(s32[2]{0:T(128)} %pad_add_fusion.kz_ref), custom_call_target="tpu_custom_call" | custom-call | tf_op jit(solution)/shard_map/window/pallas_call | solution.py:517
  58.6 5.9 %middle1.1.rest_8_ = f32[2304,128]{1,0:T(8,128)S(1)} custom-call(f32[2304,128]{1,0:T(8,128)S(1)} %bitcast.21, bf16[256,256]{1,0:T(8,128)(2,1)} %constant.67.clone.rest_0_, bf16[256,256]{1,0:T(8,128)(2,1)} %constant.68.clone.rest_1_, bf16[256,256]{1,0:T(8,128)(2,1)} %constant.69.clone.rest_2_, bf16[256,256]{1,0:T(8,128)(2,1)} %constant.70.clone.rest_3_, ...), custom_call_target="tpu_custom_call" | custom-call | tf_op jit(solution)/shard_map/middle1/pallas_call | solution.py:454
  64.5 0.0 copy-start
  64.5 1.0 copy-done
  65.5 15.5 %all-to-all-done.1 = f32[128,1,4608]{2,1,0:T(1,128)S(1)} async-done(((f32[128,1,4608]{2,1,0:T(1,128)}), f32[128,1,4608]{2,1,0:T(1,128)S(1)}, u32[]{:S(2)}, u32[]{:S(2)}) %all-to-all-start.1) | async-done | bytes 2359328 | tf_op jit(solution)/shard_map/all_to_all | solution.py:445
  81.0 8.3 %middle2.1 = f32[6912,128]{1,0:T(8,128)S(1)} custom-call(f32[4608,128]{1,0:T(8,128)S(1)} %bitcast.20, bf16[256,256]{1,0:T(8,128)(2,1)} %constant.67.clone.rest_0_, bf16[256,256]{1,0:T(8,128)(2,1)} %constant.68.clone.rest_1_, bf16[256,256]{1,0:T(8,128)(2,1)} %constant.69.clone.rest_2_, bf16[256,256]{1,0:T(8,128)(2,1)} %constant.70.clone.rest_3_, ...), custom_call_target="tpu_custom_call" | custom-call | tf_op jit(solution)/shard_map/middle2/pallas_call | solution.py:454
  89.3 0.0 copy-start.1
  89.3 0.0 copy-start.2
  89.4 52.7 %all_to_all.20 = f32[128,1,6912]{2,1,0:T(1,128)S(1)} all-to-all(f32[128,1,6912]{2,1,0:T(1,128)S(1)} %bitcast.18), channel_id=1, replica_groups=mesh['px'=8,'py'=16] {'px','py'}, dimensions={0} | all-to-all | bytes 7077888 | tf_op jit(solution)/shard_map/all_to_all | solution.py:445
  142.0 0.0 copy-done.1
  142.0 0.0 copy-done.2
  142.0 4.4 %zlast.1 = f32[48,24,384]{2,1,0:T(8,128)} custom-call(f32[6912,128]{1,0:T(8,128)S(1)} %bitcast.19, bf16[384,384]{1,0:T(8,128)(2,1)S(1)} %copy-done.2, bf16[384,384]{1,0:T(8,128)(2,1)S(1)} %copy-done.1), custom_call_target="tpu_custom_call" | custom-call | tf_op jit(solution)/shard_map/zlast/pallas_call | solution.py:528
  (1 shorter events, 0.0 us)
Async XLA Ops:
  1.6 16.0 %all-to-all-start = ((f32[16,8,128]{2,1,0:T(8,128)}), f32[16,8,128]{2,1,0:T(8,128)S(1)}, u32[]{:S(2)}, u32[]{:S(2)}) async-start(f32[16,8,128]{2,1,0:T(8,128)} %bitcast.27), calls=%async_computation | async-start | bytes 131072 | tf_op jit(solution)/shard_map/all_to_all | solution.py:484
  17.6 25.0 %all-to-all-start.2 = ((f32[128,1,2304]{2,1,0:T(1,128)}), f32[128,1,2304]{2,1,0:T(1,128)S(1)}, u32[]{:S(2)}, u32[]{:S(2)}) async-start(f32[128,1,2304]{2,1,0:T(1,128)} %bitcast.23), calls=%async_computation.2 | async-start | bytes 2359296 | tf_op jit(solution)/shard_map/all_to_all | solution.py:445
  24.2 1.3 copy-start.3
  42.6 38.4 %all-to-all-start.1 = ((f32[128,1,4608]{2,1,0:T(1,128)}), f32[128,1,4608]{2,1,0:T(1,128)S(1)}, u32[]{:S(2)}, u32[]{:S(2)}) async-start(f32[128,1,4608]{2,1,0:T(1,128)} %bitcast.22), calls=%async_computation.1 | async-start | bytes 4718592 | tf_op jit(solution)/shard_map/all_to_all | solution.py:445
  64.5 1.0 copy-start
  89.3 52.7 %copy-start.1 = (bf16[384,384]{1,0:T(8,128)(2,1)S(1)}, bf16[384,384]{1,0:T(8,128)(2,1)}, u32[]{:S(2)}) copy-start(bf16[384,384]{1,0:T(8,128)(2,1)} %constant.66.clone.t_low) | copy-start | bytes 884740
  89.3 52.7 %copy-start.2 = (bf16[384,384]{1,0:T(8,128)(2,1)S(1)}, bf16[384,384]{1,0:T(8,128)(2,1)}, u32[]{:S(2)}) copy-start(bf16[384,384]{1,0:T(8,128)(2,1)} %constant.65.clone.t_high) | copy-start | bytes 884740

commit v5 on v4

--- a/solution.py
+++ b/solution.py
@@ -46,17 +46,18 @@
     return high, low
 
 
-def z_table():
-    z = np.arange(NG)
-    table = np.zeros((3 * N_DEV, NG))
-    for d in range(N_DEV):
-        angle = 2.0 * np.pi * (((64 + d) * z) % NG) / NG
-        table[d], table[N_DEV + d] = np.cos(angle), np.sin(angle)
-    for d in range(N_DEV // 2):
-        angle = 2.0 * np.pi * ((d * z) % NG) / NG
-        table[2 * N_DEV + d], table[2 * N_DEV + 64 + d] = np.cos(angle), np.sin(angle)
-    table[2 * N_DEV + 64] = 1.0 - 2.0 * (z % 2)
-    return split_np(table)
+def z_tables():
+    z = np.arange(128)
+    kz = 3 * np.arange(N_DEV // 2)
+    angle = 2.0 * np.pi * (np.outer(kz, z) % NG) / NG
+    few = np.concatenate([np.cos(angle), np.sin(angle)])
+    few[N_DEV // 2] = 1.0 - 2.0 * (z % 2)
+    kz = 3 * np.arange(N_DEV) // 2 + 1
+    angle = 2.0 * np.pi * (np.outer(kz, z) % NG) / NG
+    sign = np.where(kz % 3 == 1, 1.0, -1.0)[:, None]
+    cos, sin = np.cos(angle), np.sin(angle)
+    many = np.block([[cos, -sign * sin], [sin, sign * cos]])
+    return (*split_np(few), *split_np(many))
 
 
 def real_form(frac):
@@ -163,18 +164,31 @@
         out[pl.ds(half, slots, stride=2), :] = jnp.where(live, total, 0.0)
 
 
-def z_density_kernel(density, t_high, t_low, out, few, high, low):
+def fold(parts):
+    t = parts[1] + parts[2]
+    return parts[0] + t, parts[0] - 0.5 * t, (parts[1] - parts[2]) * HALF_ROOT3
+
+
+def z_density_kernel(density, few_high, few_low, many_high, many_low, out, few, *scratch):
+    high0, low0, high1, low1 = scratch
     for a in range(3):
         for a2 in range(3):
+            at = slice((a * 3 + a2) * 128, (a * 3 + a2 + 1) * 128)
             block = density[a * 16 : (a + 1) * 16, a2 * 8 : (a2 + 1) * 8, :].reshape(128, NG)
-            at = slice((a * 3 + a2) * 128, (a * 3 + a2 + 1) * 128)
-            high[at, :], low[at, :] = split(block)
+            store_folded(scratch, at, fold([block[:, k * 128 : (k + 1) * 128] for k in range(3)]))
     for a in range(3):
         at = slice(a * NG, (a + 1) * NG)
-        value = dot3((t_high[...], t_low[...]), (high[at, :], low[at, :]), NT)
+        value = dot3((many_high[...], many_low[...]), (high1[at, :], low1[at, :]), NT)
         for c in range(2):
             store_plane(out, c * LB + 3 * a, WIDTH, value[c * N_DEV : (c + 1) * N_DEV])
-        few[:, at] = value[2 * N_DEV :]
+        few[:, at] = dot3((few_high[...], few_low[...]), (high0[at, :], low0[at, :]), NT)
+
+
+def store_folded(scratch, at, folded):
+    high0, low0, high1, low1 = scratch
+    high0[at, :], low0[at, :] = split(folded[0])
+    high1[at, :128], low1[at, :128] = split(folded[1])
+    high1[at, 128:], low1[at, 128:] = split(folded[2])
 
 
 def store_plane(out, start, pitch, value):
@@ -183,8 +197,10 @@
         out[rows, :] = value[:, j * 128 : (j + 1) * 128]
 
 
-def paint_kernel(weights, cells, counts, z_density, t_high, t_low, out, *scratch):
-    fields, high, low = scratch[:FIELDS], scratch[FIELDS], scratch[FIELDS + 1]
+def paint_kernel(weights, cells, counts, z_density, few_high, few_low, many_high, many_low, out,
+                 *scratch):
+    fields, folded = scratch[:FIELDS], scratch[FIELDS:]
+    high0, low0, high1, low1 = folded
     for field in fields:
         field[...] = jnp.zeros(field.shape, F32)
     lane = lax.broadcasted_iota(jnp.int32, (1, 128), 1)
@@ -213,9 +229,10 @@
         return carry
 
     lax.fori_loop(0, counts.shape[0], block, 0)
-    for part in range(3):
-        for a in range(3):
-            for a2 in range(3):
+    for a in range(3):
+        for a2 in range(3):
+            parts = []
+            for part in range(3):
                 tiles = []
                 for b in range(16):
                     row = (16 * a + b) * CY + 8 * a2
@@ -223,20 +240,21 @@
                     for field in fields[1:]:
                         tile = tile + field[pl.ds(row * 3 + part, 8, stride=3), :]
                     tiles.append(tile)
-                at = slice((a * 3 + a2) * 128, (a * 3 + a2 + 1) * 128)
-                to = slice(part * 128, (part + 1) * 128)
-                high[at, to], low[at, to] = split(jnp.concatenate(tiles, axis=0))
+                parts.append(jnp.concatenate(tiles, axis=0))
+            at = slice((a * 3 + a2) * 128, (a * 3 + a2 + 1) * 128)
+            store_folded(folded, at, fold(parts))
     pitch = 2 * WIDTH
     half = N_DEV // 2
     first = lax.broadcasted_iota(jnp.int32, (half, NG), 0) == 0
     for a in range(3):
         at = slice(a * NG, (a + 1) * NG)
-        value = dot3((t_high[...], t_low[...]), (high[at, :], low[at, :]), NT)
+        value = dot3((many_high[...], many_low[...]), (high1[at, :], low1[at, :]), NT)
         for c in range(2):
             plane = value[c * N_DEV : (c + 1) * N_DEV]
             store_plane(out, WIDTH + c * LB + 3 * a, pitch, plane)
         dens_cos, dens_sin = z_density[:half, at], z_density[half:, at]
-        phot_cos, phot_sin = value[2 * N_DEV : 2 * N_DEV + half], value[2 * N_DEV + half :]
+        value = dot3((few_high[...], few_low[...]), (high0[at, :], low0[at, :]), NT)
+        phot_cos, phot_sin = value[:half], value[half:]
         low_rows, top_rows = 3 * a, half * pitch + 3 * a
         store_plane(out, low_rows, pitch, jnp.where(first, phot_cos, dens_cos))
         store_plane(out, low_rows + LB, pitch, jnp.where(first, dens_cos, dens_sin))
@@ -263,7 +281,7 @@
     count = len(TABLE_SHAPES) + (2 if planes == 2 else 1)
     sources, out, rest = rest[:count], rest[count], rest[count + 1 :]
     tables, (tw1, work, r_high, r_low, l_high, l_low, back, sems) = rest[:count], rest[count:]
-    dev_high, dev_low, lane_high, lane_low, tw_x, tw_y, tw2, win = tables[:8]
+    dev_high, dev_low, tw_x, tw_y, tw2, lane_high, lane_low, win = tables[:8]
     copies = [
         pltpu.make_async_copy(source, table, sems.at[k])
         for k, (source, table) in enumerate(zip(sources, tables))
@@ -279,20 +297,28 @@
                 at, to = slice(c * N_DEV, (c + 1) * N_DEV), slice(j * 128, (j + 1) * 128)
                 r_high[p, at, to] = high
                 r_low[p, at, to] = low
-    for copy in copies[:7]:
-        copy.wait()
-    for k in range(N_PX):
-        cos_x, sin_x = tw_x[0, k : k + 1, :], tw_x[1, k : k + 1, :]
-        cos_y, sin_y = tw_y[0], tw_y[1]
-        at = slice(k * N_PY, (k + 1) * N_PY)
-        tw1[0, at, :] = cos_x * cos_y - sin_x * sin_y
-        tw1[1, at, :] = sin_x * cos_y + cos_x * sin_y
-    dev = (dev_high[...], dev_low[...])
-    mat = (lane_high[...], lane_low[...])
+
+    def dev():
+        return dev_high[...], dev_low[...]
+
+    def mat():
+        return lane_high[...], lane_low[...]
+
+    def arrive(stage):
+        if stage < 3:
+            for copy in copies[(0, 2, 5)[stage] : (2, 5, len(copies))[stage]]:
+                copy.wait()
+        if stage == 1:
+            for k in range(N_PX):
+                cos_x, sin_x = tw_x[0, k : k + 1, :], tw_x[1, k : k + 1, :]
+                cos_y, sin_y = tw_y[0], tw_y[1]
+                at = slice(k * N_PY, (k + 1) * N_PY)
+                tw1[0, at, :] = cos_x * cos_y - sin_x * sin_y
+                tw1[1, at, :] = sin_x * cos_y + cos_x * sin_y
 
     def across(p, a):
         at = slice(a * NG, (a + 1) * NG)
-        work[p, :, at] = dot3(dev, (r_high[p, :, at], r_low[p, :, at]))
+        work[p, :, at] = dot3(dev(), (r_high[p, :, at], r_low[p, :, at]))
 
     def row_block(block, offset=0):
         if isinstance(block, int):
@@ -318,11 +344,11 @@
 
     def along(p, k):
         at = slice(k * NG, (k + 1) * NG)
-        value = dot3((l_high[p, at, :], l_low[p, at, :]), mat)
+        value = dot3((l_high[p, at, :], l_low[p, at, :]), mat())
         w = win[planes - 1 - p, at, :]
         l_high[p, at, :128], l_low[p, at, :128] = split(value[:, :128] * w)
         l_high[p, at, 128:], l_low[p, at, 128:] = split(value[:, 128:] * w)
-        back[p, at, :] = dot3((l_high[p, at, :], l_low[p, at, :]), mat, NT)
+        back[p, at, :] = dot3((l_high[p, at, :], l_low[p, at, :]), mat(), NT)
 
     def backward(p, block):
         rows, rows_im = row_block(block), row_block(block, N_DEV)
@@ -343,20 +369,15 @@
 
     def home(p, a):
         at = slice(a * NG, (a + 1) * NG)
-        value = dot3(dev, (r_high[p, :, at], r_low[p, :, at]), TN)
+        value = dot3(dev(), (r_high[p, :, at], r_low[p, :, at]), TN)
         for c in range(2):
             start = (first_plane + p) * WIDTH + c * LB + a * 3
             store_plane(out, start, out_pitch, value[c * N_DEV : (c + 1) * N_DEV])
 
-    def wait_rest():
-        for copy in copies[7:]:
-            copy.wait()
-
     stages = [(across, 3), (forward, N_PX), (along, 3), (backward, N_PX), (home, 3)]
     if planes == 1:
         for stage, (work_of, parts) in enumerate(stages):
-            if stage == 2:
-                wait_rest()
+            arrive(stage)
             if parts == N_PX:
 
                 def step(block, carry, work_of=work_of):
@@ -369,8 +390,7 @@
                     work_of(0, part)
         return
     for stage in range(len(stages) + 1):
-        if stage == 2:
-            wait_rest()
+        arrive(stage)
         both = []
         for p in range(2):
             if 0 <= stage - p < len(stages):
@@ -382,11 +402,11 @@
         out[pl.ds(j, N_DEV, stride=PITCH), :] = tables[8][pl.ds(j, N_DEV, stride=WIDTH), :]
 
 
-def z_last_kernel(got, t_high, t_low, out):
+def z_last_kernel(got, few_high, few_low, many_high, many_low, out):
     a = pl.program_id(0)
     half = N_DEV // 2
     first = lax.broadcasted_iota(jnp.int32, (half, 128), 0) == 0
-    dens, phot = [], []
+    many, few = [[], []], [[], []]
     for a2 in range(3):
 
         def load(plane, c, begin=0, count=N_DEV):
@@ -395,41 +415,35 @@
 
         re_low, im_low = load(1, 0, 0, half), load(1, 1, 0, half)
         re_top, im_top = load(1, 0, half, half), load(1, 1, half, half)
-        dens.append(
-            jnp.concatenate(
-                [
-                    load(0, 0),
-                    load(0, 1),
-                    jnp.where(first, im_low, re_low),
-                    jnp.where(first, im_top, im_low),
-                ],
-                axis=0,
-            )
-        )
-        phot.append(
-            jnp.concatenate(
-                [
-                    load(2, 0),
-                    load(2, 1),
-                    jnp.where(first, re_low, re_top),
-                    jnp.where(first, re_top, im_top),
-                ],
-                axis=0,
-            )
-        )
-    table = (t_high[...], t_low[...])
-    smooth_d = dot3(split(jnp.concatenate(dens, axis=1)), table, TN)
-    smooth_p = dot3(split(jnp.concatenate(phot, axis=1)), table, TN)
-    value = jnp.clip(smooth_p / jnp.maximum(smooth_d, 0.5), 0.0, 1.0)
-    for a2 in range(3):
-        out[:, a2 * 8 : (a2 + 1) * 8, :] = value[a2 * 128 : (a2 + 1) * 128].reshape(16, 8, NG)
-
-
-TABLE_SHAPES = [((256, 256), BF)] * 4 + [
+        many[0].append(jnp.concatenate([load(0, 0), load(0, 1)], axis=0))
+        many[1].append(jnp.concatenate([load(2, 0), load(2, 1)], axis=0))
+        dens = [jnp.where(first, im_low, re_low), jnp.where(first, im_top, im_low)]
+        phot = [jnp.where(first, re_low, re_top), jnp.where(first, re_top, im_top)]
+        few[0].append(jnp.concatenate(dens, axis=0))
+        few[1].append(jnp.concatenate(phot, axis=0))
+    smooth = []
+    for k in range(2):
+        same = dot3(split(jnp.concatenate(few[k], axis=1)), (few_high[...], few_low[...]), TN)
+        turn = dot3(split(jnp.concatenate(many[k], axis=1)), (many_high[...], many_low[...]), TN)
+        even, odd = turn[:, :128], turn[:, 128:] * HALF_ROOT3
+        rest = same - 0.5 * even
+        smooth.append((same + even, rest + odd, rest - odd))
+    for k in range(3):
+        value = jnp.clip(smooth[1][k] / jnp.maximum(smooth[0][k], 0.5), 0.0, 1.0)
+        for a2 in range(3):
+            block = value[a2 * 128 : (a2 + 1) * 128].reshape(16, 8, 128)
+            out[:, a2 * 8 : (a2 + 1) * 8, k * 128 : (k + 1) * 128] = block
+
+
+SQUARE = [((256, 256), BF)] * 2
+TABLE_SHAPES = [
+    *SQUARE,
     ((2, N_PX, ROWS), F32),
     ((2, N_PY, ROWS), F32),
     ((8, ROWS), F32),
+    *SQUARE,
 ]
+FOLDED = [pltpu.VMEM((ROWS, width), BF) for width in (128, 128, 256, 256)]
 
 
 def placed_in(space, *arrays):
@@ -473,8 +487,8 @@
 
 
 def on_device(photons, halo_cells, halo_counts, owners, density):
-    table = z_table()
-    tables = (*device_table(), *lane_table(), *twiddles())
+    table = z_tables()
+    tables = (*device_table(), *twiddles(), *lane_table())
 
     send = pl.pallas_call(
         sort_kernel,
@@ -489,7 +503,7 @@
             jax.ShapeDtypeStruct((N_DEV * WIDTH, 128), F32),
             jax.ShapeDtypeStruct((N_DEV, ROWS), F32),
         ),
-        scratch_shapes=[pltpu.VMEM((ROWS, NG), BF), pltpu.VMEM((ROWS, NG), BF)],
+        scratch_shapes=FOLDED,
         name="zdensity",
     )(density, *table)
     send_a, halos = lax.optimization_barrier((send_a, halos))
@@ -504,31 +518,32 @@
     send_bc = pl.pallas_call(
         paint_kernel,
         out_shape=jax.ShapeDtypeStruct((N_DEV * 2 * WIDTH, 128), F32),
-        in_specs=[smem, smem, smem, vmem, vmem, vmem],
+        in_specs=[smem, smem, smem] + [vmem] * 5,
         scratch_shapes=[pltpu.VMEM((ROWS * 3, 128), F32)] * FIELDS
-        + [pltpu.VMEM((ROWS, NG), BF), pltpu.VMEM((ROWS, NG), BF)],
+        + FOLDED,
         name="paint",
     )(weights, cells, counts, few, *table)
     got_bc = exchange(send_bc)
 
     me = lax.axis_index(AXES)
     half = N_DEV // 2
-    low = jnp.where(me % half == 0, (me // half) * (NG // 2), me % half)
+    high = 3 * me // 2 + 1
+    low = jnp.where(me % half == 0, (me // half) * (NG // 2), 3 * (me % half))
     win = pl.pallas_call(
         window_kernel,
         out_shape=jax.ShapeDtypeStruct((2, ROWS, 128), F32),
         in_specs=[smem],
         name="window",
-    )(jnp.stack([me + 64, low]).astype(jnp.int32))
+    )(jnp.stack([high, low]).astype(jnp.int32))
     back_a = middle(got_a, 1, (*tables, win))
     back = middle(got_bc, 2, (*tables, win, back_a))
     got = exchange(back)
     whole = pl.BlockSpec((N_DEV * PITCH, 128), lambda i: (0, 0))
-    whole_t = pl.BlockSpec((3 * N_DEV, NG), lambda i: (0, 0))
+    whole_t = [pl.BlockSpec(t.shape, lambda i: (0, 0)) for t in table]
     return pl.pallas_call(
         z_last_kernel,
         grid=(3,),
-        in_specs=[whole, whole_t, whole_t],
+        in_specs=[whole] + whole_t,
         out_specs=pl.BlockSpec((16, CY, NG), lambda i: (i, 0, 0)),
         out_shape=jax.ShapeDtypeStruct((CX, CY, NG), F32),
         compiler_params=limit(16),

time: 149 us -> 147 us (0.987)
    pallas_call x1, Pallas kernels: 7.94 us -> 9.48 us  [on_device(): pl.pallas_call(paint_kernel, out_shape=jax.ShapeDtypeStruct((N_DEV * 2 *...]
  transfers between devices with their start and end apart: 3 -> 3, of which waited for: 3 -> 3; matrix products, arithmetic and copies ran while one was open for 1% -> 1% of each run, Pallas kernels for 18% -> 19%
where the time goes in v5:
time: 147 us; the launch traced here: 145 us
  blocking collectives  52.7 us (36%)
  Pallas kernels  40.9 us (28%)
  waiting for transfers between devices  26.8 us (18%)
  starting transfers between devices  21.2 us (14%)
  other arithmetic  1.81 us (1%)
    all_to_all x1, blocking collectives, exchange(): return lax.all_to_all(send, AXES, 0, 0, tiled=True).reshape(rows.shape)  52.7 us
    all_to_all x2, waiting for transfers between devices, exchange(): return lax.all_to_all(send, AXES, 0, 0, tiled=True).reshape(rows.shape)  23.3 us
    pallas_call x2, Pallas kernels, middle(): pl.pallas_call(functools.partial(middle_kernel, planes), out_shape=out_sh...  14.1 us
    all_to_all x2, starting transfers between devices, exchange(): return lax.all_to_all(send, AXES, 0, 0, tiled=True).reshape(rows.shape)  12.5 us
    pallas_call x1, Pallas kernels, on_device(): pl.pallas_call(paint_kernel, out_shape=jax.ShapeDtypeStruct((N_DEV * 2 *...  9.48 us
    pallas_call x1, Pallas kernels, on_device(): pl.pallas_call(window_kernel, out_shape=jax.ShapeDtypeStruct((2, ROWS, 12...  8.75 us
    all_to_all x1, starting transfers between devices, on_device(): lax.all_to_all(send.reshape(N_PY, 2 * CAP, SLOTS), 'py', 0, 0, tiled=True)  8.63 us
    pallas_call x1, Pallas kernels, on_device(): pl.pallas_call(z_density_kernel, out_shape=(jax.ShapeDtypeStruct((N_DEV *...  3.84 us
  transfers between devices with their start and end apart: 3, of which 3 were waited for; matrix products, arithmetic and copies ran while one was open for 1% of the time, Pallas kernels for 19%

profile of v5, /device:TPU:7, one launch (start us, length us, event | category | flops | bytes accessed | tf_op | source)
XLA Modules:
  0.0 144.6 jit_solution(8768191203676482124)
XLA Ops:
  0.0 1.6 %sort.1 = f32[128,128]{1,0:T(8,128)} custom-call(f32[32,128]{1,0:T(8,128)} %photons.1, s32[32,128]{1,0:T(8,128)} %cells.1, s32[1,32]{1,0:T(1,128)} %bitcast.29, s32[1,32]{1,0:T(1,128)} %bitcast.30), custom_call_target="tpu_custom_call" | custom-call | tf_op jit(solution)/shard_map/sort/pallas_call | solution.py:493
  1.6 8.6 %all-to-all-start = ((f32[16,8,128]{2,1,0:T(8,128)}), f32[16,8,128]{2,1,0:T(8,128)S(1)}, u32[]{:S(2)}, u32[]{:S(2)}) async-start(f32[16,8,128]{2,1,0:T(8,128)} %bitcast.27), calls=%async_computation | async-start | bytes 131072 | tf_op jit(solution)/shard_map/all_to_all | solution.py:498
  10.3 3.8 %zdensity.1 = (f32[2304,128]{1,0:T(8,128)}, f32[128,1152]{1,0:T(8,128)}) custom-call(f32[48,24,384]{2,1,0:T(8,128)} %density.1, bf16[128,128]{1,0:T(8,128)(2,1)} %constant.81.clone.few_high, bf16[128,128]{1,0:T(8,128)(2,1)} %constant.82.clone.few_low, bf16[256,256]{1,0:T(8,128)(2,1)} %constant.83.clone.many_high, bf16[256,256]{1,0:T(8,128)(2,1)} %constant.84.clone.many_low), custom_call_target="tpu_custom_call" | custom-call | tf_op jit(solution)/shard_map/zdensity/pallas_call | solution.py:500
  14.1 3.5 %all-to-all-done = f32[16,8,128]{2,1,0:T(8,128)S(1)} async-done(((f32[16,8,128]{2,1,0:T(8,128)}), f32[16,8,128]{2,1,0:T(8,128)S(1)}, u32[]{:S(2)}, u32[]{:S(2)}) %all-to-all-start) | async-done | bytes 65568 | tf_op jit(solution)/shard_map/all_to_all | solution.py:498
  17.6 5.9 %all-to-all-start.2 = ((f32[128,1,2304]{2,1,0:T(1,128)}), f32[128,1,2304]{2,1,0:T(1,128)S(1)}, u32[]{:S(2)}, u32[]{:S(2)}) async-start(f32[128,1,2304]{2,1,0:T(1,128)} %bitcast.23), calls=%async_computation.2 | async-start | bytes 2359296 | tf_op jit(solution)/shard_map/all_to_all | solution.py:459
  23.5 0.1 fusion
  23.5 0.0 copy-start.5
  23.6 0.6 select_reduce_fusion.counts
  24.2 0.6 convert_bitcast_fusion.cells
  24.8 0.0 copy-done.5
  24.8 9.5 %paint.1 = f32[4608,128]{1,0:T(8,128)} custom-call(f32[64,128]{1,0:T(8,128)} %bitcast.25, s32[64,128]{1,0:T(8,128)} %convert_bitcast_fusion.cells, s32[64]{0:T(128)} %select_reduce_fusion.counts, f32[128,1152]{1,0:T(8,128)} %get-tuple-element.11.z_density, bf16[128,128]{1,0:T(8,128)(2,1)} %constant.81.clone.few_high, ...), custom_call_target="tpu_custom_call" | custom-call | tf_op jit(solution)/shard_map/paint/pallas_call | solution.py:518
  34.2 7.7 %all-to-all-done.2 = f32[128,1,2304]{2,1,0:T(1,128)S(1)} async-done(((f32[128,1,2304]{2,1,0:T(1,128)}), f32[128,1,2304]{2,1,0:T(1,128)S(1)}, u32[]{:S(2)}, u32[]{:S(2)}) %all-to-all-start.2) | async-done | bytes 1179680 | tf_op jit(solution)/shard_map/all_to_all | solution.py:459
  41.9 6.7 %all-to-all-start.1 = ((f32[128,1,4608]{2,1,0:T(1,128)}), f32[128,1,4608]{2,1,0:T(1,128)S(1)}, u32[]{:S(2)}, u32[]{:S(2)}) async-start(f32[128,1,4608]{2,1,0:T(1,128)} %bitcast.22), calls=%async_computation.1 | async-start | bytes 4718592 | tf_op jit(solution)/shard_map/all_to_all | solution.py:459
  48.6 0.6 pad_add_fusion.kz_ref
  49.2 8.8 %window.1.rest_7_ = f32[2,1152,128]{2,1,0:T(8,128)} custom-call(s32[2]{0:T(128)} %pad_add_fusion.kz_ref), custom_call_target="tpu_custom_call" | custom-call | tf_op jit(solution)/shard_map/window/pallas_call | solution.py:532
  58.0 5.7 %middle1.1.rest_8_ = f32[2304,128]{1,0:T(8,128)S(1)} custom-call(f32[2304,128]{1,0:T(8,128)S(1)} %bitcast.21, bf16[256,256]{1,0:T(8,128)(2,1)} %constant.85.clone.rest_0_, bf16[256,256]{1,0:T(8,128)(2,1)} %constant.86.clone.rest_1_, f32[2,8,1152]{2,1,0:T(8,128)} %constant.87.clone.rest_2_, f32[2,16,1152]{2,1,0:T(8,128)} %constant.88.clone.rest_3_, ...), custom_call_target="tpu_custom_call" | custom-call | tf_op jit(solution)/shard_map/middle1/pallas_call | solution.py:468
  63.7 0.0 copy-start
  63.7 1.0 copy-done
  64.7 15.6 %all-to-all-done.1 = f32[128,1,4608]{2,1,0:T(1,128)S(1)} async-done(((f32[128,1,4608]{2,1,0:T(1,128)}), f32[128,1,4608]{2,1,0:T(1,128)S(1)}, u32[]{:S(2)}, u32[]{:S(2)}) %all-to-all-start.1) | async-done | bytes 2359328 | tf_op jit(solution)/shard_map/all_to_all | solution.py:459
  80.4 8.4 %middle2.1 = f32[6912,128]{1,0:T(8,128)S(1)} custom-call(f32[4608,128]{1,0:T(8,128)S(1)} %bitcast.20, bf16[256,256]{1,0:T(8,128)(2,1)} %constant.85.clone.rest_0_, bf16[256,256]{1,0:T(8,128)(2,1)} %constant.86.clone.rest_1_, f32[2,8,1152]{2,1,0:T(8,128)} %constant.87.clone.rest_2_, f32[2,16,1152]{2,1,0:T(8,128)} %constant.88.clone.rest_3_, ...), custom_call_target="tpu_custom_call" | custom-call | tf_op jit(solution)/shard_map/middle2/pallas_call | solution.py:468
  88.7 0.0 copy-start.1
  88.7 0.0 copy-start.2
  88.8 0.0 copy-start.3
  88.8 0.0 copy-start.4
  88.8 52.7 %all_to_all.20 = f32[128,1,6912]{2,1,0:T(1,128)S(1)} all-to-all(f32[128,1,6912]{2,1,0:T(1,128)S(1)} %bitcast.18), channel_id=1, replica_groups=mesh['px'=8,'py'=16] {'px','py'}, dimensions={0} | all-to-all | bytes 7077888 | tf_op jit(solution)/shard_map/all_to_all | solution.py:459
  141.5 0.0 copy-done.1
  141.5 0.0 copy-done.2
  141.5 0.0 copy-done.3
  141.5 0.0 copy-done.4
  141.5 3.1 %zlast.1 = f32[48,24,384]{2,1,0:T(8,128)} custom-call(f32[6912,128]{1,0:T(8,128)S(1)} %bitcast.19, bf16[128,128]{1,0:T(8,128)(2,1)S(1)} %copy-done.4, bf16[128,128]{1,0:T(8,128)(2,1)S(1)} %copy-done.3, bf16[256,256]{1,0:T(8,128)(2,1)S(1)} %copy-done.2, bf16[256,256]{1,0:T(8,128)(2,1)S(1)} %copy-done.1), custom_call_target="tpu_custom_call" | custom-call | tf_op jit(solution)/shard_map/zlast/pallas_call | solution.py:543
  (1 shorter events, 0.0 us)
Async XLA Ops:
  1.6 16.0 %all-to-all-start = ((f32[16,8,128]{2,1,0:T(8,128)}), f32[16,8,128]{2,1,0:T(8,128)S(1)}, u32[]{:S(2)}, u32[]{:S(2)}) async-start(f32[16,8,128]{2,1,0:T(8,128)} %bitcast.27), calls=%async_computation | async-start | bytes 131072 | tf_op jit(solution)/shard_map/all_to_all | solution.py:498
  17.6 24.3 %all-to-all-start.2 = ((f32[128,1,2304]{2,1,0:T(1,128)}), f32[128,1,2304]{2,1,0:T(1,128)S(1)}, u32[]{:S(2)}, u32[]{:S(2)}) async-start(f32[128,1,2304]{2,1,0:T(1,128)} %bitcast.23), calls=%async_computation.2 | async-start | bytes 2359296 | tf_op jit(solution)/shard_map/all_to_all | solution.py:459
  23.5 1.2 copy-start.5
  41.9 38.4 %all-to-all-start.1 = ((f32[128,1,4608]{2,1,0:T(1,128)}), f32[128,1,4608]{2,1,0:T(1,128)S(1)}, u32[]{:S(2)}, u32[]{:S(2)}) async-start(f32[128,1,4608]{2,1,0:T(1,128)} %bitcast.22), calls=%async_computation.1 | async-start | bytes 4718592 | tf_op jit(solution)/shard_map/all_to_all | solution.py:459
  63.7 1.0 copy-start
  88.7 52.7 %copy-start.1 = (bf16[256,256]{1,0:T(8,128)(2,1)S(1)}, bf16[256,256]{1,0:T(8,128)(2,1)}, u32[]{:S(2)}) copy-start(bf16[256,256]{1,0:T(8,128)(2,1)} %constant.84.clone.many_low) | copy-start | bytes 393220
  88.7 52.7 %copy-start.2 = (bf16[256,256]{1,0:T(8,128)(2,1)S(1)}, bf16[256,256]{1,0:T(8,128)(2,1)}, u32[]{:S(2)}) copy-start(bf16[256,256]{1,0:T(8,128)(2,1)} %constant.83.clone.many_high) | copy-start | bytes 393220
  88.8 52.7 %copy-start.3 = (bf16[128,128]{1,0:T(8,128)(2,1)S(1)}, bf16[128,128]{1,0:T(8,128)(2,1)}, u32[]{:S(2)}) copy-start(bf16[128,128]{1,0:T(8,128)(2,1)} %constant.82.clone.few_low) | copy-start | bytes 98308
  88.8 52.7 %copy-start.4 = (bf16[128,128]{1,0:T(8,128)(2,1)S(1)}, bf16[128,128]{1,0:T(8,128)(2,1)}, u32[]{:S(2)}) copy-start(bf16[128,128]{1,0:T(8,128)(2,1)} %constant.81.clone.few_high) | copy-start | bytes 98308

commit v6 on v5

--- a/solution.py
+++ b/solution.py
@@ -69,13 +69,15 @@
 def device_table():
     s = np.arange(N_DEV)
     i, q = s // N_PY, s % N_PY
-    return split_np(real_form(np.outer(i, i) / N_PX + np.outer(q, q) / N_PY))
+    form = real_form(np.outer(i, i) / N_PX + np.outer(q, q) / N_PY)
+    return split_np(form), split_np(form.T)
 
 
 def lane_table():
     m = np.arange(128)
     b, y = m // 8, m % 8
-    return split_np(real_form(np.outer(b, b) / 16.0 + np.outer(y, y) / 8.0).T)
+    form = real_form(np.outer(b, b) / 16.0 + np.outer(y, y) / 8.0)
+    return split_np(form.T), split_np(form)
 
 
 def twiddles():
@@ -278,10 +280,12 @@
 
 
 def middle_kernel(planes, got, *rest):
-    count = len(TABLE_SHAPES) + (2 if planes == 2 else 1)
+    count = len(TABLE_SHAPES) + planes - 1
     sources, out, rest = rest[:count], rest[count], rest[count + 1 :]
     tables, (tw1, work, r_high, r_low, l_high, l_low, back, sems) = rest[:count], rest[count:]
-    dev_high, dev_low, tw_x, tw_y, tw2, lane_high, lane_low, win = tables[:8]
+    dev_high, dev_low, tw_x, tw_y, tw2 = tables[:5]
+    lane_high, lane_low, win, lane_back_high, lane_back_low = tables[5:10]
+    dev_back_high, dev_back_low = tables[10:12]
     copies = [
         pltpu.make_async_copy(source, table, sems.at[k])
         for k, (source, table) in enumerate(zip(sources, tables))
@@ -301,13 +305,23 @@
     def dev():
         return dev_high[...], dev_low[...]
 
+    def dev_back():
+        return dev_back_high[...], dev_back_low[...]
+
     def mat():
         return lane_high[...], lane_low[...]
+
+    def mat_back():
+        return lane_back_high[...], lane_back_low[...]
 
     def arrive(stage):
         if stage < 3:
             for copy in copies[(0, 2, 5)[stage] : (2, 5, len(copies))[stage]]:
                 copy.wait()
+        if stage == 3 and planes == 2:
+            for j in range(WIDTH):
+                rows = pl.ds(j, N_DEV, stride=WIDTH)
+                out[pl.ds(j, N_DEV, stride=PITCH), :] = tables[12][rows, :]
         if stage == 1:
             for k in range(N_PX):
                 cos_x, sin_x = tw_x[0, k : k + 1, :], tw_x[1, k : k + 1, :]
@@ -316,8 +330,8 @@
                 tw1[0, at, :] = cos_x * cos_y - sin_x * sin_y
                 tw1[1, at, :] = sin_x * cos_y + cos_x * sin_y
 
-    def across(p, a):
-        at = slice(a * NG, (a + 1) * NG)
+    def across(p, k):
+        at = slice(k * 256, min((k + 1) * 256, ROWS))
         work[p, :, at] = dot3(dev(), (r_high[p, :, at], r_low[p, :, at]))
 
     def row_block(block, offset=0):
@@ -348,7 +362,7 @@
         w = win[planes - 1 - p, at, :]
         l_high[p, at, :128], l_low[p, at, :128] = split(value[:, :128] * w)
         l_high[p, at, 128:], l_low[p, at, 128:] = split(value[:, 128:] * w)
-        back[p, at, :] = dot3((l_high[p, at, :], l_low[p, at, :]), mat(), NT)
+        back[p, at, :] = dot3((l_high[p, at, :], l_low[p, at, :]), mat_back())
 
     def backward(p, block):
         rows, rows_im = row_block(block), row_block(block, N_DEV)
@@ -367,14 +381,14 @@
             r_high[p, rows, at], r_low[p, rows, at] = split(re[j] * cos - im[j] * sin)
             r_high[p, rows_im, at], r_low[p, rows_im, at] = split(im[j] * cos + re[j] * sin)
 
-    def home(p, a):
-        at = slice(a * NG, (a + 1) * NG)
-        value = dot3(dev(), (r_high[p, :, at], r_low[p, :, at]), TN)
+    def home(p, k):
+        at = slice(k * 256, min((k + 1) * 256, ROWS))
+        value = dot3(dev_back(), (r_high[p, :, at], r_low[p, :, at]))
         for c in range(2):
-            start = (first_plane + p) * WIDTH + c * LB + a * 3
+            start = (first_plane + p) * WIDTH + c * LB + k * 2
             store_plane(out, start, out_pitch, value[c * N_DEV : (c + 1) * N_DEV])
 
-    stages = [(across, 3), (forward, N_PX), (along, 3), (backward, N_PX), (home, 3)]
+    stages = [(across, 5), (forward, N_PX), (along, 3), (backward, N_PX), (home, 5)]
     if planes == 1:
         for stage, (work_of, parts) in enumerate(stages):
             arrive(stage)
@@ -398,8 +412,6 @@
                 both += [((k + 0.5) / parts, p, work_of, k) for k in range(parts)]
         for _, p, work_of, part in sorted(both, key=lambda item: item[:2]):
             work_of(p, part)
-    for j in range(WIDTH):
-        out[pl.ds(j, N_DEV, stride=PITCH), :] = tables[8][pl.ds(j, N_DEV, stride=WIDTH), :]
 
 
 def z_last_kernel(got, few_high, few_low, many_high, many_low, out):
@@ -441,6 +453,9 @@
     ((2, N_PX, ROWS), F32),
     ((2, N_PY, ROWS), F32),
     ((8, ROWS), F32),
+    *SQUARE,
+    ((2, ROWS, 128), F32),
+    *SQUARE,
     *SQUARE,
 ]
 FOLDED = [pltpu.VMEM((ROWS, width), BF) for width in (128, 128, 256, 256)]
@@ -488,7 +503,9 @@
 
 def on_device(photons, halo_cells, halo_counts, owners, density):
     table = z_tables()
-    tables = (*device_table(), *twiddles(), *lane_table())
+    dev, dev_back = device_table()
+    lane, lane_back = lane_table()
+    tw = twiddles()
 
     send = pl.pallas_call(
         sort_kernel,
@@ -535,8 +552,9 @@
         in_specs=[smem],
         name="window",
     )(jnp.stack([high, low]).astype(jnp.int32))
-    back_a = middle(got_a, 1, (*tables, win))
-    back = middle(got_bc, 2, (*tables, win, back_a))
+    tables = (*dev, *tw, *lane, win, *lane_back, *dev_back)
+    back_a = middle(got_a, 1, tables)
+    back = middle(got_bc, 2, (*tables, back_a))
     got = exchange(back)
     whole = pl.BlockSpec((N_DEV * PITCH, 128), lambda i: (0, 0))
     whole_t = [pl.BlockSpec(t.shape, lambda i: (0, 0)) for t in table]

time: 147 us -> 146 us (level)
  waiting for transfers between devices: 26.8 us -> 22.9 us
  Pallas kernels: 40.9 us -> 44.2 us
    pallas_call x1, Pallas kernels: 9.48 us -> 13.4 us  [on_device(): pl.pallas_call(paint_kernel, out_shape=jax.ShapeDtypeStruct((N_DEV * 2 *...]
    all_to_all x2, waiting for transfers between devices: 23.3 us -> 19.5 us  [exchange(): return lax.all_to_all(send, AXES, 0, 0, tiled=True).reshape(rows.shape)]
  transfers between devices with their start and end apart: 3 -> 3, of which waited for: 3 -> 3; matrix products, arithmetic and copies ran while one was open for 1% -> 1% of each run, Pallas kernels for 19% -> 22%
where the time goes in v6:
time: 146 us; the launch traced here: 144 us
  blocking collectives  52.7 us (36%)
  Pallas kernels  44.2 us (30%)
  waiting for transfers between devices  22.9 us (16%)
  starting transfers between devices  21.2 us (15%)
  other arithmetic  1.81 us (1%)
    all_to_all x1, blocking collectives, exchange(): return lax.all_to_all(send, AXES, 0, 0, tiled=True).reshape(rows.shape)  52.7 us
    all_to_all x2, waiting for transfers between devices, exchange(): return lax.all_to_all(send, AXES, 0, 0, tiled=True).reshape(rows.shape)  19.5 us
    pallas_call x1, Pallas kernels, on_device(): pl.pallas_call(paint_kernel, out_shape=jax.ShapeDtypeStruct((N_DEV * 2 *...  13.4 us
    pallas_call x2, Pallas kernels, middle(): pl.pallas_call(functools.partial(middle_kernel, planes), out_shape=out_sh...  13.4 us
    all_to_all x2, starting transfers between devices, exchange(): return lax.all_to_all(send, AXES, 0, 0, tiled=True).reshape(rows.shape)  12.5 us
    pallas_call x1, Pallas kernels, on_device(): pl.pallas_call(window_kernel, out_shape=jax.ShapeDtypeStruct((2, ROWS, 12...  8.75 us
    all_to_all x1, starting transfers between devices, on_device(): lax.all_to_all(send.reshape(N_PY, 2 * CAP, SLOTS), 'py', 0, 0, tiled=True)  8.63 us
    pallas_call x1, Pallas kernels, on_device(): pl.pallas_call(z_density_kernel, out_shape=(jax.ShapeDtypeStruct((N_DEV *...  3.84 us
  transfers between devices with their start and end apart: 3, of which 3 were waited for; matrix products, arithmetic and copies ran while one was open for 1% of the time, Pallas kernels for 22%

profile of v6, /device:TPU:7, one launch (start us, length us, event | category | flops | bytes accessed | tf_op | source)
XLA Modules:
  0.0 144.0 jit_solution(7290285139977699817)
XLA Ops:
  0.0 1.6 %sort.1 = f32[128,128]{1,0:T(8,128)} custom-call(f32[32,128]{1,0:T(8,128)} %photons.1, s32[32,128]{1,0:T(8,128)} %cells.1, s32[1,32]{1,0:T(1,128)} %bitcast.29, s32[1,32]{1,0:T(1,128)} %bitcast.30), custom_call_target="tpu_custom_call" | custom-call | tf_op jit(solution)/shard_map/sort/pallas_call | solution.py:510
  1.6 8.6 %all-to-all-start = ((f32[16,8,128]{2,1,0:T(8,128)}), f32[16,8,128]{2,1,0:T(8,128)S(1)}, u32[]{:S(2)}, u32[]{:S(2)}) async-start(f32[16,8,128]{2,1,0:T(8,128)} %bitcast.27), calls=%async_computation | async-start | bytes 131072 | tf_op jit(solution)/shard_map/all_to_all | solution.py:515
  10.3 3.8 %zdensity.1 = (f32[2304,128]{1,0:T(8,128)}, f32[128,1152]{1,0:T(8,128)}) custom-call(f32[48,24,384]{2,1,0:T(8,128)} %density.1, bf16[128,128]{1,0:T(8,128)(2,1)} %constant.89.clone.few_high, bf16[128,128]{1,0:T(8,128)(2,1)} %constant.90.clone.few_low, bf16[256,256]{1,0:T(8,128)(2,1)} %constant.91.clone.many_high, bf16[256,256]{1,0:T(8,128)(2,1)} %constant.92.clone.many_low), custom_call_target="tpu_custom_call" | custom-call | tf_op jit(solution)/shard_map/zdensity/pallas_call | solution.py:517
  14.1 3.5 %all-to-all-done = f32[16,8,128]{2,1,0:T(8,128)S(1)} async-done(((f32[16,8,128]{2,1,0:T(8,128)}), f32[16,8,128]{2,1,0:T(8,128)S(1)}, u32[]{:S(2)}, u32[]{:S(2)}) %all-to-all-start) | async-done | bytes 65568 | tf_op jit(solution)/shard_map/all_to_all | solution.py:515
  17.6 5.9 %all-to-all-start.2 = ((f32[128,1,2304]{2,1,0:T(1,128)}), f32[128,1,2304]{2,1,0:T(1,128)S(1)}, u32[]{:S(2)}, u32[]{:S(2)}) async-start(f32[128,1,2304]{2,1,0:T(1,128)} %bitcast.23), calls=%async_computation.2 | async-start | bytes 2359296 | tf_op jit(solution)/shard_map/all_to_all | solution.py:474
  23.5 0.1 fusion
  23.5 0.0 copy-start.5
  23.6 0.6 select_reduce_fusion.counts
  24.2 0.6 convert_bitcast_fusion.cells
  24.8 0.0 copy-done.5
  24.8 13.4 %paint.1 = f32[4608,128]{1,0:T(8,128)} custom-call(f32[64,128]{1,0:T(8,128)} %bitcast.25, s32[64,128]{1,0:T(8,128)} %convert_bitcast_fusion.cells, s32[64]{0:T(128)} %select_reduce_fusion.counts, f32[128,1152]{1,0:T(8,128)} %get-tuple-element.11.z_density, bf16[128,128]{1,0:T(8,128)(2,1)} %constant.89.clone.few_high, ...), custom_call_target="tpu_custom_call" | custom-call | tf_op jit(solution)/shard_map/paint/pallas_call | solution.py:535
  38.2 3.7 %all-to-all-done.2 = f32[128,1,2304]{2,1,0:T(1,128)S(1)} async-done(((f32[128,1,2304]{2,1,0:T(1,128)}), f32[128,1,2304]{2,1,0:T(1,128)S(1)}, u32[]{:S(2)}, u32[]{:S(2)}) %all-to-all-start.2) | async-done | bytes 1179680 | tf_op jit(solution)/shard_map/all_to_all | solution.py:474
  41.9 6.7 %all-to-all-start.1 = ((f32[128,1,4608]{2,1,0:T(1,128)}), f32[128,1,4608]{2,1,0:T(1,128)S(1)}, u32[]{:S(2)}, u32[]{:S(2)}) async-start(f32[128,1,4608]{2,1,0:T(1,128)} %bitcast.22), calls=%async_computation.1 | async-start | bytes 4718592 | tf_op jit(solution)/shard_map/all_to_all | solution.py:474
  48.6 0.6 pad_add_fusion.kz_ref
  49.2 8.8 %window.1.rest_7_ = f32[2,1152,128]{2,1,0:T(8,128)} custom-call(s32[2]{0:T(128)} %pad_add_fusion.kz_ref), custom_call_target="tpu_custom_call" | custom-call | tf_op jit(solution)/shard_map/window/pallas_call | solution.py:549
  58.0 5.6 %middle1.1.rest_12_ = f32[2304,128]{1,0:T(8,128)S(1)} custom-call(f32[2304,128]{1,0:T(8,128)S(1)} %bitcast.21, bf16[256,256]{1,0:T(8,128)(2,1)} %constant.93.clone.rest_0_, bf16[256,256]{1,0:T(8,128)(2,1)} %constant.94.clone.rest_1_, f32[2,8,1152]{2,1,0:T(8,128)} %constant.95.clone.rest_2_, f32[2,16,1152]{2,1,0:T(8,128)} %constant.96.clone.rest_3_, ...), custom_call_target="tpu_custom_call" | custom-call | tf_op jit(solution)/shard_map/middle1/pallas_call | solution.py:483
  63.6 0.0 copy-start
  63.6 1.0 copy-done
  64.6 15.7 %all-to-all-done.1 = f32[128,1,4608]{2,1,0:T(1,128)S(1)} async-done(((f32[128,1,4608]{2,1,0:T(1,128)}), f32[128,1,4608]{2,1,0:T(1,128)S(1)}, u32[]{:S(2)}, u32[]{:S(2)}) %all-to-all-start.1) | async-done | bytes 2359328 | tf_op jit(solution)/shard_map/all_to_all | solution.py:474
  80.4 7.8 %middle2.1 = f32[6912,128]{1,0:T(8,128)S(1)} custom-call(f32[4608,128]{1,0:T(8,128)S(1)} %bitcast.20, bf16[256,256]{1,0:T(8,128)(2,1)} %constant.93.clone.rest_0_, bf16[256,256]{1,0:T(8,128)(2,1)} %constant.94.clone.rest_1_, f32[2,8,1152]{2,1,0:T(8,128)} %constant.95.clone.rest_2_, f32[2,16,1152]{2,1,0:T(8,128)} %constant.96.clone.rest_3_, ...), custom_call_target="tpu_custom_call" | custom-call | tf_op jit(solution)/shard_map/middle2/pallas_call | solution.py:483
  88.2 0.0 copy-start.1
  88.2 0.0 copy-start.2
  88.2 0.0 copy-start.3
  88.2 0.0 copy-start.4
  88.2 52.7 %all_to_all.20 = f32[128,1,6912]{2,1,0:T(1,128)S(1)} all-to-all(f32[128,1,6912]{2,1,0:T(1,128)S(1)} %bitcast.18), channel_id=1, replica_groups=mesh['px'=8,'py'=16] {'px','py'}, dimensions={0} | all-to-all | bytes 7077888 | tf_op jit(solution)/shard_map/all_to_all | solution.py:474
  140.9 0.0 copy-done.1
  140.9 0.0 copy-done.2
  140.9 0.0 copy-done.3
  140.9 0.0 copy-done.4
  140.9 3.1 %zlast.1 = f32[48,24,384]{2,1,0:T(8,128)} custom-call(f32[6912,128]{1,0:T(8,128)S(1)} %bitcast.19, bf16[128,128]{1,0:T(8,128)(2,1)S(1)} %copy-done.4, bf16[128,128]{1,0:T(8,128)(2,1)S(1)} %copy-done.3, bf16[256,256]{1,0:T(8,128)(2,1)S(1)} %copy-done.2, bf16[256,256]{1,0:T(8,128)(2,1)S(1)} %copy-done.1), custom_call_target="tpu_custom_call" | custom-call | tf_op jit(solution)/shard_map/zlast/pallas_call | solution.py:561
  (1 shorter events, 0.0 us)
Async XLA Ops:
  1.6 16.0 %all-to-all-start = ((f32[16,8,128]{2,1,0:T(8,128)}), f32[16,8,128]{2,1,0:T(8,128)S(1)}, u32[]{:S(2)}, u32[]{:S(2)}) async-start(f32[16,8,128]{2,1,0:T(8,128)} %bitcast.27), calls=%async_computation | async-start | bytes 131072 | tf_op jit(solution)/shard_map/all_to_all | solution.py:515
  17.6 24.3 %all-to-all-start.2 = ((f32[128,1,2304]{2,1,0:T(1,128)}), f32[128,1,2304]{2,1,0:T(1,128)S(1)}, u32[]{:S(2)}, u32[]{:S(2)}) async-start(f32[128,1,2304]{2,1,0:T(1,128)} %bitcast.23), calls=%async_computation.2 | async-start | bytes 2359296 | tf_op jit(solution)/shard_map/all_to_all | solution.py:474
  23.5 1.2 copy-start.5
  41.9 38.4 %all-to-all-start.1 = ((f32[128,1,4608]{2,1,0:T(1,128)}), f32[128,1,4608]{2,1,0:T(1,128)S(1)}, u32[]{:S(2)}, u32[]{:S(2)}) async-start(f32[128,1,4608]{2,1,0:T(1,128)} %bitcast.22), calls=%async_computation.1 | async-start | bytes 4718592 | tf_op jit(solution)/shard_map/all_to_all | solution.py:474
  63.6 1.0 copy-start
  88.2 52.7 %copy-start.1 = (bf16[256,256]{1,0:T(8,128)(2,1)S(1)}, bf16[256,256]{1,0:T(8,128)(2,1)}, u32[]{:S(2)}) copy-start(bf16[256,256]{1,0:T(8,128)(2,1)} %constant.92.clone.many_low) | copy-start | bytes 393220
  88.2 52.7 %copy-start.2 = (bf16[256,256]{1,0:T(8,128)(2,1)S(1)}, bf16[256,256]{1,0:T(8,128)(2,1)}, u32[]{:S(2)}) copy-start(bf16[256,256]{1,0:T(8,128)(2,1)} %constant.91.clone.many_high) | copy-start | bytes 393220
  88.2 52.7 %copy-start.3 = (bf16[128,128]{1,0:T(8,128)(2,1)S(1)}, bf16[128,128]{1,0:T(8,128)(2,1)}, u32[]{:S(2)}) copy-start(bf16[128,128]{1,0:T(8,128)(2,1)} %constant.90.clone.few_low) | copy-start | bytes 98308
  88.2 52.7 %copy-start.4 = (bf16[128,128]{1,0:T(8,128)(2,1)S(1)}, bf16[128,128]{1,0:T(8,128)(2,1)}, u32[]{:S(2)}) copy-start(bf16[128,128]{1,0:T(8,128)(2,1)} %constant.89.clone.few_high) | copy-start | bytes 98308

commit v7 on v6

--- a/solution.py
+++ b/solution.py
@@ -294,13 +294,13 @@
         copy.start()
     first_plane, out_pitch = (1, PITCH) if planes == 2 else (0, WIDTH)
     pitch = planes * WIDTH
-    for p in range(planes):
+
+    def assemble(p, j):
         for c in range(2):
-            for j in range(LB):
-                high, low = split(got[pl.ds((p * 2 + c) * LB + j, N_DEV, stride=pitch), :])
-                at, to = slice(c * N_DEV, (c + 1) * N_DEV), slice(j * 128, (j + 1) * 128)
-                r_high[p, at, to] = high
-                r_low[p, at, to] = low
+            high, low = split(got[pl.ds((p * 2 + c) * LB + j, N_DEV, stride=pitch), :])
+            at, to = slice(c * N_DEV, (c + 1) * N_DEV), slice(j * 128, (j + 1) * 128)
+            r_high[p, at, to] = high
+            r_low[p, at, to] = low
 
     def dev():
         return dev_high[...], dev_low[...]
@@ -315,14 +315,14 @@
         return lane_back_high[...], lane_back_low[...]
 
     def arrive(stage):
-        if stage < 3:
-            for copy in copies[(0, 2, 5)[stage] : (2, 5, len(copies))[stage]]:
+        if stage < 4:
+            for copy in copies[(0, 0, 2, 5)[stage] : (0, 2, 5, len(copies))[stage]]:
                 copy.wait()
-        if stage == 3 and planes == 2:
+        if stage == 4 and planes == 2:
             for j in range(WIDTH):
                 rows = pl.ds(j, N_DEV, stride=WIDTH)
                 out[pl.ds(j, N_DEV, stride=PITCH), :] = tables[12][rows, :]
-        if stage == 1:
+        if stage == 2:
             for k in range(N_PX):
                 cos_x, sin_x = tw_x[0, k : k + 1, :], tw_x[1, k : k + 1, :]
                 cos_y, sin_y = tw_y[0], tw_y[1]
@@ -353,8 +353,10 @@
             at = slice(j * 128, (j + 1) * 128)
             cos, sin = tw2[0:1, at], tw2[1:2, at]
             to = row_block(block, j * N_DEV)
-            l_high[p, to, :128], l_low[p, to, :128] = split(re[j] * cos + im[j] * sin)
-            l_high[p, to, 128:], l_low[p, to, 128:] = split(im[j] * cos - re[j] * sin)
+            if j:
+                re[j], im[j] = re[j] * cos + im[j] * sin, im[j] * cos - re[j] * sin
+            l_high[p, to, :128], l_low[p, to, :128] = split(re[j])
+            l_high[p, to, 128:], l_low[p, to, 128:] = split(im[j])
 
     def along(p, k):
         at = slice(k * NG, (k + 1) * NG)
@@ -372,8 +374,8 @@
             cos, sin = tw2[0:1, at], tw2[1:2, at]
             of = row_block(block, j * N_DEV)
             x, y = back[p, of, :128], back[p, of, 128:]
-            re.append(x * cos - y * sin)
-            im.append(y * cos + x * sin)
+            re.append(x * cos - y * sin if j else x)
+            im.append(y * cos + x * sin if j else y)
         nine(re, im, 1.0)
         for j in range(LB):
             at = slice(j * 128, (j + 1) * 128)
@@ -388,7 +390,7 @@
             start = (first_plane + p) * WIDTH + c * LB + k * 2
             store_plane(out, start, out_pitch, value[c * N_DEV : (c + 1) * N_DEV])
 
-    stages = [(across, 5), (forward, N_PX), (along, 3), (backward, N_PX), (home, 5)]
+    stages = [(assemble, LB), (across, 5), (forward, N_PX), (along, 3), (backward, N_PX), (home, 5)]
     if planes == 1:
         for stage, (work_of, parts) in enumerate(stages):
             arrive(stage)

time: 146 us -> 146 us (level)
  Pallas kernels: 44.2 us -> 40 us
  waiting for transfers between devices: 22.9 us -> 27.1 us
    pallas_call x1, Pallas kernels: 13.4 us -> 9.25 us  [on_device(): pl.pallas_call(paint_kernel, out_shape=jax.ShapeDtypeStruct((N_DEV * 2 *...]
    all_to_all x2, waiting for transfers between devices: 19.5 us -> 23.6 us  [exchange(): return lax.all_to_all(send, AXES, 0, 0, tiled=True).reshape(rows.shape)]
  transfers between devices with their start and end apart: 3 -> 3, of which waited for: 3 -> 3; matrix products, arithmetic and copies ran while one was open for 1% -> 1% of each run, Pallas kernels for 22% -> 19%
where the time goes in v7:
time: 146 us; the launch traced here: 144 us
  blocking collectives  52.7 us (36%)
  Pallas kernels  40 us (27%)
  waiting for transfers between devices  27.1 us (19%)
  starting transfers between devices  21.2 us (15%)
  other arithmetic  1.81 us (1%)
    all_to_all x1, blocking collectives, exchange(): return lax.all_to_all(send, AXES, 0, 0, tiled=True).reshape(rows.shape)  52.7 us
    all_to_all x2, waiting for transfers between devices, exchange(): return lax.all_to_all(send, AXES, 0, 0, tiled=True).reshape(rows.shape)  23.6 us
    pallas_call x2, Pallas kernels, middle(): pl.pallas_call(functools.partial(middle_kernel, planes), out_shape=out_sh...  13.4 us
    all_to_all x2, starting transfers between devices, exchange(): return lax.all_to_all(send, AXES, 0, 0, tiled=True).reshape(rows.shape)  12.5 us
    pallas_call x1, Pallas kernels, on_device(): pl.pallas_call(paint_kernel, out_shape=jax.ShapeDtypeStruct((N_DEV * 2 *...  9.25 us
    pallas_call x1, Pallas kernels, on_device(): pl.pallas_call(window_kernel, out_shape=jax.ShapeDtypeStruct((2, ROWS, 12...  8.75 us
    all_to_all x1, starting transfers between devices, on_device(): lax.all_to_all(send.reshape(N_PY, 2 * CAP, SLOTS), 'py', 0, 0, tiled=True)  8.63 us
    pallas_call x1, Pallas kernels, on_device(): pl.pallas_call(z_density_kernel, out_shape=(jax.ShapeDtypeStruct((N_DEV *...  3.84 us
  transfers between devices with their start and end apart: 3, of which 3 were waited for; matrix products, arithmetic and copies ran while one was open for 1% of the time, Pallas kernels for 19%

profile of v7, /device:TPU:7, one launch (start us, length us, event | category | flops | bytes accessed | tf_op | source)
XLA Modules:
  0.0 144.0 jit_solution(16983363813432715474)
XLA Ops:
  0.0 1.6 %sort.1 = f32[128,128]{1,0:T(8,128)} custom-call(f32[32,128]{1,0:T(8,128)} %photons.1, s32[32,128]{1,0:T(8,128)} %cells.1, s32[1,32]{1,0:T(1,128)} %bitcast.29, s32[1,32]{1,0:T(1,128)} %bitcast.30), custom_call_target="tpu_custom_call" | custom-call | tf_op jit(solution)/shard_map/sort/pallas_call | solution.py:512
  1.6 8.6 %all-to-all-start = ((f32[16,8,128]{2,1,0:T(8,128)}), f32[16,8,128]{2,1,0:T(8,128)S(1)}, u32[]{:S(2)}, u32[]{:S(2)}) async-start(f32[16,8,128]{2,1,0:T(8,128)} %bitcast.27), calls=%async_computation | async-start | bytes 131072 | tf_op jit(solution)/shard_map/all_to_all | solution.py:517
  10.3 3.8 %zdensity.1 = (f32[2304,128]{1,0:T(8,128)}, f32[128,1152]{1,0:T(8,128)}) custom-call(f32[48,24,384]{2,1,0:T(8,128)} %density.1, bf16[128,128]{1,0:T(8,128)(2,1)} %constant.89.clone.few_high, bf16[128,128]{1,0:T(8,128)(2,1)} %constant.90.clone.few_low, bf16[256,256]{1,0:T(8,128)(2,1)} %constant.91.clone.many_high, bf16[256,256]{1,0:T(8,128)(2,1)} %constant.92.clone.many_low), custom_call_target="tpu_custom_call" | custom-call | tf_op jit(solution)/shard_map/zdensity/pallas_call | solution.py:519
  14.1 3.5 %all-to-all-done = f32[16,8,128]{2,1,0:T(8,128)S(1)} async-done(((f32[16,8,128]{2,1,0:T(8,128)}), f32[16,8,128]{2,1,0:T(8,128)S(1)}, u32[]{:S(2)}, u32[]{:S(2)}) %all-to-all-start) | async-done | bytes 65568 | tf_op jit(solution)/shard_map/all_to_all | solution.py:517
  17.6 5.9 %all-to-all-start.2 = ((f32[128,1,2304]{2,1,0:T(1,128)}), f32[128,1,2304]{2,1,0:T(1,128)S(1)}, u32[]{:S(2)}, u32[]{:S(2)}) async-start(f32[128,1,2304]{2,1,0:T(1,128)} %bitcast.23), calls=%async_computation.2 | async-start | bytes 2359296 | tf_op jit(solution)/shard_map/all_to_all | solution.py:476
  23.5 0.1 fusion
  23.5 0.0 copy-start.5
  23.6 0.6 select_reduce_fusion.counts
  24.2 0.6 convert_bitcast_fusion.cells
  24.8 0.0 copy-done.5
  24.8 9.3 %paint.1 = f32[4608,128]{1,0:T(8,128)} custom-call(f32[64,128]{1,0:T(8,128)} %bitcast.25, s32[64,128]{1,0:T(8,128)} %convert_bitcast_fusion.cells, s32[64]{0:T(128)} %select_reduce_fusion.counts, f32[128,1152]{1,0:T(8,128)} %get-tuple-element.11.z_density, bf16[128,128]{1,0:T(8,128)(2,1)} %constant.89.clone.few_high, ...), custom_call_target="tpu_custom_call" | custom-call | tf_op jit(solution)/shard_map/paint/pallas_call | solution.py:537
  34.0 7.9 %all-to-all-done.2 = f32[128,1,2304]{2,1,0:T(1,128)S(1)} async-done(((f32[128,1,2304]{2,1,0:T(1,128)}), f32[128,1,2304]{2,1,0:T(1,128)S(1)}, u32[]{:S(2)}, u32[]{:S(2)}) %all-to-all-start.2) | async-done | bytes 1179680 | tf_op jit(solution)/shard_map/all_to_all | solution.py:476
  41.9 6.7 %all-to-all-start.1 = ((f32[128,1,4608]{2,1,0:T(1,128)}), f32[128,1,4608]{2,1,0:T(1,128)S(1)}, u32[]{:S(2)}, u32[]{:S(2)}) async-start(f32[128,1,4608]{2,1,0:T(1,128)} %bitcast.22), calls=%async_computation.1 | async-start | bytes 4718592 | tf_op jit(solution)/shard_map/all_to_all | solution.py:476
  48.6 0.6 pad_add_fusion.kz_ref
  49.2 8.8 %window.1.rest_7_ = f32[2,1152,128]{2,1,0:T(8,128)} custom-call(s32[2]{0:T(128)} %pad_add_fusion.kz_ref), custom_call_target="tpu_custom_call" | custom-call | tf_op jit(solution)/shard_map/window/pallas_call | solution.py:551
  58.0 5.6 %middle1.1.rest_12_ = f32[2304,128]{1,0:T(8,128)S(1)} custom-call(f32[2304,128]{1,0:T(8,128)S(1)} %bitcast.21, bf16[256,256]{1,0:T(8,128)(2,1)} %constant.93.clone.rest_0_, bf16[256,256]{1,0:T(8,128)(2,1)} %constant.94.clone.rest_1_, f32[2,8,1152]{2,1,0:T(8,128)} %constant.95.clone.rest_2_, f32[2,16,1152]{2,1,0:T(8,128)} %constant.96.clone.rest_3_, ...), custom_call_target="tpu_custom_call" | custom-call | tf_op jit(solution)/shard_map/middle1/pallas_call | solution.py:485
  63.6 0.0 copy-start
  63.6 1.0 copy-done
  64.6 15.7 %all-to-all-done.1 = f32[128,1,4608]{2,1,0:T(1,128)S(1)} async-done(((f32[128,1,4608]{2,1,0:T(1,128)}), f32[128,1,4608]{2,1,0:T(1,128)S(1)}, u32[]{:S(2)}, u32[]{:S(2)}) %all-to-all-start.1) | async-done | bytes 2359328 | tf_op jit(solution)/shard_map/all_to_all | solution.py:476
  80.4 7.8 %middle2.1 = f32[6912,128]{1,0:T(8,128)S(1)} custom-call(f32[4608,128]{1,0:T(8,128)S(1)} %bitcast.20, bf16[256,256]{1,0:T(8,128)(2,1)} %constant.93.clone.rest_0_, bf16[256,256]{1,0:T(8,128)(2,1)} %constant.94.clone.rest_1_, f32[2,8,1152]{2,1,0:T(8,128)} %constant.95.clone.rest_2_, f32[2,16,1152]{2,1,0:T(8,128)} %constant.96.clone.rest_3_, ...), custom_call_target="tpu_custom_call" | custom-call | tf_op jit(solution)/shard_map/middle2/pallas_call | solution.py:485
  88.2 0.0 copy-start.1
  88.2 0.0 copy-start.2
  88.2 0.0 copy-start.3
  88.2 0.0 copy-start.4
  88.2 52.7 %all_to_all.20 = f32[128,1,6912]{2,1,0:T(1,128)S(1)} all-to-all(f32[128,1,6912]{2,1,0:T(1,128)S(1)} %bitcast.18), channel_id=1, replica_groups=mesh['px'=8,'py'=16] {'px','py'}, dimensions={0} | all-to-all | bytes 7077888 | tf_op jit(solution)/shard_map/all_to_all | solution.py:476
  140.9 0.0 copy-done.1
  140.9 0.0 copy-done.2
  140.9 0.0 copy-done.3
  140.9 0.0 copy-done.4
  140.9 3.1 %zlast.1 = f32[48,24,384]{2,1,0:T(8,128)} custom-call(f32[6912,128]{1,0:T(8,128)S(1)} %bitcast.19, bf16[128,128]{1,0:T(8,128)(2,1)S(1)} %copy-done.4, bf16[128,128]{1,0:T(8,128)(2,1)S(1)} %copy-done.3, bf16[256,256]{1,0:T(8,128)(2,1)S(1)} %copy-done.2, bf16[256,256]{1,0:T(8,128)(2,1)S(1)} %copy-done.1), custom_call_target="tpu_custom_call" | custom-call | tf_op jit(solution)/shard_map/zlast/pallas_call | solution.py:563
  (1 shorter events, 0.0 us)
Async XLA Ops:
  1.6 16.0 %all-to-all-start = ((f32[16,8,128]{2,1,0:T(8,128)}), f32[16,8,128]{2,1,0:T(8,128)S(1)}, u32[]{:S(2)}, u32[]{:S(2)}) async-start(f32[16,8,128]{2,1,0:T(8,128)} %bitcast.27), calls=%async_computation | async-start | bytes 131072 | tf_op jit(solution)/shard_map/all_to_all | solution.py:517
  17.6 24.3 %all-to-all-start.2 = ((f32[128,1,2304]{2,1,0:T(1,128)}), f32[128,1,2304]{2,1,0:T(1,128)S(1)}, u32[]{:S(2)}, u32[]{:S(2)}) async-start(f32[128,1,2304]{2,1,0:T(1,128)} %bitcast.23), calls=%async_computation.2 | async-start | bytes 2359296 | tf_op jit(solution)/shard_map/all_to_all | solution.py:476
  23.5 1.2 copy-start.5
  41.9 38.4 %all-to-all-start.1 = ((f32[128,1,4608]{2,1,0:T(1,128)}), f32[128,1,4608]{2,1,0:T(1,128)S(1)}, u32[]{:S(2)}, u32[]{:S(2)}) async-start(f32[128,1,4608]{2,1,0:T(1,128)} %bitcast.22), calls=%async_computation.1 | async-start | bytes 4718592 | tf_op jit(solution)/shard_map/all_to_all | solution.py:476
  63.6 1.0 copy-start
  88.2 52.7 %copy-start.1 = (bf16[256,256]{1,0:T(8,128)(2,1)S(1)}, bf16[256,256]{1,0:T(8,128)(2,1)}, u32[]{:S(2)}) copy-start(bf16[256,256]{1,0:T(8,128)(2,1)} %constant.92.clone.many_low) | copy-start | bytes 393220
  88.2 52.7 %copy-start.2 = (bf16[256,256]{1,0:T(8,128)(2,1)S(1)}, bf16[256,256]{1,0:T(8,128)(2,1)}, u32[]{:S(2)}) copy-start(bf16[256,256]{1,0:T(8,128)(2,1)} %constant.91.clone.many_high) | copy-start | bytes 393220
  88.2 52.7 %copy-start.3 = (bf16[128,128]{1,0:T(8,128)(2,1)S(1)}, bf16[128,128]{1,0:T(8,128)(2,1)}, u32[]{:S(2)}) copy-start(bf16[128,128]{1,0:T(8,128)(2,1)} %constant.90.clone.few_low) | copy-start | bytes 98308
  88.2 52.7 %copy-start.4 = (bf16[128,128]{1,0:T(8,128)(2,1)S(1)}, bf16[128,128]{1,0:T(8,128)(2,1)}, u32[]{:S(2)}) copy-start(bf16[128,128]{1,0:T(8,128)(2,1)} %constant.89.clone.few_high) | copy-start | bytes 98308
